TPU v7x, 32 devices: a whole 2x2x4 slice. The times are simulated.
32 devices in a mesh: dp: 2 (over x), ei: 4 (over z), eo: 4 (over y, core).
Axes of the slice: x: 2, y: 2, z: 4, core: 2. Of those that a mesh axis runs over, the one named last changes fastest.
Arguments:
- tokens: bfloat16 [8192, 2048], P(('dp', 'ei', 'eo')), parts along dimension 0
- expert_idx: int32 [8192, 4], P(('dp', 'ei', 'eo')), parts along dimension 0
- gates: float32 [8192, 4], P(('dp', 'ei', 'eo')), parts along dimension 0
- w_gate: bfloat16 [16, 2048, 1408], P(('ei', 'eo'))
- w_up: bfloat16 [16, 2048, 1408], P(('ei', 'eo'))
- w_down: bfloat16 [16, 1408, 2048], P(('ei', 'eo'))
- grad_out: bfloat16 [8192, 2048], P(('dp', 'ei', 'eo')), parts along dimension 0
Outputs:
- output 1: bfloat16 [8192, 2048], P(('dp', 'ei', 'eo')), parts along dimension 0
- output 2: bfloat16 [8192, 2048], P(('dp', 'ei', 'eo')), parts along dimension 0
- output 3: float32 [8192, 4], P(('dp', 'ei', 'eo')), parts along dimension 0
- output 4: bfloat16 [32, 2048, 1408], P(('dp', 'ei', 'eo')), parts along dimension 0
- output 5: bfloat16 [32, 2048, 1408], P(('dp', 'ei', 'eo')), parts along dimension 0
- output 6: bfloat16 [32, 1408, 2048], P(('dp', 'ei', 'eo')), parts along dimension 0
There are 2 independent parts. A program takes and returns all parts, laid end to end along the dimension named above; an argument that names none is the same for every part.
All inputs are finite; a program needn't handle non-finite values.
Results may differ from a plain program's by a relative error of at most 0.00495966.
Values are sent between devices in bfloat16 or wider.
A program may use at most 1 GiB of HBM per device.

v0:
```python
import jax
import jax.numpy as jnp
from jax import lax
from jax.sharding import PartitionSpec as P


def slot_tables(flat_ids, num_experts, capacity):
    n_assign = flat_ids.shape[0]
    sort_order = jnp.argsort(flat_ids, stable=True).astype(jnp.int32)
    sorted_ids = flat_ids[sort_order]
    counts = jnp.zeros((num_experts,), jnp.int32).at[flat_ids].add(1)
    starts = jnp.cumsum(counts) - counts
    slot_sorted = sorted_ids * capacity + jnp.arange(n_assign, dtype=jnp.int32) - starts[sorted_ids]
    slot_of = jnp.zeros((n_assign,), jnp.int32).at[sort_order].set(slot_sorted)
    filler = jnp.full((num_experts * capacity,), n_assign, jnp.int32).at[slot_sorted].set(sort_order)
    return slot_of, filler


def exchange(buffer, ei_size, eo_size):
    row_shape = buffer.shape[1:]
    peer_grid = buffer.reshape((ei_size, eo_size) + row_shape)
    peer_grid = lax.all_to_all(peer_grid, 'eo', 1, 1, tiled=True)
    peer_grid = lax.all_to_all(peer_grid, 'ei', 0, 0, tiled=True)
    return peer_grid.reshape(buffer.shape)


def solution(mesh):
    ei_size = mesh.shape['ei']
    eo_size = mesh.shape['eo']
    group_size = ei_size * eo_size
    tok_spec = P(('dp', 'ei', 'eo'))
    exp_spec = P(('ei', 'eo'))

    def device_step(tok_loc, idx_loc, gate_loc, w_gate, w_up, w_down, dy_loc):
        tok_dev, top_k = idx_loc.shape
        exp_dev, d_model, d_ff = w_gate.shape
        num_experts = exp_dev * group_size
        capacity = min(tok_dev, tok_dev * top_k // (4 * exp_dev))
        send_rows = exp_dev * capacity
        slot_of, filler = slot_tables(idx_loc.reshape(-1), num_experts, capacity)
        tok_ids = filler // top_k
        zero_row = jnp.zeros((1, d_model), jnp.bfloat16)
        send_x = jnp.concatenate([tok_loc, zero_row])[tok_ids].reshape(group_size, send_rows, d_model)
        x_recv = exchange(send_x, ei_size, eo_size).reshape(group_size, exp_dev, capacity, d_model)
        h_gate = jnp.einsum('secd,edf->secf', x_recv, w_gate, preferred_element_type=jnp.float32)
        h_up = jnp.einsum('secd,edf->secf', x_recv, w_up, preferred_element_type=jnp.float32)
        sig_gate = jax.nn.sigmoid(h_gate)
        hidden = (h_gate * sig_gate * h_up).astype(jnp.bfloat16)
        y_expert = jnp.einsum('secf,efd->secd', hidden, w_down, preferred_element_type=jnp.float32).astype(jnp.bfloat16)
        y_back = exchange(y_expert.reshape(group_size, send_rows, d_model), ei_size, eo_size)
        y_rows = y_back.reshape(num_experts * capacity, d_model)[slot_of].reshape(tok_dev, top_k, d_model)
        layer_out = jnp.sum(gate_loc[:, :, None] * y_rows, axis=1).astype(jnp.bfloat16)
        grad_gates = jnp.einsum('tkd,td->tk', y_rows, dy_loc, preferred_element_type=jnp.float32)
        gate_slot = jnp.concatenate([gate_loc.reshape(-1), jnp.zeros((1,), jnp.float32)])[filler]
        dy_slot = jnp.concatenate([dy_loc, zero_row])[tok_ids]
        send_dy = (gate_slot[:, None] * dy_slot).astype(jnp.bfloat16).reshape(group_size, send_rows, d_model)
        dy_recv = exchange(send_dy, ei_size, eo_size).reshape(group_size, exp_dev, capacity, d_model)
        d_hidden = jnp.einsum('secd,efd->secf', dy_recv, w_down, preferred_element_type=jnp.float32)
        d_up = (d_hidden * h_gate * sig_gate).astype(jnp.bfloat16)
        d_gate = (d_hidden * h_up * sig_gate * (1.0 + h_gate * (1.0 - sig_gate))).astype(jnp.bfloat16)
        dx_expert = (jnp.einsum('secf,edf->secd', d_gate, w_gate, preferred_element_type=jnp.float32) + jnp.einsum('secf,edf->secd', d_up, w_up, preferred_element_type=jnp.float32)).astype(jnp.bfloat16)
        grad_w_gate = jnp.einsum('secd,secf->edf', x_recv, d_gate, preferred_element_type=jnp.float32).astype(jnp.bfloat16)
        grad_w_up = jnp.einsum('secd,secf->edf', x_recv, d_up, preferred_element_type=jnp.float32).astype(jnp.bfloat16)
        grad_w_down = jnp.einsum('secf,secd->efd', hidden, dy_recv, preferred_element_type=jnp.float32).astype(jnp.bfloat16)
        dx_back = exchange(dx_expert.reshape(group_size, send_rows, d_model), ei_size, eo_size)
        dx_rows = dx_back.reshape(num_experts * capacity, d_model)[slot_of].reshape(tok_dev, top_k, d_model)
        grad_tokens = jnp.sum(dx_rows.astype(jnp.float32), axis=1).astype(jnp.bfloat16)
        return layer_out, grad_tokens, grad_gates, grad_w_gate, grad_w_up, grad_w_down

    return jax.shard_map(device_step, mesh=mesh, in_specs=(tok_spec, tok_spec, tok_spec, exp_spec, exp_spec, exp_spec, tok_spec), out_specs=(tok_spec, tok_spec, tok_spec, tok_spec, tok_spec, tok_spec), check_vma=False)
```

profile of v0, /device:TPU:0, one launch (start us, length us, event | category | flops | bytes accessed | tf_op | source)
XLA Modules:
  0.0 2424.0 jit_solution(3802877349728158995)
XLA Ops:
  0.6 0.8 copy.60
  1.5 0.1 reshape.188
  1.6 0.1 reshape.189
  1.7 7.6 scatter_custom_fusion
  9.3 0.1 copy.62
  9.5 0.1 reduce.2
  9.6 0.7 fusion.58
  10.3 4.4 sort.17
  14.7 0.6 compare_select_fusion.11
  15.3 4.5 gather_fusion
  19.8 4.4 compare_select_fusion.4
  24.2 0.1 compare_reduce_fusion.8
  24.3 6.3 add_subtract_fusion
  30.6 4.3 scatter_custom_fusion.1
  35.0 1.3 concatenate.9
  36.3 21.0 gather_fusion.1
  57.3 14.1 copy.63
  71.4 7.1 all-to-all-start
  78.5 0.1 copy.59
  78.7 0.6 copy-done
  79.3 0.1 reshape.198
  79.5 23.0 gather_fusion.3
  102.5 0.1 concatenate.11
  102.7 20.8 gather_fusion.4
  123.4 14.7 fusion
  138.1 123.9 %all-to-all-done = bf16[4,4,256,2048]{3,2,0,1:T(8,128)(2,1)} async-done(((bf16[4,4,256,2048]{3,2,0,1:T(8,128)(2,1)}), bf16[4,4,256,2048]{3,2,0,1:T(8,128)(2,1)}, u32[]{:S(2)}, u32[]{:S(2)}) %all-to-all-start) | async-done | bytes 16777248 | tf_op jit(solution)/shard_map/all_to_all | solution.py:22
  262.0 7.0 all-to-all-start.4
  268.9 14.1 copy.64
  283.1 168.6 %all-to-all-done.4 = bf16[4,4,256,2048]{3,2,0,1:T(8,128)(2,1)} async-done(((bf16[4,4,256,2048]{3,2,0,1:T(8,128)(2,1)}), bf16[4,4,256,2048]{3,2,0,1:T(8,128)(2,1)}, u32[]{:S(2)}, u32[]{:S(2)}) %all-to-all-start.4) | async-done | bytes 16777248 | tf_op jit(solution)/shard_map/all_to_all | solution.py:22
  451.6 7.0 all-to-all-start.1
  458.6 14.1 copy.70
  472.7 349.1 %all-to-all-done.1 = bf16[4,4,256,2048]{3,2,1,0:T(8,128)(2,1)} async-done(((bf16[4,4,256,2048]{3,2,1,0:T(8,128)(2,1)}), bf16[4,4,256,2048]{3,2,1,0:T(8,128)(2,1)}, u32[]{:S(2)}, u32[]{:S(2)}) %all-to-all-start.1) | async-done | bytes 16777248 | tf_op jit(solution)/shard_map/all_to_all | solution.py:23
  821.9 7.6 all-to-all-start.5
  829.5 33.2 %fusion.40 = f32[16,256,1408]{2,1,0:T(8,128)} fusion(bf16[16,256,2048]{2,1,0:T(8,128)(2,1)} %bitcast.23, bf16[1,2048,1408]{2,1,0:T(8,128)(2,1)} %param.11), kind=kOutput, calls=%fused_computation.50 | convolution fusion | flops 23622320128 | bytes 45613056 | tf_op jit(solution)/shard_map/secd,edf->secf/dot_general | solution.py:46
  862.7 31.3 %fusion.43 = f32[16,256,1408]{2,1,0:T(8,128)} fusion(bf16[16,256,2048]{2,1,0:T(8,128)(2,1)} %bitcast.23, bf16[1,2048,1408]{2,1,0:T(8,128)(2,1)S(1)} %bitcast.186), kind=kOutput, calls=%fused_computation.53 | convolution fusion | flops 23622320128 | bytes 45613056 | tf_op jit(solution)/shard_map/secd,edf->secf/dot_general | solution.py:45
  894.0 297.5 %all-to-all-done.5 = bf16[4,4,256,2048]{3,2,1,0:T(8,128)(2,1)} async-done(((bf16[4,4,256,2048]{3,2,1,0:T(8,128)(2,1)}), bf16[4,4,256,2048]{3,2,1,0:T(8,128)(2,1)}, u32[]{:S(2)}, u32[]{:S(2)}) %all-to-all-start.5) | async-done | bytes 16777248 | tf_op jit(solution)/shard_map/all_to_all | solution.py:23
  1191.5 44.6 %fusion.5 = (bf16[16,1,256,1408]{3,2,0,1:T(8,128)(2,1)}, bf16[16,1,256,1408]{3,2,0,1:T(8,128)(2,1)}, bf16[16,1,256,1408]{3,2,0,1:T(8,128)(2,1)}) fusion(f32[16,256,1408]{2,1,0:T(8,128)} %fusion.43, f32[16,256,1408]{2,1,0:T(8,128)} %fusion.40, bf16[16,256,2048]{2,1,0:T(8,128)(2,1)} %bitcast.45, bf16[1,1408,2048]{2,1,0:T(8,128)(2,1)} %param.12), kind=kOutput, calls=%fused_computation.18 | convolution fusion | flops 23714594816 | bytes 103284736 | tf_op jit(solution)/shard_map/secd,efd->secf/dot_general | solution.py:58
  1236.1 30.2 %convolution_convert_fusion = bf16[16,256,2048]{2,1,0:T(8,128)(2,1)S(1)} fusion(bf16[16,1,256,1408]{3,2,0,1:T(8,128)(2,1)} %get-tuple-element.23, bf16[1,1408,2048]{2,1,0:T(8,128)(2,1)} %param.12), kind=kOutput, calls=%fused_computation.28 | convolution fusion | flops 23630708736 | bytes 34078720 | tf_op jit(solution)/shard_map/secf,efd->secd/dot_general | solution.py:49
  1266.3 6.6 copy.65
  1272.9 7.2 all-to-all-start.2
  1280.1 33.5 %fusion.16 = f32[16,256,2048]{2,1,0:T(8,128)} fusion(bf16[16,1,256,1408]{3,2,0,1:T(8,128)(2,1)} %get-tuple-element.22, bf16[1,2048,1408]{2,1,0:T(8,128)(2,1)} %param.10), kind=kOutput, calls=%fused_computation.37 | convolution fusion | flops 23622320128 | bytes 50855936 | tf_op jit(solution)/shard_map/secf,edf->secd/dot_general | solution.py:61
  1313.6 34.7 %add_convert_fusion = bf16[16,256,2048]{2,1,0:T(8,128)(2,1)} fusion(f32[16,256,2048]{2,1,0:T(8,128)} %fusion.16, bf16[16,1,256,1408]{3,2,0,1:T(8,128)(2,1)} %get-tuple-element.21, bf16[1,2048,1408]{2,1,0:T(8,128)(2,1)} %param.11), kind=kOutput, calls=%fused_computation.11 | convolution fusion | flops 23639097344 | bytes 67633152 | tf_op jit(solution)/shard_map/secf,edf->secd/dot_general | solution.py:61
  1348.3 14.1 copy.71
  1362.4 100.4 %all-to-all-done.2 = bf16[4,4,256,2048]{3,2,0,1:T(8,128)(2,1)} async-done(((bf16[4,4,256,2048]{3,2,0,1:T(8,128)(2,1)}), bf16[4,4,256,2048]{3,2,0,1:T(8,128)(2,1)}, u32[]{:S(2)}, u32[]{:S(2)}) %all-to-all-start.2) | async-done | bytes 16777248 | tf_op jit(solution)/shard_map/all_to_all | solution.py:22
  1462.8 7.0 all-to-all-start.6
  1469.8 14.1 copy.66
  1483.9 168.6 %all-to-all-done.6 = bf16[4,4,256,2048]{3,2,0,1:T(8,128)(2,1)} async-done(((bf16[4,4,256,2048]{3,2,0,1:T(8,128)(2,1)}), bf16[4,4,256,2048]{3,2,0,1:T(8,128)(2,1)}, u32[]{:S(2)}, u32[]{:S(2)}) %all-to-all-start.6) | async-done | bytes 16777248 | tf_op jit(solution)/shard_map/all_to_all | solution.py:22
  1652.5 7.0 all-to-all-start.3
  1659.5 14.1 copy.72
  1673.6 348.4 %all-to-all-done.3 = bf16[4,4,256,2048]{3,2,1,0:T(8,128)(2,1)} async-done(((bf16[4,4,256,2048]{3,2,1,0:T(8,128)(2,1)}), bf16[4,4,256,2048]{3,2,1,0:T(8,128)(2,1)}, u32[]{:S(2)}, u32[]{:S(2)}) %all-to-all-start.3) | async-done | bytes 16777248 | tf_op jit(solution)/shard_map/all_to_all | solution.py:23
  2022.0 7.0 all-to-all-start.7
  2029.0 4.5 scatter_custom_fusion.2
  2033.5 32.0 %fusion.33 = bf16[1,1408,2048]{2,1,0:T(8,128)(2,1)} fusion(bf16[16,256,2048]{2,1,0:T(8,128)(2,1)} %bitcast.45, bf16[16,1,256,1408]{3,2,0,1:T(8,128)(2,1)} %get-tuple-element.23), kind=kOutput, calls=%fused_computation.45 | convolution fusion | flops 23625203712 | bytes 34078720 | tf_op jit(solution)/shard_map/secf,secd->efd/dot_general | solution.py:64
  2065.5 33.8 %fusion.30 = bf16[1,2048,1408]{2,1,0:T(8,128)(2,1)} fusion(bf16[16,256,2048]{2,1,0:T(8,128)(2,1)} %bitcast.23, bf16[16,1,256,1408]{3,2,0,1:T(8,128)(2,1)} %get-tuple-element.21), kind=kOutput, calls=%fused_computation.44 | convolution fusion | flops 23625203712 | bytes 34078720 | tf_op jit(solution)/shard_map/secd,secf->edf/dot_general | solution.py:63
  2099.3 30.4 %fusion.27 = bf16[1,2048,1408]{2,1,0:T(8,128)(2,1)} fusion(bf16[16,256,2048]{2,1,0:T(8,128)(2,1)} %bitcast.23, bf16[16,1,256,1408]{3,2,0,1:T(8,128)(2,1)S(1)} %bitcast.188), kind=kOutput, calls=%fused_computation.43 | convolution fusion | flops 23625203712 | bytes 34078720 | tf_op jit(solution)/shard_map/secd,secf->edf/dot_general | solution.py:62
  2129.7 16.8 gather_fusion.2
  2146.6 7.4 reshape.197
  2154.0 7.7 fusion.45
  2161.7 0.7 copy.77
  2162.4 10.0 multiply_reduce_fusion
  2172.5 218.6 %all-to-all-done.7 = bf16[4,4,256,2048]{3,2,1,0:T(8,128)(2,1)} async-done(((bf16[4,4,256,2048]{3,2,1,0:T(8,128)(2,1)}), bf16[4,4,256,2048]{3,2,1,0:T(8,128)(2,1)}, u32[]{:S(2)}, u32[]{:S(2)}) %all-to-all-start.7) | async-done | bytes 16777248 | tf_op jit(solution)/shard_map/all_to_all | solution.py:23
  2391.1 17.0 gather_fusion.5
  2408.1 7.2 reshape.202
  2415.3 8.3 reduce_sum.22
  (32 shorter events, 0.2 us)
Async XLA Ops:
  71.4 7.1 copy-start.4
  71.4 190.6 %all-to-all-start = ((bf16[4,4,256,2048]{3,2,0,1:T(8,128)(2,1)}), bf16[4,4,256,2048]{3,2,0,1:T(8,128)(2,1)}, u32[]{:S(2)}, u32[]{:S(2)}) async-start(bf16[4,4,256,2048]{3,2,0,1:T(8,128)(2,1)} %copy.63), calls=%async_computation | async-start | bytes 33554432 | tf_op jit(solution)/shard_map/all_to_all | solution.py:22
  78.5 24.0 copy-start.2
  78.7 0.7 copy-start
  262.0 189.7 %all-to-all-start.4 = ((bf16[4,4,256,2048]{3,2,0,1:T(8,128)(2,1)}), bf16[4,4,256,2048]{3,2,0,1:T(8,128)(2,1)}, u32[]{:S(2)}, u32[]{:S(2)}) async-start(bf16[4,4,256,2048]{3,2,0,1:T(8,128)(2,1)} %fusion), calls=%async_computation.4 | async-start | bytes 33554432 | tf_op jit(solution)/shard_map/all_to_all | solution.py:22
  451.6 370.2 %all-to-all-start.1 = ((bf16[4,4,256,2048]{3,2,1,0:T(8,128)(2,1)}), bf16[4,4,256,2048]{3,2,1,0:T(8,128)(2,1)}, u32[]{:S(2)}, u32[]{:S(2)}) async-start(bf16[4,4,256,2048]{3,2,1,0:T(8,128)(2,1)} %copy.64), calls=%async_computation.1 | async-start | bytes 33554432 | tf_op jit(solution)/shard_map/all_to_all | solution.py:23
  821.9 40.8 %slice-start = ((s8[5767168]{0:T(1024)(128)(4,1)}), s8[1572864]{0:T(1024)(128)(4,1)S(1)}, s32[]{:S(2)}) async-start(s8[5767168]{0:T(1024)(128)(4,1)} %bitcast.185), calls=%async_computation.8 | async-start | bytes 3145728
  821.9 369.6 %all-to-all-start.5 = ((bf16[4,4,256,2048]{3,2,1,0:T(8,128)(2,1)}), bf16[4,4,256,2048]{3,2,1,0:T(8,128)(2,1)}, u32[]{:S(2)}, u32[]{:S(2)}) async-start(bf16[4,4,256,2048]{3,2,1,0:T(8,128)(2,1)} %copy.70), calls=%async_computation.5 | async-start | bytes 33554432 | tf_op jit(solution)/shard_map/all_to_all | solution.py:23
  829.5 33.2 %slice-start.1 = ((s8[5767168]{0:T(1024)(128)(4,1)}), s8[4194304]{0:T(1024)(128)(4,1)S(1)}, s32[]{:S(2)}) async-start(s8[5767168]{0:T(1024)(128)(4,1)} %bitcast.185), calls=%async_computation.9 | async-start | bytes 8388608
  1272.9 189.9 %all-to-all-start.2 = ((bf16[4,4,256,2048]{3,2,0,1:T(8,128)(2,1)}), bf16[4,4,256,2048]{3,2,0,1:T(8,128)(2,1)}, u32[]{:S(2)}, u32[]{:S(2)}) async-start(bf16[4,4,256,2048]{3,2,0,1:T(8,128)(2,1)} %copy.65), calls=%async_computation.2 | async-start | bytes 33554432 | tf_op jit(solution)/shard_map/all_to_all | solution.py:22
  1462.8 189.7 %all-to-all-start.6 = ((bf16[4,4,256,2048]{3,2,0,1:T(8,128)(2,1)}), bf16[4,4,256,2048]{3,2,0,1:T(8,128)(2,1)}, u32[]{:S(2)}, u32[]{:S(2)}) async-start(bf16[4,4,256,2048]{3,2,0,1:T(8,128)(2,1)} %copy.71), calls=%async_computation.6 | async-start | bytes 33554432 | tf_op jit(solution)/shard_map/all_to_all | solution.py:22
  1652.5 369.5 %all-to-all-start.3 = ((bf16[4,4,256,2048]{3,2,1,0:T(8,128)(2,1)}), bf16[4,4,256,2048]{3,2,1,0:T(8,128)(2,1)}, u32[]{:S(2)}, u32[]{:S(2)}) async-start(bf16[4,4,256,2048]{3,2,1,0:T(8,128)(2,1)} %copy.66), calls=%async_computation.3 | async-start | bytes 33554432 | tf_op jit(solution)/shard_map/all_to_all | solution.py:23
  2022.0 369.0 %all-to-all-start.7 = ((bf16[4,4,256,2048]{3,2,1,0:T(8,128)(2,1)}), bf16[4,4,256,2048]{3,2,1,0:T(8,128)(2,1)}, u32[]{:S(2)}, u32[]{:S(2)}) async-start(bf16[4,4,256,2048]{3,2,1,0:T(8,128)(2,1)} %copy.72), calls=%async_computation.7 | async-start | bytes 33554432 | tf_op jit(solution)/shard_map/all_to_all | solution.py:23
  2033.5 65.8 %slice-start.2 = ((s8[11534336]{0:T(1024)(128)(4,1)}), s8[4194304]{0:T(1024)(128)(4,1)S(1)}, s32[]{:S(2)}) async-start(s8[11534336]{0:T(1024)(128)(4,1)} %bitcast.187), calls=%async_computation.10 | async-start | bytes 8388608
  2033.5 65.8 %slice-start.3 = ((s8[11534336]{0:T(1024)(128)(4,1)}), s8[4194304]{0:T(1024)(128)(4,1)S(1)}, s32[]{:S(2)}) async-start(s8[11534336]{0:T(1024)(128)(4,1)} %bitcast.187), calls=%async_computation.11 | async-start | bytes 8388608
  2065.5 33.8 %slice-start.4 = ((s8[11534336]{0:T(1024)(128)(4,1)}), s8[3145728]{0:T(1024)(128)(4,1)S(1)}, s32[]{:S(2)}) async-start(s8[11534336]{0:T(1024)(128)(4,1)} %bitcast.187), calls=%async_computation.12 | async-start | bytes 6291456
  2129.7 24.3 %copy-start.3 = (bf16[256,2048]{1,0:T(8,128)(2,1)S(1)}, bf16[256,2048]{1,0:T(8,128)(2,1)}, u32[]{:S(2)}) copy-start(bf16[256,2048]{1,0:T(8,128)(2,1)} %param.13) | copy-start | bytes 3145732
  2146.6 15.9 copy-start.1
where the time goes:
time: 2430 us; the launch traced here: 2420 us
  waiting for transfers between devices  1770 us (73%)
  matrix products  311 us (13%)
  local copies, waits for them, and re-layouts  223 us (9%)
  starting transfers between devices  56.8 us (2%)
  other arithmetic  56.6 us (2%)
    all_to_all x4, waiting for transfers between devices, exchange(): peer_grid = lax.all_to_all(peer_grid, 'ei', 0, 0, tiled=True)  1210 us
    all_to_all x4, waiting for transfers between devices, exchange(): peer_grid = lax.all_to_all(peer_grid, 'eo', 1, 1, tiled=True)  561 us
    all_to_all x4, local copies, waits for them, and re-layouts, exchange(): peer_grid = lax.all_to_all(peer_grid, 'eo', 1, 1, tiled=True)  56.5 us
  transfers between devices with their start and end apart: 8, of which 8 were waited for; matrix products, arithmetic and copies ran while one was open for 17% of the time, Pallas kernels for 0%

commit v1 on v0

v1 whole, which is shorter than its diff:
```python
import jax
import jax.numpy as jnp
from jax import lax
from jax.sharding import PartitionSpec as P


def solution(mesh):
    axes = ('ei', 'eo')
    eo_size = mesh.shape['eo']
    tok_spec = P(('dp', 'ei', 'eo'))
    exp_spec = P(('ei', 'eo'))

    def device_step(tok_loc, idx_loc, gate_loc, w_gate, w_up, w_down, dy_loc):
        me = lax.axis_index('ei') * eo_size + lax.axis_index('eo')
        w_gate, w_up, w_down = w_gate[0], w_up[0], w_down[0]
        x = lax.all_gather(tok_loc, axes, axis=0, tiled=True)
        dy = lax.all_gather(dy_loc, axes, axis=0, tiled=True)
        idx = lax.all_gather(idx_loc, axes, axis=0, tiled=True)
        gates = lax.all_gather(gate_loc, axes, axis=0, tiled=True)
        hit = idx == me
        routed = jnp.any(hit, axis=1, keepdims=True)
        gate = jnp.sum(jnp.where(hit, gates, 0.0), axis=1, keepdims=True)
        f32 = jnp.float32
        a = jnp.where(routed, jnp.dot(x, w_gate, preferred_element_type=f32), 0.0)
        b = jnp.where(routed, jnp.dot(x, w_up, preferred_element_type=f32), 0.0)
        s = jax.nn.sigmoid(a)
        h = (a * s * b).astype(jnp.bfloat16)
        o = jnp.dot(h, w_down, preferred_element_type=f32).astype(jnp.bfloat16).astype(f32)
        layer_out = lax.psum_scatter(gate * o, axes, scatter_dimension=0, tiled=True).astype(jnp.bfloat16)
        dyf = dy.astype(f32)
        dg_tok = jnp.sum(dyf * o, axis=1)
        dg_all = lax.all_gather(dg_tok.reshape(16, -1)[:, None, :], axes, axis=1, tiled=True)
        mine = lax.dynamic_index_in_dim(dg_all, me, 0, keepdims=False)
        grad_gates = jnp.take_along_axis(mine.T, idx_loc, axis=1)
        u = (gate * dyf).astype(jnp.bfloat16)
        q = lax.dot_general(u, w_down, (((1,), (1,)), ((), ())), preferred_element_type=f32)
        du = (q * a * s).astype(jnp.bfloat16)
        dg = (q * b * s * (1.0 + a * (1.0 - s))).astype(jnp.bfloat16)
        nt = (((1,), (1,)), ((), ()))
        tn = (((0,), (0,)), ((), ()))
        dx = (lax.dot_general(dg, w_gate, nt, preferred_element_type=f32) + lax.dot_general(du, w_up, nt, preferred_element_type=f32)).astype(jnp.bfloat16).astype(f32)
        grad_tokens = lax.psum_scatter(dx, axes, scatter_dimension=0, tiled=True).astype(jnp.bfloat16)
        gwg = lax.dot_general(x, dg, tn, preferred_element_type=f32).astype(jnp.bfloat16)
        gwu = lax.dot_general(x, du, tn, preferred_element_type=f32).astype(jnp.bfloat16)
        gwd = lax.dot_general(h, u, tn, preferred_element_type=f32).astype(jnp.bfloat16)
        return layer_out, grad_tokens, grad_gates, gwg[None], gwu[None], gwd[None]

    return jax.shard_map(device_step, mesh=mesh, in_specs=(tok_spec, tok_spec, tok_spec, exp_spec, exp_spec, exp_spec, tok_spec), out_specs=(tok_spec, tok_spec, tok_spec, tok_spec, tok_spec, tok_spec), check_vma=False)
```

time: 2430 us -> 1040 us (0.43)
  waiting for transfers between devices: 1770 us -> 597 us
  local copies, waits for them, and re-layouts: 223 us -> 30.4 us
  blocking collectives: 0 us -> 63.1 us
  starting transfers between devices: 56.8 us -> 0.16 us
  other arithmetic: 56.6 us -> 5.12 us
    all_to_all x8 -> x0, waiting for transfers between devices: 1770 us -> none  [the longest x4 1210 us: exchange(): peer_grid = lax.all_to_all(peer_grid, 'ei', 0, 0, tiled=True)]
    reduce_scatter x0 -> x2, waiting for transfers between devices: none -> 443 us  [the longest x1 329 us: device_step(): lax.psum_scatter(dx, axes, scatter_dimension=0, tiled=True)]
    all_gather x0 -> x2, waiting for transfers between devices: none -> 153 us  [the longest x1 87.2 us: device_step(): x = lax.all_gather(tok_loc, axes, axis=0, tiled=True)]
    gather x7 -> x5, local copies, waits for them, and re-layouts: 104 us -> 9.32 us  [device_step(): grad_gates = jnp.take_along_axis(mine.T, idx_loc, axis=1)]
    all_gather x0 -> x3, blocking collectives: none -> 63.1 us  [the longest x1 23.5 us: device_step(): gates = lax.all_gather(gate_loc, axes, axis=0, tiled=True)]
    all_to_all x8 -> x0, starting transfers between devices: 56.8 us -> none  [the longest x4 28.6 us: exchange(): peer_grid = lax.all_to_all(peer_grid, 'ei', 0, 0, tiled=True)]
    all_to_all x4 -> x0, local copies, waits for them, and re-layouts: 56.5 us -> none  [exchange(): peer_grid = lax.all_to_all(peer_grid, 'eo', 1, 1, tiled=True)]
    another operation x4 -> x1, local copies, waits for them, and re-layouts: 34.9 us -> 0.01 us  [device_step(): dg_tok.reshape(16, -1)[:, None, :]]
  transfers between devices with their start and end apart: 8 -> 4, of which waited for: 8 -> 4; matrix products, arithmetic and copies ran while one was open for 17% -> 25% of each run, Pallas kernels for 0% -> 0%
where the time goes in v1:
time: 1040 us; the launch traced here: 1030 us
  waiting for transfers between devices  597 us (57%)
  matrix products  316 us (30%)
  blocking collectives  63.1 us (6%)
  local copies, waits for them, and re-layouts  30.4 us (3%)
  between operations  14.3 us (1%)
    reduce_scatter x1, waiting for transfers between devices, device_step(): lax.psum_scatter(dx, axes, scatter_dimension=0, tiled=True)  329 us
    reduce_scatter x1, waiting for transfers between devices, device_step(): lax.psum_scatter(gate * o, axes, scatter_dimension=0, tiled=True)  115 us
    all_gather x1, waiting for transfers between devices, device_step(): x = lax.all_gather(tok_loc, axes, axis=0, tiled=True)  87.2 us
    all_gather x1, waiting for transfers between devices, device_step(): dy = lax.all_gather(dy_loc, axes, axis=0, tiled=True)  66 us
    dot_general x1, matrix products, device_step(): lax.dot_general(u, w_down, (((1,), (1,)), ((), ())), preferred_element_ty...  49.7 us
    dot_general x1, matrix products, device_step(): jnp.dot(h, w_down, preferred_element_type=f32).astype(jnp.bfloat16)  36.8 us
    dot_general x1, matrix products, device_step(): lax.dot_general(du, w_up, nt, preferred_element_type=f32)  36.6 us
    dot_general x1, matrix products, device_step(): lax.dot_general(dg, w_gate, nt, preferred_element_type=f32)  33.7 us
  transfers between devices with their start and end apart: 4, of which 4 were waited for; matrix products, arithmetic and copies ran while one was open for 25% of the time, Pallas kernels for 0%

profile of v1, /device:TPU:0, one launch (start us, length us, event | category | flops | bytes accessed | tf_op | source)
XLA Modules:
  0.0 1026.2 jit_solution(1794272171645669317)
XLA Ops:
  7.2 0.0 all-gather.3.cloned.1.call-start
  7.2 0.7 all-gather.3.cloned.1.call-update
  7.9 0.0 all-gather.5.cloned.1.call-start
  7.9 2.3 copy.37
  10.2 0.0 all-gather.5.cloned.1.call-update
  10.2 0.0 reduce-scatter.3.cloned.1.call-start
  10.3 23.5 %all_gather.16 = f32[4096,4]{0,1:T(4,128)S(1)} all-gather(f32[256,4]{0,1:T(4,128)} %param.9), channel_id=1, replica_groups=mesh['dp'=2,'ei'=4,'eo'=4] {'ei','eo'}, dimensions={0}, use_global_device_ids=true | all-gather | bytes 69632 | tf_op jit(solution)/shard_map/all_gather | solution.py:19
  33.8 17.9 %all_gather.15 = s32[4096,4]{0,1:T(4,128)S(1)} all-gather(s32[256,4]{0,1:T(4,128)} %param.8), channel_id=1, replica_groups=mesh['dp'=2,'ei'=4,'eo'=4] {'ei','eo'}, dimensions={0}, use_global_device_ids=true | all-gather | bytes 69632 | tf_op jit(solution)/shard_map/all_gather | solution.py:18
  51.7 0.1 select_reduce_fusion
  51.8 0.0 copy-start.1
  51.8 0.1 reduce_or.9
  51.9 87.2 %all-gather.3.cloned.1.call-done = bf16[4096,2048]{1,0:T(8,128)(2,1)} async-done(((bf16[256,2048]{1,0:T(8,128)(2,1)}), bf16[4096,2048]{1,0:T(8,128)(2,1)}) %all-gather.3.cloned.1.call-update) | async-done | bytes 16777232 | tf_op jit(solution)/shard_map/all_gather | solution.py:16
  139.1 0.0 copy-start.3
  139.1 33.1 %fusion.22 = f32[4096,1408]{1,0:T(8,128)} fusion(bf16[4096,2048]{1,0:T(8,128)(2,1)} %all-gather.3.cloned.1.call-done, bf16[1,2048,1408]{2,1,0:T(8,128)(2,1)} %param.10), kind=kOutput, calls=%fused_computation.28 | convolution fusion | flops 23622320128 | bytes 45613056 | tf_op jit(solution)/shard_map/dot_general | solution.py:24
  172.2 0.0 copy-done.3
  172.2 31.6 %fusion.18 = f32[4096,1408]{1,0:T(8,128)} fusion(bf16[4096,2048]{1,0:T(8,128)(2,1)S(1)} %copy-done.3, bf16[1,2048,1408]{2,1,0:T(8,128)(2,1)} %param.11), kind=kOutput, calls=%fused_computation.24 | convolution fusion | flops 23622320128 | bytes 45613056 | tf_op jit(solution)/shard_map/dot_general | solution.py:25
  203.9 66.0 %all-gather.5.cloned.1.call-done = bf16[4096,2048]{0,1:T(8,128)(2,1)} async-done(((bf16[256,2048]{0,1:T(8,128)(2,1)}), bf16[4096,2048]{0,1:T(8,128)(2,1)}) %all-gather.5.cloned.1.call-update) | async-done | bytes 16777232 | tf_op jit(solution)/shard_map/all_gather | solution.py:17
  269.9 49.7 %multiply_convert_fusion = (bf16[4096,1408]{1,0:T(8,128)(2,1)}, bf16[4096,1408]{1,0:T(8,128)(2,1)}, bf16[4096,1408]{1,0:T(8,128)(2,1)}) fusion(f32[4096,1408]{1,0:T(8,128)} %fusion.22, pred[4096]{0:T(1024)(128)(4,1)S(1)} %reduce_or.9, f32[4096,1408]{1,0:T(8,128)} %fusion.18, bf16[1,1408,2048]{2,1,0:T(8,128)(2,1)} %param.12, ...), kind=kOutput, calls=%fused_computation.7 | convolution fusion | flops 23751294976 | bytes 103305216 | tf_op jit(solution)/shard_map/dot_general | solution.py:36
  319.5 0.0 copy-done.1
  319.5 36.8 %fusion.1 = (f32[4096]{0:T(1024)S(1)}, f32[4096,2048]{0,1:T(8,128)}) fusion(bf16[4096,2048]{0,1:T(8,128)(2,1)} %all-gather.5.cloned.1.call-done, f32[4096]{0:T(1024)S(1)} %get-tuple-element.30, bf16[4096,1408]{1,0:T(8,128)(2,1)} %get-tuple-element.34, bf16[1,1408,2048]{2,1,0:T(8,128)(2,1)} %param.12), kind=kOutput, calls=%fused_computation.5 | convolution fusion | flops 23672647680 | bytes 67665920 | tf_op jit(solution)/shard_map/dot_general | solution.py:28
  356.3 0.0 reduce-scatter.3.cloned.1.call-update
  356.3 0.0 reduce-scatter.5.cloned.1.call-start
  356.4 33.7 %fusion.20 = f32[4096,2048]{1,0:T(8,128)} fusion(bf16[4096,1408]{1,0:T(8,128)(2,1)} %get-tuple-element.33, bf16[1,2048,1408]{2,1,0:T(8,128)(2,1)} %param.10), kind=kOutput, calls=%fused_computation.26 | convolution fusion | flops 23622320128 | bytes 50855936 | tf_op jit(solution)/shard_map/dot_general | solution.py:41
  390.1 36.6 %fusion.2 = f32[4096,2048]{1,0:T(8,128)} fusion(f32[4096,2048]{1,0:T(8,128)} %fusion.20, bf16[4096,1408]{1,0:T(8,128)(2,1)} %get-tuple-element.32, bf16[1,2048,1408]{2,1,0:T(8,128)(2,1)} %param.11), kind=kOutput, calls=%fused_computation.12 | convolution fusion | flops 23647485952 | bytes 84410368 | tf_op jit(solution)/shard_map/dot_general | solution.py:41
  426.6 0.0 copy-start
  426.6 0.0 reduce-scatter.5.cloned.1.call-update
  426.6 0.7 copy-done
  427.3 0.1 copy.38
  427.5 0.1 reshape.24
  427.6 21.6 %all_gather.19 = f32[16,16,256]{2,0,1:T(8,128)S(1)} all-gather(f32[16,1,256]{2,0,1:T(8,128)S(1)} %broadcast_in_dim_reshape.3), channel_id=1, replica_groups=mesh['dp'=2,'ei'=4,'eo'=4] {'ei','eo'}, dimensions={1}, use_global_device_ids=true | all-gather | bytes 278528 | tf_op jit(solution)/shard_map/all_gather | solution.py:32
  449.3 8.9 gather_fusion
  458.1 0.1 reshape.27
  458.3 0.1 copy.39
  458.3 31.4 %fusion.10 = bf16[1,2048,1408]{1,2,0:T(8,128)(2,1)} fusion(bf16[4096,1408]{1,0:T(8,128)(2,1)} %get-tuple-element.33, bf16[4096,2048]{1,0:T(8,128)(2,1)} %all-gather.3.cloned.1.call-done), kind=kOutput, calls=%fused_computation.18 | convolution fusion | flops 23625203712 | bytes 34078720 | tf_op jit(solution)/shard_map/dot_general | solution.py:43
  489.7 8.3 copy.41
  498.0 0.0 copy-start.2
  498.0 31.4 %fusion.11 = bf16[1,2048,1408]{1,2,0:T(8,128)(2,1)} fusion(bf16[4096,1408]{1,0:T(8,128)(2,1)} %get-tuple-element.32, bf16[4096,2048]{1,0:T(8,128)(2,1)} %all-gather.3.cloned.1.call-done), kind=kOutput, calls=%fused_computation.19 | convolution fusion | flops 23625203712 | bytes 34078720 | tf_op jit(solution)/shard_map/dot_general | solution.py:44
  529.4 8.3 copy.42
  537.7 0.6 and_select_fusion
  538.3 0.0 copy-done.2
  538.3 31.7 %fusion.12 = bf16[1,1408,2048]{2,1,0:T(8,128)(2,1)} fusion(bf16[4096,1408]{1,0:T(8,128)(2,1)} %get-tuple-element.34, bf16[4096,2048]{0,1:T(8,128)(2,1)} %all-gather.5.cloned.1.call-done, f32[4096]{0:T(1024)S(1)} %copy-done.2), kind=kOutput, calls=%fused_computation.20 | convolution fusion | flops 23650369536 | bytes 34095104 | tf_op jit(solution)/shard_map/dot_general | solution.py:45
  570.1 114.6 %reduce-scatter.3.cloned.1.call-done = f32[256,2048]{0,1:T(8,128)} async-done(((f32[4096,2048]{0,1:T(8,128)}), f32[256,2048]{0,1:T(8,128)}) %reduce-scatter.3.cloned.1.call-update) | async-done | bytes 2097168 | tf_op jit(solution)/shard_map/reduce_scatter | solution.py:29
  684.7 1.7 convert_element_type.51
  686.4 1.4 copy.40
  687.8 328.7 %reduce-scatter.5.cloned.1.call-done = f32[256,2048]{1,0:T(8,128)} async-done(((f32[4096,2048]{1,0:T(8,128)}), f32[256,2048]{1,0:T(8,128)}) %reduce-scatter.5.cloned.1.call-update) | async-done | bytes 2097168 | tf_op jit(solution)/shard_map/reduce_scatter | solution.py:42
  1016.5 2.7 convert_element_type.58
  (4 shorter events, 0.0 us)
Async XLA Ops:
  7.2 131.9 %all-gather.3.cloned.1.call-start = ((), (), s32[]{:S(2)}) async-start(), calls=%async_computation.2 | async-start | bytes 17825792 | tf_op jit(solution)/shard_map/all_gather | solution.py:16
  7.9 262.0 %all-gather.5.cloned.1.call-start = ((), (), s32[]{:S(2)}) async-start(), calls=%async_computation.4 | async-start | bytes 17825792 | tf_op jit(solution)/shard_map/all_gather | solution.py:17
  10.2 674.5 %reduce-scatter.3.cloned.1.call-start = ((), (), s32[]{:S(2)}) async-start(), calls=%async_computation.3 | async-start | bytes 35651584 | tf_op jit(solution)/shard_map/reduce_scatter | solution.py:29
  51.8 267.7 %copy-start.1 = (f32[4096]{0:T(1024)}, f32[4096]{0:T(1024)S(1)}, u32[]{:S(2)}) copy-start(f32[4096]{0:T(1024)S(1)} %get-tuple-element.30) | copy-start | bytes 49156
  139.1 33.1 %copy-start.3 = (bf16[4096,2048]{1,0:T(8,128)(2,1)S(1)}, bf16[4096,2048]{1,0:T(8,128)(2,1)}, u32[]{:S(2)}) copy-start(bf16[4096,2048]{1,0:T(8,128)(2,1)} %all-gather.3.cloned.1.call-done) | copy-start | bytes 50331652
  356.3 660.2 %reduce-scatter.5.cloned.1.call-start = ((), (), s32[]{:S(2)}) async-start(), calls=%async_computation.5 | async-start | bytes 35651584 | tf_op jit(solution)/shard_map/reduce_scatter | solution.py:42
  426.6 0.7 copy-start
  498.0 40.3 %copy-start.2 = (f32[4096]{0:T(1024)S(1)}, f32[4096]{0:T(1024)}, u32[]{:S(2)}) copy-start(f32[4096]{0:T(1024)} %copy-done.1) | copy-start | bytes 49156
Sparse Core Ops, SparseCore 0:
  10.1 128.8 all-gather.2
  141.8 128.0 all-gather.4
  356.5 328.2 reduce-scatter.2
  688.8 327.6 reduce-scatter.4

commit v2 on v1

v2 whole, which is shorter than its diff:
```python
import jax
import jax.numpy as jnp
from jax import lax
from jax.sharding import PartitionSpec as P


def ring_tables(ei_size, eo_size):
    chips_y = eo_size // 2
    walk = [(z, 0) for z in range(ei_size)] + [(z, 1) for z in reversed(range(ei_size))]
    assert chips_y == 2
    return [[z * eo_size + y * 2 + core for core in range(2)] for z, y in walk]


def solution(mesh):
    axes = ('ei', 'eo')
    ei_size, eo_size = mesh.shape['ei'], mesh.shape['eo']
    table = ring_tables(ei_size, eo_size)
    ring = len(table)
    half = ring // 2
    group = ei_size * eo_size
    pairs = lambda step: [(table[p][c], table[(p + step) % ring][c]) for p in range(ring) for c in range(2)]
    cw_perm, ccw_perm = pairs(1), pairs(-1)
    swap_perm = [(table[p][c], table[p][1 - c]) for p in range(ring) for c in range(2)]
    rel_order = [None] * group
    for p in range(ring):
        for c in range(2):
            rel_order[table[p][c]] = [table[(p + r) % ring][c ^ k] for r in range(ring) for k in range(2)]
    tok_spec = P(('dp', 'ei', 'eo'))
    exp_spec = P(('ei', 'eo'))
    f32 = jnp.float32
    bf16 = jnp.bfloat16
    nt = (((1,), (1,)), ((), ()))
    tn = (((0,), (0,)), ((), ()))
    chunks = [(0,)] + [(ring - k, k) for k in range(1, half)] + [(half,)]

    def cw(v):
        return lax.ppermute(v, axes, cw_perm)

    def ccw(v):
        return lax.ppermute(v, axes, ccw_perm)

    def swap(v):
        return lax.ppermute(v, axes, swap_perm)

    def gather_rings(*owns):
        width = owns[0].shape[1] // 2
        got = [[own] + [None] * (ring - 1) for own in owns]
        for k in range(1, half):
            for blocks in got:
                blocks[ring - k] = cw(blocks[(ring - k + 1) % ring])
                blocks[k] = ccw(blocks[k - 1])
        for blocks in got:
            left = cw(blocks[half + 1][:, :width])
            right = ccw(blocks[half - 1][:, width:])
            blocks[half] = jnp.concatenate([left, right], axis=1)
        return [[(v, swap(v)) for v in blocks] for blocks in got]

    def scatter_step(s, acc, term):
        if s == 0:
            return term(ring - 1, 0), term(1, 1)
        left = cw(acc[0])
        right = ccw(acc[1])
        return left + term(ring - 1 - s, 0), right + term((1 + s) % ring, 1)

    def device_step(tok_loc, idx_loc, gate_loc, w_gate, w_up, w_down, dy_loc):
        me = lax.axis_index('ei') * eo_size + lax.axis_index('eo')
        tok_dev, top_k = idx_loc.shape
        d_model = tok_loc.shape[1]
        width = d_model // 2
        w_gate, w_up, w_down = w_gate[0], w_up[0], w_down[0]

        meta = jnp.concatenate([idx_loc.astype(f32), gate_loc], axis=1)
        meta = lax.all_gather(meta, axes, axis=0, tiled=True)
        meta, tok_loc, dy_loc = lax.optimization_barrier((meta, tok_loc, dy_loc))
        meta = meta.reshape(group, tok_dev, 2 * top_k)
        x_blk, dy_blk = gather_rings(tok_loc, dy_loc)
        meta = meta[jnp.array(rel_order, jnp.int32)[me]]
        ids, gates = meta[:, :, :top_k].astype(jnp.int32), meta[:, :, top_k:]

        def gate_of(expert):
            hit = ids == expert
            return jnp.any(hit, axis=2), jnp.sum(jnp.where(hit, gates, 0.0), axis=2)

        routed, gate = gate_of(me)
        _, gate_mate = gate_of(me ^ 1)

        saved = []
        y_of, dx_of, y_mate, dx_mate = {}, {}, {}, {}

        def y_term(r, side):
            cols = slice(side * width, (side + 1) * width)
            return gate[r * 2][:, None] * y_of[r, 0][:, cols].astype(f32) + gate_mate[r * 2][:, None] * y_mate[r][:, cols].astype(f32)

        def dx_term(r, side):
            cols = slice(side * width, (side + 1) * width)
            return dx_of[r, 0][:, cols].astype(f32) + dx_mate[r][:, cols].astype(f32)

        def dot_term(r):
            dyf = dy_blk[r][0].astype(f32)
            own = jnp.sum(dyf * y_of[r, 0].astype(f32), axis=1)
            mate = jnp.sum(dyf * y_mate[r].astype(f32), axis=1)
            return jnp.where(ids[r * 2] == me, own[:, None], 0.0).T + jnp.where(ids[r * 2] == (me ^ 1), mate[:, None], 0.0).T

        y_acc = dx_acc = dot_acc = None

        def advance(s):
            nonlocal y_acc, dx_acc, dot_acc
            dot_acc = dot_term(ring - 1 - s) if s == 0 else cw(dot_acc) + dot_term(ring - 1 - s)
            y_acc = scatter_step(s, y_acc, y_term)
            dx_acc = scatter_step(s, dx_acc, dx_term)
            if s < ring - 1:
                y_acc, dx_acc, dot_acc = lax.optimization_barrier((y_acc, dx_acc, dot_acc))

        for n, offs in enumerate(chunks):
            names = [(r, k) for r in offs for k in range(2)]
            x = jnp.concatenate([x_blk[r][k] for r, k in names])
            dy = jnp.concatenate([dy_blk[r][k] for r, k in names])
            pick = lambda v: jnp.concatenate([v[r * 2 + k] for r, k in names])[:, None]
            on, g = pick(routed), pick(gate)
            a = jnp.where(on, jnp.dot(x, w_gate, preferred_element_type=f32), 0.0)
            b = jnp.where(on, jnp.dot(x, w_up, preferred_element_type=f32), 0.0)
            s = jax.nn.sigmoid(a)
            h = (a * s * b).astype(bf16)
            o = jnp.dot(h, w_down, preferred_element_type=f32).astype(bf16)
            u = (g * dy.astype(f32)).astype(bf16)
            q = lax.dot_general(u, w_down, nt, preferred_element_type=f32)
            du = (q * a * s).astype(bf16)
            dg = (q * b * s * (1.0 + a * (1.0 - s))).astype(bf16)
            dx = (lax.dot_general(dg, w_gate, nt, preferred_element_type=f32) + lax.dot_general(du, w_up, nt, preferred_element_type=f32)).astype(bf16)
            saved.append((h, u, dg, du))
            for i, (r, k) in enumerate(names):
                rows = slice(i * tok_dev, (i + 1) * tok_dev)
                y_of[r, k], dx_of[r, k] = o[rows], dx[rows]
            for r in offs:
                y_mate[r], dx_mate[r] = swap(y_of[r, 1]), swap(dx_of[r, 1])
            if n >= 1:
                advance(n - 1)

        for s in range(len(chunks) - 1, ring):
            advance(s)
        layer_out = jnp.concatenate(y_acc, axis=1).astype(bf16)
        grad_tokens = jnp.concatenate(dx_acc, axis=1).astype(bf16)
        grad_gates = dot_acc.T

        x_cat = jnp.concatenate([x_blk[r][k] for offs in chunks for r in offs for k in range(2)])
        h, u, dg, du = (jnp.concatenate(v) for v in zip(*saved))
        gwg = lax.dot_general(x_cat, dg, tn, preferred_element_type=f32).astype(bf16)
        gwu = lax.dot_general(x_cat, du, tn, preferred_element_type=f32).astype(bf16)
        gwd = lax.dot_general(h, u, tn, preferred_element_type=f32).astype(bf16)
        return layer_out, grad_tokens, grad_gates, gwg[None], gwu[None], gwd[None]

    return jax.shard_map(device_step, mesh=mesh, in_specs=(tok_spec, tok_spec, tok_spec, exp_spec, exp_spec, exp_spec, tok_spec), out_specs=(tok_spec, tok_spec, tok_spec, tok_spec, tok_spec, tok_spec), check_vma=False)
```

time: 1040 us -> 802 us (0.77)
  waiting for transfers between devices: 597 us -> 197 us
  matrix products: 316 us -> 400 us
  other arithmetic: 5.12 us -> 65.5 us
  starting transfers between devices: 0.16 us -> 58.6 us
  blocking collectives: 63.1 us -> 23.6 us
  local copies, waits for them, and re-layouts: 30.4 us -> 45.2 us
  between operations: 14.3 us -> 2.32 us
    reduce_scatter x2 -> x0, waiting for transfers between devices: 443 us -> none  [the longest x1 329 us: device_step(): lax.psum_scatter(dx, axes, scatter_dimension=0, tiled=True)]
    ppermute x0 -> x83, waiting for transfers between devices: none -> 197 us  [the longest x29 159 us: cw(): return lax.ppermute(v, axes, cw_perm)]
    all_gather x2 -> x0, waiting for transfers between devices: 153 us -> none  [the longest x1 87.2 us: device_step(): x = lax.all_gather(tok_loc, axes, axis=0, tiled=True)]
    dot_general x7 -> x23, matrix products: 246 us -> 311 us  [the longest x5 75.4 us: device_step(): a = jnp.where(on, jnp.dot(x, w_gate, preferred_element_type=f32), 0.0)]
    ppermute x0 -> x83, starting transfers between devices: none -> 58.6 us  [the longest x22 29.8 us: ccw(): return lax.ppermute(v, axes, ccw_perm)]
    all_gather x3 -> x1, blocking collectives: 63.1 us -> 23.6 us  [device_step(): meta = lax.all_gather(meta, axes, axis=0, tiled=True)]
    add x0 -> x21, other arithmetic: none -> 24.7 us  [the longest x12 20 us: scatter_step(): return (left + term(ring - 1 - s, 0), right + term((1 + s) % ring, 1))]
    unnamed x0 -> x11, other arithmetic: none -> 18.9 us
  transfers between devices with their start and end apart: 4 -> 83, of which waited for: 4 -> 25; matrix products, arithmetic and copies ran while one was open for 25% -> 64% of each run, Pallas kernels for 0% -> 0%
where the time goes in v2:
time: 802 us; the launch traced here: 793 us
  matrix products  400 us (50%)
  waiting for transfers between devices  197 us (25%)
  other arithmetic  65.5 us (8%)
  starting transfers between devices  58.6 us (7%)
  local copies, waits for them, and re-layouts  45.2 us (6%)
  blocking collectives  23.6 us (3%)
    ppermute x29, waiting for transfers between devices, cw(): return lax.ppermute(v, axes, cw_perm)  159 us
    dot_general x5, matrix products, device_step(): a = jnp.where(on, jnp.dot(x, w_gate, preferred_element_type=f32), 0.0)  75.4 us
    dot_general x5, matrix products, device_step(): q = lax.dot_general(u, w_down, nt, preferred_element_type=f32)  56.1 us
    dot_general x5, matrix products, device_step(): lax.dot_general(dg, w_gate, nt, preferred_element_type=f32)  46.3 us
    dot_general x5, matrix products, device_step(): lax.dot_general(du, w_up, nt, preferred_element_type=f32)  43.3 us
    dot_general x5, matrix products, device_step(): o = jnp.dot(h, w_down, preferred_element_type=f32).astype(bf16)  42 us
    dot_general x5, matrix products, device_step(): b = jnp.where(on, jnp.dot(x, w_up, preferred_element_type=f32), 0.0)  38.5 us
    ppermute x22, waiting for transfers between devices, ccw(): return lax.ppermute(v, axes, ccw_perm)  38.2 us
  transfers between devices with their start and end apart: 83, of which 25 were waited for; matrix products, arithmetic and copies ran while one was open for 64% of the time, Pallas kernels for 0%

profile of v2, /device:TPU:0, one launch (start us, length us, event | category | flops | bytes accessed | tf_op | source)
XLA Modules:
  0.0 792.9 jit_solution(14963050708102953913)
XLA Ops:
  2.2 23.6 %all_gather.3 = f32[4096,8]{0,1:T(8,128)S(1)} all-gather(f32[256,8]{0,1:T(8,128)S(1)} %pad_maximum_fusion.5), channel_id=1, replica_groups=mesh['dp'=2,'ei'=4,'eo'=4] {'ei','eo'}, dimensions={0}, use_global_device_ids=true | all-gather | bytes 139264 | tf_op jit(solution)/shard_map/all_gather | solution.py:73
  37.8 2.6 constant_dynamic-update-slice_fusion.32
  40.4 5.0 fusion.81
  45.5 6.3 fusion.3
  51.8 8.1 %constant_dynamic-update-slice_fusion.38 = (bf16[4096,1408]{1,0:T(8,128)(2,1)}, bf16[512,1408]{1,0:T(8,128)(2,1)S(1)}, bf16[4096,1408]{1,0:T(8,128)(2,1)}, bf16[...) fusion(f32[512,1408]{1,0:T(8,128)} %fusion.3, f32[512,1408]{1,0:T(8,128)} %fusion.81, ...), kind=kOutput, calls=%fused_computation.211 | convolution fusion | flops 2965045248 | bytes 22282752 | tf_op jit(solution)/shard_map/dot_general | solution.py:120
  60.0 5.0 fusion.23
  65.0 6.3 add_convert_fusion.3
  71.8 6.1 fusion.97
  78.3 2.5 constant_dynamic-update-slice_fusion.31
  87.2 8.4 %fusion.41 = f32[1024,1408]{1,0:T(8,128)} fusion(bf16[1024,2048]{1,0:T(8,128)(2,1)S(1)} %get-tuple-element.228, bf16[1,2048,1408]{2,1,0:T(8,128)(2,1)S(1)} %copy-done.110), kind=kOutput, calls=%fused_computation.51 | convolution fusion | flops 5905580032 | bytes 15728640 | tf_op jit(solution)/shard_map/dot_general | solution.py:121
  97.4 12.9 %fusion.19 = f32[1024,1408]{1,0:T(8,128)} fusion(bf16[1,1408,2048]{2,1,0:T(8,128)(2,1)S(1)} %bitcast.263, bf16[256,2048]{1,0:T(8,128)(2,1)S(1)} %collective-permute-done.9, bf16[256,2048]{1,0:T(8,128)(2,1)S(1)} %collective-permute-done.8, bf16[256,2048]{1,0:T(8,128)(2,1)S(1)} %collective-permute-done.7, bf16[256,2048]{1,0:T(8,128)(2,1)} %collective-permute-done.6, ...), kind=kOutput, calls=%fused_computation.29 | convolution fusion | flops 5926551552 | bytes 15732736 | tf_op jit(solution)/shard_map/dot_general | solution.py:126
  110.3 17.1 %constant_dynamic-update-slice_fusion.37 = (bf16[4096,1408]{1,0:T(8,128)(2,1)}, bf16[1024,1408]{1,0:T(8,128)(2,1)}, bf16[4096,1408]{1,0:T(8,128)(2,1)}, bf16[102...) fusion(bf16[4096,1408]{1,0:T(8,128)(2,1)} %get-tuple-element.144, ...), kind=kOutput, calls=%fused_computation.210 | convolution fusion | flops 5931532288 | bytes 38798336 | tf_op jit(solution)/shard_map/dot_general | solution.py:120
  127.4 9.7 %fusion.63 = bf16[1024,2048]{1,0:T(8,128)(2,1)S(1)} fusion(bf16[1024,1408]{1,0:T(8,128)(2,1)} %get-tuple-element.156, bf16[1,1408,2048]{2,1,0:T(8,128)(2,1)} %param.13), kind=kOutput, calls=%fused_computation.89 | convolution fusion | flops 5907677184 | bytes 12845056 | tf_op jit(solution)/shard_map/dot_general | solution.py:124
  138.7 2.4 copy-done.114
  141.1 10.9 %fusion.39 = f32[1024,2048]{1,0:T(8,128)} fusion(bf16[1024,1408]{1,0:T(8,128)(2,1)S(1)} %copy-done.114, bf16[1,2048,1408]{2,1,0:T(8,128)(2,1)} %param.12), kind=kOutput, calls=%fused_computation.49 | convolution fusion | flops 5905580032 | bytes 17039360 | tf_op jit(solution)/shard_map/dot_general | solution.py:129
  152.0 10.2 %add_convert_fusion.2 = bf16[1024,2048]{1,0:T(8,128)(2,1)S(1)} fusion(f32[1024,2048]{1,0:T(8,128)} %fusion.39, bf16[1024,1408]{1,0:T(8,128)(2,1)} %get-tuple-element.143, bf16[1,2048,1408]{2,1,0:T(8,128)(2,1)S(1)} %bitcast.275), kind=kOutput, calls=%fused_computation.5 | convolution fusion | flops 5909774336 | bytes 21233664 | tf_op jit(solution)/shard_map/dot_general | solution.py:129
  166.8 2.6 constant_dynamic-update-slice_fusion.25
  171.5 8.5 %fusion.37 = f32[1024,1408]{1,0:T(8,128)} fusion(bf16[1024,2048]{1,0:T(8,128)(2,1)S(1)} %get-tuple-element.220, bf16[1,2048,1408]{2,1,0:T(8,128)(2,1)S(1)} %bitcast.265), kind=kOutput, calls=%fused_computation.47 | convolution fusion | flops 5905580032 | bytes 15728640 | tf_op jit(solution)/shard_map/dot_general | solution.py:121
  182.1 14.3 %fusion.15 = f32[1024,1408]{1,0:T(8,128)} fusion(bf16[1,1408,2048]{2,1,0:T(8,128)(2,1)} %param.13, bf16[256,2048]{1,0:T(8,128)(2,1)S(1)} %collective-permute-done.24, bf16[256,2048]{1,0:T(8,128)(2,1)S(1)} %collective-permute-done.23, bf16[256,2048]{1,0:T(8,128)(2,1)S(1)} %collective-permute-done.22, bf16[256,2048]{1,0:T(8,128)(2,1)S(1)} %collective-permute-done.21, ...), kind=kOutput, calls=%fused_computation.25 | convolution fusion | flops 5926551552 | bytes 15732736 | tf_op jit(solution)/shard_map/dot_general | solution.py:126
  196.3 18.7 %constant_dynamic-update-slice_fusion.36 = (bf16[4096,1408]{1,0:T(8,128)(2,1)}, bf16[1024,1408]{1,0:T(8,128)(2,1)}, bf16[4096,1408]{1,0:T(8,128)(2,1)}, bf16[102...) fusion(bf16[4096,1408]{1,0:T(8,128)(2,1)} %get-tuple-element.142, ...), kind=kOutput, calls=%fused_computation.209 | convolution fusion | flops 5931532288 | bytes 38798336 | tf_op jit(solution)/shard_map/dot_general | solution.py:120
  215.0 11.9 %fusion.35 = f32[1024,2048]{1,0:T(8,128)} fusion(bf16[1024,1408]{1,0:T(8,128)(2,1)} %get-tuple-element.154, bf16[1,2048,1408]{2,1,0:T(8,128)(2,1)} %param.12), kind=kOutput, calls=%fused_computation.45 | convolution fusion | flops 5905580032 | bytes 17039360 | tf_op jit(solution)/shard_map/dot_general | solution.py:129
  226.8 10.9 %add_convert_fusion.1 = bf16[1024,2048]{1,0:T(8,128)(2,1)S(1)} fusion(f32[1024,2048]{1,0:T(8,128)} %fusion.35, bf16[1024,1408]{1,0:T(8,128)(2,1)S(1)} %copy-done.115, bf16[1,2048,1408]{2,1,0:T(8,128)(2,1)} %param.11), kind=kOutput, calls=%fused_computation.3 | convolution fusion | flops 5909774336 | bytes 21233664 | tf_op jit(solution)/shard_map/dot_general | solution.py:129
  241.7 10.0 %fusion.66 = bf16[1024,2048]{1,0:T(8,128)(2,1)S(1)} fusion(bf16[1024,1408]{1,0:T(8,128)(2,1)} %get-tuple-element.152, bf16[1,1408,2048]{2,1,0:T(8,128)(2,1)} %param.13), kind=kOutput, calls=%fused_computation.90 | convolution fusion | flops 5907677184 | bytes 12845056 | tf_op jit(solution)/shard_map/dot_general | solution.py:124
  252.2 3.4 fusion.112
  262.0 2.9 convert_add_fusion
  268.2 8.5 %collective-permute-done.53 = bf16[256,1024]{1,0:T(8,128)(2,1)S(1)} collective-permute-done((bf16[256,1024]{1,0:T(8,128)(2,1)S(1)}, bf16[256,1024]{1,0:T(8,128)(2,1)S(1)}, u32[]{:S(2)}, u32[]{:S(2)}) %collective-permute-start.53) | collective-permute-done | bytes 524320 | tf_op jit(solution)/shard_map/ppermute | solution.py:37
  281.8 8.4 %fusion.33 = f32[1024,1408]{1,0:T(8,128)} fusion(bf16[1024,2048]{1,0:T(8,128)(2,1)S(1)} %get-tuple-element.212, bf16[1,2048,1408]{2,1,0:T(8,128)(2,1)S(1)} %bitcast.267), kind=kOutput, calls=%fused_computation.43 | convolution fusion | flops 5905580032 | bytes 15728640 | tf_op jit(solution)/shard_map/dot_general | solution.py:121
  290.6 14.6 %fusion.11 = f32[1024,1408]{1,0:T(8,128)} fusion(bf16[1,1408,2048]{2,1,0:T(8,128)(2,1)} %param.13, bf16[256,2048]{1,0:T(8,128)(2,1)S(1)} %collective-permute-done.41, bf16[256,2048]{1,0:T(8,128)(2,1)S(1)} %collective-permute-done.40, bf16[256,2048]{1,0:T(8,128)(2,1)S(1)} %collective-permute-done.39, bf16[256,2048]{1,0:T(8,128)(2,1)S(1)} %collective-permute-done.38, ...), kind=kOutput, calls=%fused_computation.21 | convolution fusion | flops 5926551552 | bytes 15732736 | tf_op jit(solution)/shard_map/dot_general | solution.py:126
  305.2 18.6 %constant_dynamic-update-slice_fusion.35 = (bf16[4096,1408]{1,0:T(8,128)(2,1)}, bf16[1024,1408]{1,0:T(8,128)(2,1)}, bf16[4096,1408]{1,0:T(8,128)(2,1)}, bf16[102...) fusion(bf16[4096,1408]{1,0:T(8,128)(2,1)} %get-tuple-element.140, ...), kind=kOutput, calls=%fused_computation.208 | convolution fusion | flops 5931532288 | bytes 38798336 | tf_op jit(solution)/shard_map/dot_general | solution.py:120
  323.8 9.7 %fusion.69 = bf16[1024,2048]{1,0:T(8,128)(2,1)S(1)} fusion(bf16[1024,1408]{1,0:T(8,128)(2,1)} %get-tuple-element.148, bf16[1,1408,2048]{2,1,0:T(8,128)(2,1)} %param.13), kind=kOutput, calls=%fused_computation.91 | convolution fusion | flops 5907677184 | bytes 12845056 | tf_op jit(solution)/shard_map/dot_general | solution.py:124
  338.8 9.6 %collective-permute-done.48 = bf16[256,1024]{1,0:T(8,128)(2,1)S(1)} collective-permute-done((bf16[256,1024]{1,0:T(8,128)(2,1)S(1)}, bf16[256,1024]{1,0:T(8,128)(2,1)S(1)}, u32[]{:S(2)}, u32[]{:S(2)}) %collective-permute-start.48) | collective-permute-done | bytes 524320 | tf_op jit(solution)/shard_map/ppermute | solution.py:40
  350.5 2.3 constant_dynamic-update-slice_fusion.19
  355.6 5.9 collective-permute-done.20
  361.5 9.4 %collective-permute-done.26 = f32[256,1024]{1,0:T(8,128)S(1)} collective-permute-done((f32[256,1024]{1,0:T(8,128)S(1)}, f32[256,1024]{1,0:T(8,128)S(1)}, u32[]{:S(2)}, u32[]{:S(2)}) %collective-permute-start.26) | collective-permute-done | bytes 1048608 | tf_op jit(solution)/shard_map/ppermute | solution.py:40
  372.9 10.6 %collective-permute-done.12 = f32[256,1024]{1,0:T(8,128)S(1)} collective-permute-done((f32[256,1024]{1,0:T(8,128)S(1)}, f32[256,1024]{1,0:T(8,128)S(1)}, u32[]{:S(2)}, u32[]{:S(2)}) %collective-permute-start.12) | collective-permute-done | bytes 1048608 | tf_op jit(solution)/shard_map/ppermute | solution.py:37
  383.5 9.3 %collective-permute-done.18 = f32[256,1024]{1,0:T(8,128)S(1)} collective-permute-done((f32[256,1024]{1,0:T(8,128)S(1)}, f32[256,1024]{1,0:T(8,128)S(1)}, u32[]{:S(2)}, u32[]{:S(2)}) %collective-permute-start.18) | collective-permute-done | bytes 1048608 | tf_op jit(solution)/shard_map/ppermute | solution.py:40
  395.3 9.0 %fusion.31 = f32[1024,2048]{1,0:T(8,128)} fusion(bf16[1024,1408]{1,0:T(8,128)(2,1)S(1)} %copy-done.113, bf16[1,2048,1408]{2,1,0:T(8,128)(2,1)S(1)} %bitcast.269), kind=kOutput, calls=%fused_computation.41 | convolution fusion | flops 5905580032 | bytes 17039360 | tf_op jit(solution)/shard_map/dot_general | solution.py:129
  404.3 10.8 %add_convert_fusion = bf16[1024,2048]{1,0:T(8,128)(2,1)S(1)} fusion(f32[1024,2048]{1,0:T(8,128)} %fusion.31, bf16[1024,1408]{1,0:T(8,128)(2,1)} %get-tuple-element.139, bf16[1,2048,1408]{2,1,0:T(8,128)(2,1)} %param.11), kind=kOutput, calls=%fused_computation.1 | convolution fusion | flops 5909774336 | bytes 21233664 | tf_op jit(solution)/shard_map/dot_general | solution.py:129
  415.8 8.0 %fusion.7 = f32[512,1408]{1,0:T(8,128)} fusion(bf16[1,1408,2048]{2,1,0:T(8,128)(2,1)} %param.13, bf16[256,2048]{1,0:T(8,128)(2,1)} %collective-permute-done.55, bf16[256,2048]{1,0:T(8,128)(2,1)S(1)} %constant_dynamic-update-slice_fusion.14, f32[512]{0:T(512)S(1)} %copy-done.101), kind=kOutput, calls=%fused_computation.17 | convolution fusion | flops 2959081472 | bytes 10749952 | tf_op jit(solution)/shard_map/dot_general | solution.py:126
  424.0 8.3 %fusion.78 = f32[512,1408]{1,0:T(8,128)} fusion(bf16[1,2048,1408]{2,1,0:T(8,128)(2,1)} %param.12, pred[512]{0:T(512)(128)(4,1)S(1)} %copy-done.111, bf16[256,2048]{1,0:T(8,128)(2,1)} %collective-permute-done.49, bf16[256,2048]{1,0:T(8,128)(2,1)} %get-tuple-element.240), kind=kOutput, calls=%fused_computation.94 | convolution fusion | flops 2957705216 | bytes 10748416 | tf_op jit(solution)/shard_map/dot_general | solution.py:121
  432.3 13.0 %constant_dynamic-update-slice_fusion.34 = (bf16[4096,1408]{1,0:T(8,128)(2,1)}, bf16[512,1408]{1,0:T(8,128)(2,1)}, bf16[4096,1408]{1,0:T(8,128)(2,1)}, bf16[512,...) fusion(bf16[4096,1408]{1,0:T(8,128)(2,1)} %get-tuple-element.138, ...), kind=kOutput, calls=%fused_computation.207 | convolution fusion | flops 2969239552 | bytes 22282752 | tf_op jit(solution)/shard_map/dot_general | solution.py:120
  449.6 6.5 fusion.94
  458.7 13.1 %collective-permute-done.37 = f32[256,1024]{1,0:T(8,128)S(1)} collective-permute-done((f32[256,1024]{1,0:T(8,128)}, f32[256,1024]{1,0:T(8,128)S(1)}, u32[]{:S(2)}, u32[]{:S(2)}) %collective-permute-start.37) | collective-permute-done | bytes 1048608 | tf_op jit(solution)/shard_map/ppermute | solution.py:37
  471.9 2.9 add_add_fusion.16
  474.7 18.8 %collective-permute-done.29 = f32[256,1024]{1,0:T(8,128)S(1)} collective-permute-done((f32[256,1024]{1,0:T(8,128)}, f32[256,1024]{1,0:T(8,128)S(1)}, u32[]{:S(2)}, u32[]{:S(2)}) %collective-permute-start.29) | collective-permute-done | bytes 1048608 | tf_op jit(solution)/shard_map/ppermute | solution.py:37
  496.6 6.5 fusion.27
  503.1 8.1 %add_convert_fusion.4 = bf16[512,2048]{1,0:T(8,128)(2,1)} fusion(f32[512,2048]{1,0:T(8,128)} %fusion.27, bf16[512,1408]{1,0:T(8,128)(2,1)S(1)} %copy-done.112, bf16[1,2048,1408]{2,1,0:T(8,128)(2,1)} %param.11), kind=kOutput, calls=%fused_computation.87 | convolution fusion | flops 2954887168 | bytes 13500416 | tf_op jit(solution)/shard_map/dot_general | solution.py:129
  512.8 3.2 constant_dynamic-update-slice_fusion.53
  521.3 3.8 constant_dynamic-update-slice_fusion.52
  527.2 16.1 %collective-permute-done.52 = f32[256,1024]{1,0:T(8,128)} collective-permute-done((f32[256,1024]{1,0:T(8,128)S(1)}, f32[256,1024]{1,0:T(8,128)}, u32[]{:S(2)}, u32[]{:S(2)}) %collective-permute-start.52) | collective-permute-done | bytes 1048608 | tf_op jit(solution)/shard_map/ppermute | solution.py:37
  545.0 2.3 add_add_fusion.12
  547.4 17.7 %collective-permute-done.46 = f32[256,1024]{1,0:T(8,128)} collective-permute-done((f32[256,1024]{1,0:T(8,128)S(1)}, f32[256,1024]{1,0:T(8,128)}, u32[]{:S(2)}, u32[]{:S(2)}) %collective-permute-start.46) | collective-permute-done | bytes 1048608 | tf_op jit(solution)/shard_map/ppermute | solution.py:37
  575.5 3.7 constant_dynamic-update-slice_fusion.51
  579.2 15.7 %collective-permute-done.63 = f32[4,256]{1,0:T(4,128)S(1)} collective-permute-done((f32[4,256]{1,0:T(4,128)S(1)}, f32[4,256]{1,0:T(4,128)S(1)}, u32[]{:S(2)}, u32[]{:S(2)}) %collective-permute-start.63) | collective-permute-done | bytes 4128 | tf_op jit(solution)/shard_map/ppermute | solution.py:37
  598.8 16.8 %collective-permute-done.59 = f32[256,1024]{1,0:T(8,128)S(1)} collective-permute-done((f32[256,1024]{1,0:T(8,128)S(1)}, f32[256,1024]{1,0:T(8,128)S(1)}, u32[]{:S(2)}, u32[]{:S(2)}) %collective-permute-start.59) | collective-permute-done | bytes 1048608 | tf_op jit(solution)/shard_map/ppermute | solution.py:37
  619.4 8.2 %constant_dynamic-update-slice_fusion.50 = bf16[4096,2048]{1,0:T(8,128)(2,1)} fusion(bf16[4096,2048]{1,0:T(8,128)(2,1)} %constant_dynamic-update-slice_fusion.51, bf16[256,2048]{1,0:T(8,128)(2,1)S(1)} %copy-done.63, bf16[256,2048]{1,0:T(8,128)(2,1)S(1)} %collective-permute-done.40, bf16[256,2048]{1,0:T(8,128)(2,1)S(1)} %copy-done.61, ...), kind=kLoop, calls=%fused_computation.223 | loop fusion | flops 20971520 | bytes 8392704
  629.7 3.0 constant_dynamic-update-slice_fusion.49
  634.0 2.5 constant_dynamic-update-slice_fusion.18
  636.5 26.5 %collective-permute-done.68 = f32[4,256]{1,0:T(4,128)S(1)} collective-permute-done((f32[4,256]{1,0:T(4,128)S(1)}, f32[4,256]{1,0:T(4,128)S(1)}, u32[]{:S(2)}, u32[]{:S(2)}) %collective-permute-start.68) | collective-permute-done | bytes 4128 | tf_op jit(solution)/shard_map/ppermute | solution.py:37
  670.3 33.8 %fusion.2 = bf16[1,2048,1408]{2,1,0:T(8,128)(2,1)} fusion(bf16[4096,2048]{1,0:T(8,128)(2,1)} %constant_dynamic-update-slice_fusion.18, bf16[4096,1408]{1,0:T(8,128)(2,1)} %get-tuple-element.161), kind=kOutput, calls=%fused_computation.12 | convolution fusion | flops 23625203712 | bytes 34078720 | tf_op jit(solution)/shard_map/dot_general | solution.py:148
  706.2 3.9 collective-permute-done.69
  713.5 33.6 %fusion.1 = bf16[1,2048,1408]{2,1,0:T(8,128)(2,1)} fusion(bf16[4096,2048]{1,0:T(8,128)(2,1)} %constant_dynamic-update-slice_fusion.18, bf16[4096,1408]{1,0:T(8,128)(2,1)} %get-tuple-element.136), kind=kOutput, calls=%fused_computation.11 | convolution fusion | flops 23625203712 | bytes 34078720 | tf_op jit(solution)/shard_map/dot_general | solution.py:147
  751.3 31.5 %fusion = bf16[1,1408,2048]{2,1,0:T(8,128)(2,1)} fusion(bf16[4096,1408]{1,0:T(8,128)(2,1)} %get-tuple-element.159, bf16[4096,2048]{1,0:T(8,128)(2,1)} %constant_dynamic-update-slice_fusion.49), kind=kOutput, calls=%fused_computation.10 | convolution fusion | flops 23625203712 | bytes 34078720 | tf_op jit(solution)/shard_map/dot_general | solution.py:149
  785.0 5.2 collective-permute-done.74
  (492 shorter events, 131.2 us)
Async XLA Ops:
  26.1 38.9 %collective-permute-start = (bf16[256,2048]{1,0:T(8,128)(2,1)}, bf16[256,2048]{1,0:T(8,128)(2,1)}, u32[]{:S(2)}, u32[]{:S(2)}) collective-permute-start(bf16[256,2048]{1,0:T(8,128)(2,1)} %param.8), channel_id=1, source_target_pairs={{0,4},{1,5},{4,8},{5,9},{8,12},{9,13},{12,14},{13,15},{14,10},{15,... | collective-permute-start | bytes 3145736 | tf_op jit(solution)/shard_map/ppermute | solution.py:37
  26.1 45.2 %collective-permute-start.2 = (bf16[256,2048]{1,0:T(8,128)(2,1)}, bf16[256,2048]{1,0:T(8,128)(2,1)S(1)}, u32[]{:S(2)}, u32[]{:S(2)}) collective-permute-start(bf16[256,2048]{1,0:T(8,128)(2,1)} %param.8), channel_id=1, source_target_pairs={{0,2},{1,3},{4,0},{5,1},{8,4},{9,5},{12,8},{13,9},{14,12},{15,13},... | collective-permute-start | bytes 3145736 | tf_op jit(solution)/shard_map/ppermute | solution.py:40
  28.1 52.7 %collective-permute-start.6 = (bf16[256,2048]{1,0:T(8,128)(2,1)}, bf16[256,2048]{1,0:T(8,128)(2,1)}, u32[]{:S(2)}, u32[]{:S(2)}) collective-permute-start(bf16[256,2048]{1,0:T(8,128)(2,1)} %param.14), channel_id=1, source_target_pairs={{0,4},{1,5},{4,8},{5,9},{8,12},{9,13},{12,14},{13,15},{14,10},{15,... | collective-permute-start | bytes 3145736 | tf_op jit(solution)/shard_map/ppermute | solution.py:37
  35.8 49.6 %collective-permute-start.8 = (bf16[256,2048]{1,0:T(8,128)(2,1)S(1)}, bf16[256,2048]{1,0:T(8,128)(2,1)S(1)}, u32[]{:S(2)}, u32[]{:S(2)}) collective-permute-start(bf16[256,2048]{1,0:T(8,128)(2,1)S(1)} %copy-done.5), channel_id=1, source_target_pairs={{0,2},{1,3},{4,0},{5,1},{8,4},{9,5},{12,8},{13,9},{14,12},{15,13},... | collective-permute-start | bytes 3145736 | tf_op jit(solution)/shard_map/ppermute | solution.py:40
  77.9 74.1 %collective-permute-start.13 = (bf16[256,2048]{1,0:T(8,128)(2,1)}, bf16[256,2048]{1,0:T(8,128)(2,1)S(1)}, u32[]{:S(2)}, u32[]{:S(2)}) collective-permute-start(bf16[256,2048]{1,0:T(8,128)(2,1)} %collective-permute-done), channel_id=1, source_target_pairs={{0,4},{1,5},{4,8},{5,9},{8,12},{9,13},{12,14},{13,15},{14,10},{15,... | collective-permute-start | bytes 3145736 | tf_op jit(solution)/shard_map/ppermute | solution.py:37
  80.8 81.4 %collective-permute-start.15 = (bf16[256,2048]{1,0:T(8,128)(2,1)S(1)}, bf16[256,2048]{1,0:T(8,128)(2,1)}, u32[]{:S(2)}, u32[]{:S(2)}) collective-permute-start(bf16[256,2048]{1,0:T(8,128)(2,1)S(1)} %collective-permute-done.2), channel_id=1, source_target_pairs={{0,2},{1,3},{4,0},{5,1},{8,4},{9,5},{12,8},{13,9},{14,12},{15,13},... | collective-permute-start | bytes 3145736 | tf_op jit(solution)/shard_map/ppermute | solution.py:40
  85.3 84.0 %collective-permute-start.21 = (bf16[256,2048]{1,0:T(8,128)(2,1)}, bf16[256,2048]{1,0:T(8,128)(2,1)S(1)}, u32[]{:S(2)}, u32[]{:S(2)}) collective-permute-start(bf16[256,2048]{1,0:T(8,128)(2,1)} %collective-permute-done.6), channel_id=1, source_target_pairs={{0,4},{1,5},{4,8},{5,9},{8,12},{9,13},{12,14},{13,15},{14,10},{15,... | collective-permute-start | bytes 3145736 | tf_op jit(solution)/shard_map/ppermute | solution.py:37
  95.7 74.0 %collective-permute-start.23 = (bf16[256,2048]{1,0:T(8,128)(2,1)S(1)}, bf16[256,2048]{1,0:T(8,128)(2,1)S(1)}, u32[]{:S(2)}, u32[]{:S(2)}) collective-permute-start(bf16[256,2048]{1,0:T(8,128)(2,1)S(1)} %collective-permute-done.8), channel_id=1, source_target_pairs={{0,2},{1,3},{4,0},{5,1},{8,4},{9,5},{12,8},{13,9},{14,12},{15,13},... | collective-permute-start | bytes 3145736 | tf_op jit(solution)/shard_map/ppermute | solution.py:40
  138.7 113.0 %collective-permute-start.4 = (bf16[256,2048]{1,0:T(8,128)(2,1)}, bf16[256,2048]{1,0:T(8,128)(2,1)S(1)}, u32[]{:S(2)}, u32[]{:S(2)}) collective-permute-start(bf16[256,2048]{1,0:T(8,128)(2,1)} %get-tuple-element.202), channel_id=1, source_target_pairs={{0,1},{1,0},{4,5},{5,4},{8,9},{9,8},{12,13},{13,12},{14,15},{15,14... | collective-permute-start | bytes 3145736 | tf_op jit(solution)/shard_map/ppermute | solution.py:43
  165.6 86.5 %collective-permute-start.5 = (bf16[256,2048]{1,0:T(8,128)(2,1)}, bf16[256,2048]{1,0:T(8,128)(2,1)S(1)}, u32[]{:S(2)}, u32[]{:S(2)}) collective-permute-start(bf16[256,2048]{1,0:T(8,128)(2,1)} %get-tuple-element.201), channel_id=1, source_target_pairs={{0,1},{1,0},{4,5},{5,4},{8,9},{9,8},{12,13},{13,12},{14,15},{15,14... | collective-permute-start | bytes 3145736 | tf_op jit(solution)/shard_map/ppermute | solution.py:43
  169.3 68.4 %collective-permute-start.30 = (bf16[256,2048]{1,0:T(8,128)(2,1)S(1)}, bf16[256,2048]{1,0:T(8,128)(2,1)S(1)}, u32[]{:S(2)}, u32[]{:S(2)}) collective-permute-start(bf16[256,2048]{1,0:T(8,128)(2,1)S(1)} %collective-permute-done.13), channel_id=1, source_target_pairs={{0,4},{1,5},{4,8},{5,9},{8,12},{9,13},{12,14},{13,15},{14,10},{15,... | collective-permute-start | bytes 3145736 | tf_op jit(solution)/shard_map/ppermute | solution.py:37
  180.0 59.0 %collective-permute-start.38 = (bf16[256,2048]{1,0:T(8,128)(2,1)S(1)}, bf16[256,2048]{1,0:T(8,128)(2,1)S(1)}, u32[]{:S(2)}, u32[]{:S(2)}) collective-permute-start(bf16[256,2048]{1,0:T(8,128)(2,1)S(1)} %collective-permute-done.21), channel_id=1, source_target_pairs={{0,4},{1,5},{4,8},{5,9},{8,12},{9,13},{12,14},{13,15},{14,10},{15,... | collective-permute-start | bytes 3145736 | tf_op jit(solution)/shard_map/ppermute | solution.py:37
  180.1 59.7 %collective-permute-start.40 = (bf16[256,2048]{1,0:T(8,128)(2,1)S(1)}, bf16[256,2048]{1,0:T(8,128)(2,1)S(1)}, u32[]{:S(2)}, u32[]{:S(2)}) collective-permute-start(bf16[256,2048]{1,0:T(8,128)(2,1)S(1)} %collective-permute-done.23), channel_id=1, source_target_pairs={{0,2},{1,3},{4,0},{5,1},{8,4},{9,5},{12,8},{13,9},{14,12},{15,13},... | collective-permute-start | bytes 3145736 | tf_op jit(solution)/shard_map/ppermute | solution.py:40
  239.0 22.9 %collective-permute-start.11 = (bf16[256,2048]{1,0:T(8,128)(2,1)S(1)}, bf16[256,2048]{1,0:T(8,128)(2,1)S(1)}, u32[]{:S(2)}, u32[]{:S(2)}) collective-permute-start(bf16[256,2048]{1,0:T(8,128)(2,1)S(1)} %copy-done.50), channel_id=1, source_target_pairs={{0,1},{1,0},{4,5},{5,4},{8,9},{9,8},{12,13},{13,12},{14,15},{15,14... | collective-permute-start | bytes 3145736 | tf_op jit(solution)/shard_map/ppermute | solution.py:43
  239.9 26.3 %collective-permute-start.32 = (bf16[256,2048]{1,0:T(8,128)(2,1)}, bf16[256,2048]{1,0:T(8,128)(2,1)S(1)}, u32[]{:S(2)}, u32[]{:S(2)}) collective-permute-start(bf16[256,2048]{1,0:T(8,128)(2,1)} %collective-permute-done.15), channel_id=1, source_target_pairs={{0,2},{1,3},{4,0},{5,1},{8,4},{9,5},{12,8},{13,9},{14,12},{15,13},... | collective-permute-start | bytes 3145736 | tf_op jit(solution)/shard_map/ppermute | solution.py:40
  251.7 83.6 %collective-permute-start.47 = (bf16[256,1024]{1,0:T(8,128)(2,1)}, bf16[256,1024]{1,0:T(8,128)(2,1)}, u32[]{:S(2)}, u32[]{:S(2)}) collective-permute-start(bf16[256,1024]{1,0:T(8,128)(2,1)} %slice.719), channel_id=1, source_target_pairs={{0,4},{1,5},{4,8},{5,9},{8,12},{9,13},{12,14},{13,15},{14,10},{15,... | collective-permute-start | bytes 1572872 | tf_op jit(solution)/shard_map/ppermute | solution.py:37
  252.1 24.7 %collective-permute-start.53 = (bf16[256,1024]{1,0:T(8,128)(2,1)S(1)}, bf16[256,1024]{1,0:T(8,128)(2,1)S(1)}, u32[]{:S(2)}, u32[]{:S(2)}) collective-permute-start(bf16[256,1024]{1,0:T(8,128)(2,1)S(1)} %slice.728), channel_id=1, source_target_pairs={{0,4},{1,5},{4,8},{5,9},{8,12},{9,13},{12,14},{13,15},{14,10},{15,... | collective-permute-start | bytes 1572872 | tf_op jit(solution)/shard_map/ppermute | solution.py:37
  276.8 58.6 %collective-permute-start.17 = (bf16[256,2048]{1,0:T(8,128)(2,1)}, bf16[256,2048]{1,0:T(8,128)(2,1)S(1)}, u32[]{:S(2)}, u32[]{:S(2)}) collective-permute-start(bf16[256,2048]{1,0:T(8,128)(2,1)} %get-tuple-element.194), channel_id=1, source_target_pairs={{0,1},{1,0},{4,5},{5,4},{8,9},{9,8},{12,13},{13,12},{14,15},{15,14... | collective-permute-start | bytes 3145736 | tf_op jit(solution)/shard_map/ppermute | solution.py:43
  276.8 59.0 %collective-permute-start.19 = (bf16[256,2048]{1,0:T(8,128)(2,1)}, bf16[256,2048]{1,0:T(8,128)(2,1)S(1)}, u32[]{:S(2)}, u32[]{:S(2)}) collective-permute-start(bf16[256,2048]{1,0:T(8,128)(2,1)} %get-tuple-element.193), channel_id=1, source_target_pairs={{0,1},{1,0},{4,5},{5,4},{8,9},{9,8},{12,13},{13,12},{14,15},{15,14... | collective-permute-start | bytes 3145736 | tf_op jit(solution)/shard_map/ppermute | solution.py:43
  290.2 43.3 %collective-permute-start.28 = (f32[4,256]{1,0:T(4,128)S(1)}, f32[4,256]{1,0:T(4,128)S(1)}, u32[]{:S(2)}, u32[]{:S(2)}) collective-permute-start(f32[4,256]{1,0:T(4,128)S(1)} %add_bitcast_fusion), channel_id=1, source_target_pairs={{0,4},{1,5},{4,8},{5,9},{8,12},{9,13},{12,14},{13,15},{14,10},{15,... | collective-permute-start | bytes 12296 | tf_op jit(solution)/shard_map/ppermute | solution.py:37
  290.6 58.2 %collective-permute-start.25 = (bf16[256,2048]{1,0:T(8,128)(2,1)}, bf16[256,2048]{1,0:T(8,128)(2,1)S(1)}, u32[]{:S(2)}, u32[]{:S(2)}) collective-permute-start(bf16[256,2048]{1,0:T(8,128)(2,1)} %get-tuple-element.190), channel_id=1, source_target_pairs={{0,1},{1,0},{4,5},{5,4},{8,9},{9,8},{12,13},{13,12},{14,15},{15,14... | collective-permute-start | bytes 3145736 | tf_op jit(solution)/shard_map/ppermute | solution.py:43
  335.4 26.1 %collective-permute-start.20 = (f32[256,1024]{1,0:T(8,128)S(1)}, f32[256,1024]{1,0:T(8,128)S(1)}, u32[]{:S(2)}, u32[]{:S(2)}) collective-permute-start(f32[256,1024]{1,0:T(8,128)S(1)} %copy-done.49), channel_id=1, source_target_pairs={{0,4},{1,5},{4,8},{5,9},{8,12},{9,13},{12,14},{13,15},{14,10},{15,... | collective-permute-start | bytes 3145736 | tf_op jit(solution)/shard_map/ppermute | solution.py:37
  335.8 35.1 %collective-permute-start.26 = (f32[256,1024]{1,0:T(8,128)S(1)}, f32[256,1024]{1,0:T(8,128)S(1)}, u32[]{:S(2)}, u32[]{:S(2)}) collective-permute-start(f32[256,1024]{1,0:T(8,128)S(1)} %get-tuple-element.50), channel_id=1, source_target_pairs={{0,2},{1,3},{4,0},{5,1},{8,4},{9,5},{12,8},{13,9},{14,12},{15,13},... | collective-permute-start | bytes 3145736 | tf_op jit(solution)/shard_map/ppermute | solution.py:40
  348.5 35.0 %collective-permute-start.12 = (f32[256,1024]{1,0:T(8,128)S(1)}, f32[256,1024]{1,0:T(8,128)S(1)}, u32[]{:S(2)}, u32[]{:S(2)}) collective-permute-start(f32[256,1024]{1,0:T(8,128)S(1)} %copy-done.43), channel_id=1, source_target_pairs={{0,4},{1,5},{4,8},{5,9},{8,12},{9,13},{12,14},{13,15},{14,10},{15,... | collective-permute-start | bytes 3145736 | tf_op jit(solution)/shard_map/ppermute | solution.py:37
  348.8 44.0 %collective-permute-start.18 = (f32[256,1024]{1,0:T(8,128)S(1)}, f32[256,1024]{1,0:T(8,128)S(1)}, u32[]{:S(2)}, u32[]{:S(2)}) collective-permute-start(f32[256,1024]{1,0:T(8,128)S(1)} %copy-done.42), channel_id=1, source_target_pairs={{0,2},{1,3},{4,0},{5,1},{8,4},{9,5},{12,8},{13,9},{14,12},{15,13},... | collective-permute-start | bytes 3145736 | tf_op jit(solution)/shard_map/ppermute | solution.py:40
  355.6 59.8 %collective-permute-start.55 = (bf16[256,2048]{1,0:T(8,128)(2,1)S(1)}, bf16[256,2048]{1,0:T(8,128)(2,1)}, u32[]{:S(2)}, u32[]{:S(2)}) collective-permute-start(bf16[256,2048]{1,0:T(8,128)(2,1)S(1)} %constant_dynamic-update-slice_fusion.14), channel_id=1, source_target_pairs={{0,1},{1,0},{4,5},{5,4},{8,9},{9,8},{12,13},{13,12},{14,15},{15,14... | collective-permute-start | bytes 3145736 | tf_op jit(solution)/shard_map/ppermute | solution.py:43
  361.5 62.3 %collective-permute-start.49 = (bf16[256,2048]{1,0:T(8,128)(2,1)}, bf16[256,2048]{1,0:T(8,128)(2,1)}, u32[]{:S(2)}, u32[]{:S(2)}) collective-permute-start(bf16[256,2048]{1,0:T(8,128)(2,1)} %get-tuple-element.240), channel_id=1, source_target_pairs={{0,1},{1,0},{4,5},{5,4},{8,9},{9,8},{12,13},{13,12},{14,15},{15,14... | collective-permute-start | bytes 3145736 | tf_op jit(solution)/shard_map/ppermute | solution.py:43
  370.9 74.7 %collective-permute-start.34 = (bf16[256,2048]{1,0:T(8,128)(2,1)}, bf16[256,2048]{1,0:T(8,128)(2,1)S(1)}, u32[]{:S(2)}, u32[]{:S(2)}) collective-permute-start(bf16[256,2048]{1,0:T(8,128)(2,1)} %get-tuple-element.186), channel_id=1, source_target_pairs={{0,1},{1,0},{4,5},{5,4},{8,9},{9,8},{12,13},{13,12},{14,15},{15,14... | collective-permute-start | bytes 3145736 | tf_op jit(solution)/shard_map/ppermute | solution.py:43
  383.5 64.0 %collective-permute-start.36 = (bf16[256,2048]{1,0:T(8,128)(2,1)}, bf16[256,2048]{1,0:T(8,128)(2,1)S(1)}, u32[]{:S(2)}, u32[]{:S(2)}) collective-permute-start(bf16[256,2048]{1,0:T(8,128)(2,1)} %get-tuple-element.185), channel_id=1, source_target_pairs={{0,1},{1,0},{4,5},{5,4},{8,9},{9,8},{12,13},{13,12},{14,15},{15,14... | collective-permute-start | bytes 3145736 | tf_op jit(solution)/shard_map/ppermute | solution.py:43
  394.6 50.7 %collective-permute-start.45 = (f32[4,256]{1,0:T(4,128)S(1)}, f32[4,256]{1,0:T(4,128)S(1)}, u32[]{:S(2)}, u32[]{:S(2)}) collective-permute-start(f32[4,256]{1,0:T(4,128)S(1)} %bitcast_add_fusion.6), channel_id=1, source_target_pairs={{0,4},{1,5},{4,8},{5,9},{8,12},{9,13},{12,14},{13,15},{14,10},{15,... | collective-permute-start | bytes 12296 | tf_op jit(solution)/shard_map/ppermute | solution.py:37
  415.4 32.2 %collective-permute-start.42 = (bf16[256,2048]{1,0:T(8,128)(2,1)S(1)}, bf16[256,2048]{1,0:T(8,128)(2,1)S(1)}, u32[]{:S(2)}, u32[]{:S(2)}) collective-permute-start(bf16[256,2048]{1,0:T(8,128)(2,1)S(1)} %get-tuple-element.182), channel_id=1, source_target_pairs={{0,1},{1,0},{4,5},{5,4},{8,9},{9,8},{12,13},{13,12},{14,15},{15,14... | collective-permute-start | bytes 3145736 | tf_op jit(solution)/shard_map/ppermute | solution.py:43
  423.8 34.8 %collective-permute-start.44 = (bf16[256,2048]{1,0:T(8,128)(2,1)S(1)}, bf16[256,2048]{1,0:T(8,128)(2,1)}, u32[]{:S(2)}, u32[]{:S(2)}) collective-permute-start(bf16[256,2048]{1,0:T(8,128)(2,1)S(1)} %get-tuple-element.181), channel_id=1, source_target_pairs={{0,1},{1,0},{4,5},{5,4},{8,9},{9,8},{12,13},{13,12},{14,15},{15,14... | collective-permute-start | bytes 3145736 | tf_op jit(solution)/shard_map/ppermute | solution.py:43
  445.3 26.5 %collective-permute-start.37 = (f32[256,1024]{1,0:T(8,128)}, f32[256,1024]{1,0:T(8,128)S(1)}, u32[]{:S(2)}, u32[]{:S(2)}) collective-permute-start(f32[256,1024]{1,0:T(8,128)} %get-tuple-element.54), channel_id=1, source_target_pairs={{0,4},{1,5},{4,8},{5,9},{8,12},{9,13},{12,14},{13,15},{14,10},{15,... | collective-permute-start | bytes 3145736 | tf_op jit(solution)/shard_map/ppermute | solution.py:37
  445.6 26.2 %collective-permute-start.43 = (f32[256,1024]{1,0:T(8,128)}, f32[256,1024]{1,0:T(8,128)S(1)}, u32[]{:S(2)}, u32[]{:S(2)}) collective-permute-start(f32[256,1024]{1,0:T(8,128)} %get-tuple-element.55), channel_id=1, source_target_pairs={{0,2},{1,3},{4,0},{5,1},{8,4},{9,5},{12,8},{13,9},{14,12},{15,13},... | collective-permute-start | bytes 3145736 | tf_op jit(solution)/shard_map/ppermute | solution.py:40
  447.5 46.0 %collective-permute-start.29 = (f32[256,1024]{1,0:T(8,128)}, f32[256,1024]{1,0:T(8,128)S(1)}, u32[]{:S(2)}, u32[]{:S(2)}) collective-permute-start(f32[256,1024]{1,0:T(8,128)} %get-tuple-element.52), channel_id=1, source_target_pairs={{0,4},{1,5},{4,8},{5,9},{8,12},{9,13},{12,14},{13,15},{14,10},{15,... | collective-permute-start | bytes 3145736 | tf_op jit(solution)/shard_map/ppermute | solution.py:37
  447.7 46.0 %collective-permute-start.35 = (f32[256,1024]{1,0:T(8,128)}, f32[256,1024]{1,0:T(8,128)S(1)}, u32[]{:S(2)}, u32[]{:S(2)}) collective-permute-start(f32[256,1024]{1,0:T(8,128)} %get-tuple-element.53), channel_id=1, source_target_pairs={{0,2},{1,3},{4,0},{5,1},{8,4},{9,5},{12,8},{13,9},{14,12},{15,13},... | collective-permute-start | bytes 3145736 | tf_op jit(solution)/shard_map/ppermute | solution.py:40
  458.6 62.3 %collective-permute-start.50 = (bf16[256,2048]{1,0:T(8,128)(2,1)}, bf16[256,2048]{1,0:T(8,128)(2,1)S(1)}, u32[]{:S(2)}, u32[]{:S(2)}) collective-permute-start(bf16[256,2048]{1,0:T(8,128)(2,1)} %slice.723), channel_id=1, source_target_pairs={{0,1},{1,0},{4,5},{5,4},{8,9},{9,8},{12,13},{13,12},{14,15},{15,14... | collective-permute-start | bytes 3145736 | tf_op jit(solution)/shard_map/ppermute | solution.py:43
  495.5 23.7 %collective-permute-start.58 = (f32[4,256]{1,0:T(4,128)S(1)}, f32[4,256]{1,0:T(4,128)S(1)}, u32[]{:S(2)}, u32[]{:S(2)}) collective-permute-start(f32[4,256]{1,0:T(4,128)S(1)} %bitcast_add_fusion.5), channel_id=1, source_target_pairs={{0,4},{1,5},{4,8},{5,9},{8,12},{9,13},{12,14},{13,15},{14,10},{15,... | collective-permute-start | bytes 12296 | tf_op jit(solution)/shard_map/ppermute | solution.py:37
  517.2 26.1 %collective-permute-start.52 = (f32[256,1024]{1,0:T(8,128)S(1)}, f32[256,1024]{1,0:T(8,128)}, u32[]{:S(2)}, u32[]{:S(2)}) collective-permute-start(f32[256,1024]{1,0:T(8,128)S(1)} %copy-done.55), channel_id=1, source_target_pairs={{0,4},{1,5},{4,8},{5,9},{8,12},{9,13},{12,14},{13,15},{14,10},{15,... | collective-permute-start | bytes 3145736 | tf_op jit(solution)/shard_map/ppermute | solution.py:37
  518.9 26.1 %collective-permute-start.57 = (f32[256,1024]{1,0:T(8,128)S(1)}, f32[256,1024]{1,0:T(8,128)}, u32[]{:S(2)}, u32[]{:S(2)}) collective-permute-start(f32[256,1024]{1,0:T(8,128)S(1)} %copy-done.53), channel_id=1, source_target_pairs={{0,2},{1,3},{4,0},{5,1},{8,4},{9,5},{12,8},{13,9},{14,12},{15,13},... | collective-permute-start | bytes 3145736 | tf_op jit(solution)/shard_map/ppermute | solution.py:40
  519.2 45.9 %collective-permute-start.46 = (f32[256,1024]{1,0:T(8,128)S(1)}, f32[256,1024]{1,0:T(8,128)}, u32[]{:S(2)}, u32[]{:S(2)}) collective-permute-start(f32[256,1024]{1,0:T(8,128)S(1)} %copy-done.54), channel_id=1, source_target_pairs={{0,4},{1,5},{4,8},{5,9},{8,12},{9,13},{12,14},{13,15},{14,10},{15,... | collective-permute-start | bytes 3145736 | tf_op jit(solution)/shard_map/ppermute | solution.py:37
  520.9 45.6 %collective-permute-start.51 = (f32[256,1024]{1,0:T(8,128)S(1)}, f32[256,1024]{1,0:T(8,128)}, u32[]{:S(2)}, u32[]{:S(2)}) collective-permute-start(f32[256,1024]{1,0:T(8,128)S(1)} %copy-done.52), channel_id=1, source_target_pairs={{0,2},{1,3},{4,0},{5,1},{8,4},{9,5},{12,8},{13,9},{14,12},{15,13},... | collective-permute-start | bytes 3145736 | tf_op jit(solution)/shard_map/ppermute | solution.py:40
  525.1 45.7 %collective-permute-start.76 = (bf16[256,2048]{1,0:T(8,128)(2,1)S(1)}, bf16[256,2048]{1,0:T(8,128)(2,1)S(1)}, u32[]{:S(2)}, u32[]{:S(2)}) collective-permute-start(bf16[256,2048]{1,0:T(8,128)(2,1)S(1)} %slice.772), channel_id=1, source_target_pairs={{0,1},{1,0},{4,5},{5,4},{8,9},{9,8},{12,13},{13,12},{14,15},{15,14... | collective-permute-start | bytes 3145736 | tf_op jit(solution)/shard_map/ppermute | solution.py:43
  568.7 26.2 %collective-permute-start.61 = (f32[256,1024]{1,0:T(8,128)S(1)}, f32[256,1024]{1,0:T(8,128)}, u32[]{:S(2)}, u32[]{:S(2)}) collective-permute-start(f32[256,1024]{1,0:T(8,128)S(1)} %get-tuple-element.64), channel_id=1, source_target_pairs={{0,4},{1,5},{4,8},{5,9},{8,12},{9,13},{12,14},{13,15},{14,10},{15,... | collective-permute-start | bytes 3145736 | tf_op jit(solution)/shard_map/ppermute | solution.py:37
  570.5 26.1 %collective-permute-start.62 = (f32[256,1024]{1,0:T(8,128)S(1)}, f32[256,1024]{1,0:T(8,128)}, u32[]{:S(2)}, u32[]{:S(2)}) collective-permute-start(f32[256,1024]{1,0:T(8,128)S(1)} %get-tuple-element.65), channel_id=1, source_target_pairs={{0,2},{1,3},{4,0},{5,1},{8,4},{9,5},{12,8},{13,9},{14,12},{15,13},... | collective-permute-start | bytes 3145736 | tf_op jit(solution)/shard_map/ppermute | solution.py:40
  571.5 23.4 %collective-permute-start.63 = (f32[4,256]{1,0:T(4,128)S(1)}, f32[4,256]{1,0:T(4,128)S(1)}, u32[]{:S(2)}, u32[]{:S(2)}) collective-permute-start(f32[4,256]{1,0:T(4,128)S(1)} %bitcast_add_fusion.4), channel_id=1, source_target_pairs={{0,4},{1,5},{4,8},{5,9},{8,12},{9,13},{12,14},{13,15},{14,10},{15,... | collective-permute-start | bytes 12296 | tf_op jit(solution)/shard_map/ppermute | solution.py:37
  573.4 42.1 %collective-permute-start.59 = (f32[256,1024]{1,0:T(8,128)S(1)}, f32[256,1024]{1,0:T(8,128)S(1)}, u32[]{:S(2)}, u32[]{:S(2)}) collective-permute-start(f32[256,1024]{1,0:T(8,128)S(1)} %get-tuple-element.62), channel_id=1, source_target_pairs={{0,4},{1,5},{4,8},{5,9},{8,12},{9,13},{12,14},{13,15},{14,10},{15,... | collective-permute-start | bytes 3145736 | tf_op jit(solution)/shard_map/ppermute | solution.py:37
  574.8 42.0 %collective-permute-start.60 = (f32[256,1024]{1,0:T(8,128)S(1)}, f32[256,1024]{1,0:T(8,128)S(1)}, u32[]{:S(2)}, u32[]{:S(2)}) collective-permute-start(f32[256,1024]{1,0:T(8,128)S(1)} %get-tuple-element.63), channel_id=1, source_target_pairs={{0,2},{1,3},{4,0},{5,1},{8,4},{9,5},{12,8},{13,9},{14,12},{15,13},... | collective-permute-start | bytes 3145736 | tf_op jit(solution)/shard_map/ppermute | solution.py:40
  617.4 45.7 %collective-permute-start.66 = (f32[256,1024]{1,0:T(8,128)S(1)}, f32[256,1024]{1,0:T(8,128)S(1)}, u32[]{:S(2)}, u32[]{:S(2)}) collective-permute-start(f32[256,1024]{1,0:T(8,128)S(1)} %get-tuple-element.69), channel_id=1, source_target_pairs={{0,4},{1,5},{4,8},{5,9},{8,12},{9,13},{12,14},{13,15},{14,10},{15,... | collective-permute-start | bytes 3145736 | tf_op jit(solution)/shard_map/ppermute | solution.py:37
  618.8 44.3 %collective-permute-start.67 = (f32[256,1024]{1,0:T(8,128)S(1)}, f32[256,1024]{1,0:T(8,128)S(1)}, u32[]{:S(2)}, u32[]{:S(2)}) collective-permute-start(f32[256,1024]{1,0:T(8,128)S(1)} %get-tuple-element.70), channel_id=1, source_target_pairs={{0,2},{1,3},{4,0},{5,1},{8,4},{9,5},{12,8},{13,9},{14,12},{15,13},... | collective-permute-start | bytes 3145736 | tf_op jit(solution)/shard_map/ppermute | solution.py:40
  627.7 35.9 %collective-permute-start.64 = (f32[256,1024]{1,0:T(8,128)S(1)}, f32[256,1024]{1,0:T(8,128)S(1)}, u32[]{:S(2)}, u32[]{:S(2)}) collective-permute-start(f32[256,1024]{1,0:T(8,128)S(1)} %get-tuple-element.67), channel_id=1, source_target_pairs={{0,4},{1,5},{4,8},{5,9},{8,12},{9,13},{12,14},{13,15},{14,10},{15,... | collective-permute-start | bytes 3145736 | tf_op jit(solution)/shard_map/ppermute | solution.py:37
  629.0 35.0 %collective-permute-start.65 = (f32[256,1024]{1,0:T(8,128)S(1)}, f32[256,1024]{1,0:T(8,128)S(1)}, u32[]{:S(2)}, u32[]{:S(2)}) collective-permute-start(f32[256,1024]{1,0:T(8,128)S(1)} %get-tuple-element.68), channel_id=1, source_target_pairs={{0,2},{1,3},{4,0},{5,1},{8,4},{9,5},{12,8},{13,9},{14,12},{15,13},... | collective-permute-start | bytes 3145736 | tf_op jit(solution)/shard_map/ppermute | solution.py:40
  632.6 30.4 %collective-permute-start.68 = (f32[4,256]{1,0:T(4,128)S(1)}, f32[4,256]{1,0:T(4,128)S(1)}, u32[]{:S(2)}, u32[]{:S(2)}) collective-permute-start(f32[4,256]{1,0:T(4,128)S(1)} %bitcast_add_fusion.3), channel_id=1, source_target_pairs={{0,4},{1,5},{4,8},{5,9},{8,12},{9,13},{12,14},{13,15},{14,10},{15,... | collective-permute-start | bytes 12296 | tf_op jit(solution)/shard_map/ppermute | solution.py:37
  664.6 39.6 %collective-permute-start.73 = (f32[4,256]{1,0:T(4,128)S(1)}, f32[4,256]{1,0:T(4,128)S(1)}, u32[]{:S(2)}, u32[]{:S(2)}) collective-permute-start(f32[4,256]{1,0:T(4,128)S(1)} %bitcast_add_fusion.2), channel_id=1, source_target_pairs={{0,4},{1,5},{4,8},{5,9},{8,12},{9,13},{12,14},{13,15},{14,10},{15,... | collective-permute-start | bytes 12296 | tf_op jit(solution)/shard_map/ppermute | solution.py:37
  665.9 38.4 %collective-permute-start.71 = (f32[256,1024]{1,0:T(8,128)S(1)}, f32[256,1024]{1,0:T(8,128)S(1)}, u32[]{:S(2)}, u32[]{:S(2)}) collective-permute-start(f32[256,1024]{1,0:T(8,128)S(1)} %get-tuple-element.74), channel_id=1, source_target_pairs={{0,4},{1,5},{4,8},{5,9},{8,12},{9,13},{12,14},{13,15},{14,10},{15,... | collective-permute-start | bytes 3145736 | tf_op jit(solution)/shard_map/ppermute | solution.py:37
  666.8 37.5 %collective-permute-start.72 = (f32[256,1024]{1,0:T(8,128)S(1)}, f32[256,1024]{1,0:T(8,128)S(1)}, u32[]{:S(2)}, u32[]{:S(2)}) collective-permute-start(f32[256,1024]{1,0:T(8,128)S(1)} %get-tuple-element.75), channel_id=1, source_target_pairs={{0,2},{1,3},{4,0},{5,1},{8,4},{9,5},{12,8},{13,9},{14,12},{15,13},... | collective-permute-start | bytes 3145736 | tf_op jit(solution)/shard_map/ppermute | solution.py:40
  667.9 42.1 %collective-permute-start.69 = (f32[256,1024]{1,0:T(8,128)S(1)}, f32[256,1024]{1,0:T(8,128)S(1)}, u32[]{:S(2)}, u32[]{:S(2)}) collective-permute-start(f32[256,1024]{1,0:T(8,128)S(1)} %get-tuple-element.72), channel_id=1, source_target_pairs={{0,4},{1,5},{4,8},{5,9},{8,12},{9,13},{12,14},{13,15},{14,10},{15,... | collective-permute-start | bytes 3145736 | tf_op jit(solution)/shard_map/ppermute | solution.py:37
  668.8 42.1 %collective-permute-start.70 = (f32[256,1024]{1,0:T(8,128)S(1)}, f32[256,1024]{1,0:T(8,128)S(1)}, u32[]{:S(2)}, u32[]{:S(2)}) collective-permute-start(f32[256,1024]{1,0:T(8,128)S(1)} %get-tuple-element.73), channel_id=1, source_target_pairs={{0,2},{1,3},{4,0},{5,1},{8,4},{9,5},{12,8},{13,9},{14,12},{15,13},... | collective-permute-start | bytes 3145736 | tf_op jit(solution)/shard_map/ppermute | solution.py:40
  704.2 79.3 %collective-permute-start.80 = (bf16[256,2048]{1,0:T(8,128)(2,1)S(1)}, bf16[256,2048]{1,0:T(8,128)(2,1)S(1)}, u32[]{:S(2)}, u32[]{:S(2)}) collective-permute-start(bf16[256,2048]{1,0:T(8,128)(2,1)S(1)} %copy-done.44), channel_id=1, source_target_pairs={{0,1},{1,0},{4,5},{5,4},{8,9},{9,8},{12,13},{13,12},{14,15},{15,14... | collective-permute-start | bytes 3145736 | tf_op jit(solution)/shard_map/ppermute | solution.py:43
  712.6 37.6 %collective-permute-start.82 = (f32[4,256]{1,0:T(4,128)S(1)}, f32[4,256]{1,0:T(4,128)S(1)}, u32[]{:S(2)}, u32[]{:S(2)}) collective-permute-start(f32[4,256]{1,0:T(4,128)S(1)} %bitcast_add_fusion.1), channel_id=1, source_target_pairs={{0,4},{1,5},{4,8},{5,9},{8,12},{9,13},{12,14},{13,15},{14,10},{15,... | collective-permute-start | bytes 12296 | tf_op jit(solution)/shard_map/ppermute | solution.py:37
  747.1 36.3 %collective-permute-start.78 = (f32[256,1024]{1,0:T(8,128)S(1)}, f32[256,1024]{1,0:T(8,128)S(1)}, u32[]{:S(2)}, u32[]{:S(2)}) collective-permute-start(f32[256,1024]{1,0:T(8,128)S(1)} %get-tuple-element.79), channel_id=1, source_target_pairs={{0,4},{1,5},{4,8},{5,9},{8,12},{9,13},{12,14},{13,15},{14,10},{15,... | collective-permute-start | bytes 3145736 | tf_op jit(solution)/shard_map/ppermute | solution.py:37
  748.1 35.3 %collective-permute-start.81 = (f32[256,1024]{1,0:T(8,128)S(1)}, f32[256,1024]{1,0:T(8,128)S(1)}, u32[]{:S(2)}, u32[]{:S(2)}) collective-permute-start(f32[256,1024]{1,0:T(8,128)S(1)} %get-tuple-element.80), channel_id=1, source_target_pairs={{0,2},{1,3},{4,0},{5,1},{8,4},{9,5},{12,8},{13,9},{14,12},{15,13},... | collective-permute-start | bytes 3145736 | tf_op jit(solution)/shard_map/ppermute | solution.py:40
  749.1 41.1 %collective-permute-start.74 = (f32[256,1024]{1,0:T(8,128)S(1)}, f32[256,1024]{1,0:T(8,128)S(1)}, u32[]{:S(2)}, u32[]{:S(2)}) collective-permute-start(f32[256,1024]{1,0:T(8,128)S(1)} %get-tuple-element.77), channel_id=1, source_target_pairs={{0,4},{1,5},{4,8},{5,9},{8,12},{9,13},{12,14},{13,15},{14,10},{15,... | collective-permute-start | bytes 3145736 | tf_op jit(solution)/shard_map/ppermute | solution.py:37
  750.3 40.8 %collective-permute-start.77 = (f32[256,1024]{1,0:T(8,128)S(1)}, f32[256,1024]{1,0:T(8,128)S(1)}, u32[]{:S(2)}, u32[]{:S(2)}) collective-permute-start(f32[256,1024]{1,0:T(8,128)S(1)} %get-tuple-element.78), channel_id=1, source_target_pairs={{0,2},{1,3},{4,0},{5,1},{8,4},{9,5},{12,8},{13,9},{14,12},{15,13},... | collective-permute-start | bytes 3145736 | tf_op jit(solution)/shard_map/ppermute | solution.py:40
  (149 other events, 2783.8 us)

commit v3 on v2

v3 whole, which is shorter than its diff:
```python
import jax
import jax.numpy as jnp
from jax import lax
from jax.sharding import PartitionSpec as P


def ring_tables(ei_size, eo_size):
    chips_y = eo_size // 2
    walk = [(z, 0) for z in range(ei_size)] + [(z, 1) for z in reversed(range(ei_size))]
    assert chips_y == 2
    return [[z * eo_size + y * 2 + core for core in range(2)] for z, y in walk]


def solution(mesh):
    axes = ('ei', 'eo')
    ei_size, eo_size = mesh.shape['ei'], mesh.shape['eo']
    table = ring_tables(ei_size, eo_size)
    ring = len(table)
    half = ring // 2
    pairs = lambda step: [(table[p][c], table[(p + step) % ring][c]) for p in range(ring) for c in range(2)]
    cw_perm, ccw_perm = pairs(1), pairs(-1)
    swap_perm = [(table[p][c], table[p][1 - c]) for p in range(ring) for c in range(2)]
    tok_spec = P(('dp', 'ei', 'eo'))
    exp_spec = P(('ei', 'eo'))
    f32 = jnp.float32
    bf16 = jnp.bfloat16
    nt = (((1,), (1,)), ((), ()))
    tn = (((0,), (0,)), ((), ()))
    chunks = [(ring - k, k) for k in range(1, half)] + [(half,), (0,)]

    def cw(v):
        return lax.ppermute(v, axes, cw_perm)

    def ccw(v):
        return lax.ppermute(v, axes, ccw_perm)

    def swap(v):
        return lax.ppermute(v, axes, swap_perm)

    def direct(v, r, k):
        perm = [(table[(p + r) % ring][c ^ k], table[p][c]) for p in range(ring) for c in range(2)]
        return lax.ppermute(v, axes, perm) if r or k else v

    def gather_rings(*owns):
        got = [[own] + [None] * (ring - 1) for own in owns]
        for k in range(1, half):
            for blocks in got:
                blocks[ring - k] = cw(blocks[(ring - k + 1) % ring])
                blocks[k] = ccw(blocks[k - 1])
        for blocks in got:
            width = blocks[0].shape[1] // 2
            left = cw(blocks[half + 1][:, :width])
            right = ccw(blocks[half - 1][:, width:])
            blocks[half] = jnp.concatenate([left, right], axis=1)
        return [[(v, swap(v)) for v in blocks] for blocks in got]

    def scatter_step(s, acc, term):
        if s == 0:
            return term(ring - 1, 0), term(1, 1)
        left = cw(acc[0])
        right = ccw(acc[1])
        return left + term(ring - 1 - s, 0), right + term((1 + s) % ring, 1)

    def device_step(tok_loc, idx_loc, gate_loc, w_gate, w_up, w_down, dy_loc):
        me = lax.axis_index('ei') * eo_size + lax.axis_index('eo')
        tok_dev, top_k = idx_loc.shape
        d_model = tok_loc.shape[1]
        width = d_model // 2
        w_gate, w_up, w_down = w_gate[0], w_up[0], w_down[0]

        meta_loc = jnp.concatenate([idx_loc.astype(f32), gate_loc], axis=1).T
        meta_blk = [[direct(meta_loc, r, k) for k in range(2)] for r in range(ring)]
        x_blk, dy_blk = gather_rings(tok_loc, dy_loc)

        def gate_of(meta, expert):
            hit = meta[:top_k].astype(jnp.int32) == expert
            return hit, jnp.sum(jnp.where(hit, meta[top_k:], 0.0), axis=0)[:, None]

        saved = []
        y_of, dx_of, y_mate, dx_mate = {}, {}, {}, {}

        def y_term(r, side):
            cols = slice(side * width, (side + 1) * width)
            return gate_of(meta_blk[r][0], me)[1] * y_of[r][:, cols].astype(f32) + gate_of(meta_blk[r][0], me ^ 1)[1] * y_mate[r][:, cols].astype(f32)

        def dx_term(r, side):
            cols = slice(side * width, (side + 1) * width)
            return dx_of[r][:, cols].astype(f32) + dx_mate[r][:, cols].astype(f32)

        def dot_term(r):
            dyf = dy_blk[r][0].astype(f32)
            own = jnp.sum(dyf * y_of[r].astype(f32), axis=1)
            mate = jnp.sum(dyf * y_mate[r].astype(f32), axis=1)
            hit, hit_mate = (gate_of(meta_blk[r][0], expert)[0] for expert in (me, me ^ 1))
            return jnp.where(hit, own[None, :], 0.0) + jnp.where(hit_mate, mate[None, :], 0.0)

        y_acc = dx_acc = dot_acc = None

        def advance(s):
            nonlocal y_acc, dx_acc, dot_acc
            dot_acc = dot_term(ring - 1 - s) if s == 0 else cw(dot_acc) + dot_term(ring - 1 - s)
            y_acc = scatter_step(s, y_acc, y_term)
            dx_acc = scatter_step(s, dx_acc, dx_term)
            if s < ring - 1:
                y_acc, dx_acc, dot_acc = lax.optimization_barrier((y_acc, dx_acc, dot_acc))

        for n, offs in enumerate(chunks):
            names = [(r, k) for k in range(2) for r in offs]
            x = jnp.concatenate([x_blk[r][k] for r, k in names])
            dy = jnp.concatenate([dy_blk[r][k] for r, k in names])
            meta = jnp.concatenate([meta_blk[r][k] for r, k in names], axis=1)
            hit, g = gate_of(meta, me)
            on = jnp.any(hit, axis=0)[:, None]
            a = jnp.where(on, jnp.dot(x, w_gate, preferred_element_type=f32), 0.0)
            b = jnp.where(on, jnp.dot(x, w_up, preferred_element_type=f32), 0.0)
            s = jax.nn.sigmoid(a)
            h = (a * s * b).astype(bf16)
            o = jnp.dot(h, w_down, preferred_element_type=f32).astype(bf16)
            u = (g * dy.astype(f32)).astype(bf16)
            q = lax.dot_general(u, w_down, nt, preferred_element_type=f32)
            du = (q * a * s).astype(bf16)
            dg = (q * b * s * (1.0 + a * (1.0 - s))).astype(bf16)
            dx = (lax.dot_general(dg, w_gate, nt, preferred_element_type=f32) + lax.dot_general(du, w_up, nt, preferred_element_type=f32)).astype(bf16)
            saved.append((h, u, dg, du))
            split = len(offs) * tok_dev
            o_mate, dxs_mate = swap(o[split:]), swap(dx[split:])
            for i, r in enumerate(offs):
                rows = slice(i * tok_dev, (i + 1) * tok_dev)
                y_of[r], dx_of[r] = o[rows], dx[rows]
                y_mate[r], dx_mate[r] = o_mate[rows], dxs_mate[rows]
            if n < half:
                advance(n)

        for s in range(half, ring):
            advance(s)
        layer_out = jnp.concatenate(y_acc, axis=1).astype(bf16)
        grad_tokens = jnp.concatenate(dx_acc, axis=1).astype(bf16)
        grad_gates = dot_acc.T

        x_cat = jnp.concatenate([x_blk[r][k] for offs in chunks for k in range(2) for r in offs])
        h, u, dg, du = (jnp.concatenate(v) for v in zip(*saved))
        gwg = lax.dot_general(x_cat, dg, tn, preferred_element_type=f32).astype(bf16)
        gwu = lax.dot_general(x_cat, du, tn, preferred_element_type=f32).astype(bf16)
        gwd = lax.dot_general(h, u, tn, preferred_element_type=f32).astype(bf16)
        return layer_out, grad_tokens, grad_gates, gwg[None], gwu[None], gwd[None]

    return jax.shard_map(device_step, mesh=mesh, in_specs=(tok_spec, tok_spec, tok_spec, exp_spec, exp_spec, exp_spec, tok_spec), out_specs=(tok_spec, tok_spec, tok_spec, tok_spec, tok_spec, tok_spec), check_vma=False)
```

time: 802 us -> 806 us (level)
  blocking collectives: 23.6 us -> 0 us
  starting transfers between devices: 58.6 us -> 73.3 us
  other arithmetic: 65.5 us -> 77.5 us
    ppermute x0 -> x15, waiting for transfers between devices: none -> 69.6 us  [direct(): return lax.ppermute(v, axes, perm) if r or k else v]
    ppermute x29, waiting for transfers between devices: 159 us -> 112 us  [cw(): return lax.ppermute(v, axes, cw_perm)]
    ppermute x22, waiting for transfers between devices: 38.2 us -> 13.4 us  [ccw(): return lax.ppermute(v, axes, ccw_perm)]
    all_gather x1 -> x0, blocking collectives: 23.6 us -> none  [device_step(): meta = lax.all_gather(meta, axes, axis=0, tiled=True)]
    ppermute x0 -> x15, starting transfers between devices: none -> 13 us  [direct(): return lax.ppermute(v, axes, perm) if r or k else v]
    ppermute x29, starting transfers between devices: 23.5 us -> 34 us  [cw(): return lax.ppermute(v, axes, cw_perm)]
    ppermute x22, starting transfers between devices: 29.8 us -> 20.6 us  [ccw(): return lax.ppermute(v, axes, ccw_perm)]
    unnamed x11 -> x12, other arithmetic: 18.9 us -> 25.7 us
  transfers between devices with their start and end apart: 83 -> 92, of which waited for: 25 -> 37; matrix products, arithmetic and copies ran while one was open for 64% -> 65% of each run, Pallas kernels for 0% -> 0%
where the time goes in v3:
time: 806 us; the launch traced here: 799 us
  matrix products  408 us (51%)
  waiting for transfers between devices  195 us (24%)
  other arithmetic  77.5 us (10%)
  starting transfers between devices  73.3 us (9%)
  local copies, waits for them, and re-layouts  42.7 us (5%)
    ppermute x29, waiting for transfers between devices, cw(): return lax.ppermute(v, axes, cw_perm)  112 us
    dot_general x5, matrix products, device_step(): a = jnp.where(on, jnp.dot(x, w_gate, preferred_element_type=f32), 0.0)  81.6 us
    ppermute x15, waiting for transfers between devices, direct(): return lax.ppermute(v, axes, perm) if r or k else v  69.6 us
    dot_general x5, matrix products, device_step(): q = lax.dot_general(u, w_down, nt, preferred_element_type=f32)  56.2 us
    dot_general x5, matrix products, device_step(): lax.dot_general(du, w_up, nt, preferred_element_type=f32)  48.9 us
    dot_general x5, matrix products, device_step(): lax.dot_general(dg, w_gate, nt, preferred_element_type=f32)  47.1 us
    dot_general x5, matrix products, device_step(): o = jnp.dot(h, w_down, preferred_element_type=f32).astype(bf16)  39.1 us
    dot_general x5, matrix products, device_step(): b = jnp.where(on, jnp.dot(x, w_up, preferred_element_type=f32), 0.0)  36.5 us
  transfers between devices with their start and end apart: 92, of which 37 were waited for; matrix products, arithmetic and copies ran while one was open for 65% of the time, Pallas kernels for 0%

profile of v3, /device:TPU:0, one launch (start us, length us, event | category | flops | bytes accessed | tf_op | source)
XLA Modules:
  0.0 798.7 jit_solution(4856391868162573937)
XLA Ops:
  2.1 3.1 collective-permute-start
  8.9 22.6 %collective-permute-done.1 = f32[8,256]{1,0:T(8,128)S(1)} collective-permute-done((f32[8,256]{1,0:T(8,128)S(1)}, f32[8,256]{1,0:T(8,128)S(1)}, u32[]{:S(2)}, u32[]{:S(2)}) %collective-permute-start.1) | collective-permute-done | bytes 8224 | tf_op jit(solution)/shard_map/ppermute | solution.py:42
  31.5 3.1 collective-permute-done.2
  34.6 3.1 collective-permute-done.3
  42.4 4.3 collective-permute-done.16
  46.8 4.0 collective-permute-done.17
  50.7 4.0 collective-permute-done.18
  57.0 4.0 collective-permute-done.53
  61.9 4.9 collective-permute-done.54
  72.3 5.4 collective-permute-done.35
  77.7 4.9 collective-permute-done.36
  82.6 4.9 collective-permute-done.37
  100.7 7.9 fusion.3
  112.2 7.4 collective-permute-done.10
  121.3 8.4 %fusion.41 = f32[1024,1408]{1,0:T(8,128)} fusion(bf16[1024,2048]{1,0:T(8,128)(2,1)S(1)} %get-tuple-element.248, bf16[1,2048,1408]{2,1,0:T(8,128)(2,1)S(1)} %bitcast.141), kind=kOutput, calls=%fused_computation.50 | convolution fusion | flops 5905580032 | bytes 15728640 | tf_op jit(solution)/shard_map/dot_general | solution.py:115
  132.1 11.6 %fusion.19 = f32[1024,1408]{1,0:T(8,128)} fusion(bf16[1,1408,2048]{2,1,0:T(8,128)(2,1)S(1)} %bitcast.151, bf16[256,2048]{1,0:T(8,128)(2,1)S(1)} %collective-permute-done.12, bf16[256,2048]{1,0:T(8,128)(2,1)S(1)} %collective-permute-done.11, bf16[256,2048]{1,0:T(8,128)(2,1)S(1)} %collective-permute-done.10, ...), kind=kOutput, calls=%fused_computation.28 | convolution fusion | flops 5926551552 | bytes 15732736 | tf_op jit(solution)/shard_map/dot_general | solution.py:120
  143.7 18.5 %constant_dynamic-update-slice_fusion.52 = (bf16[4096,1408]{1,0:T(8,128)(2,1)}, bf16[1024,1408]{1,0:T(8,128)(2,1)}, bf16[4096,1408]{1,0:T(8,128)(2,1)}, bf16[102...) fusion(f32[1024,1408]{1,0:T(8,128)} %fusion.19, f32[1024,1408]{1,0:T(8,128)} %fusion.41, ...), kind=kOutput, calls=%fused_computation.224 | convolution fusion | flops 5931532288 | bytes 38798336 | tf_op jit(solution)/shard_map/dot_general | solution.py:114
  162.3 11.8 %fusion.39 = f32[1024,2048]{1,0:T(8,128)} fusion(bf16[1024,1408]{1,0:T(8,128)(2,1)} %get-tuple-element.186, bf16[1,2048,1408]{2,1,0:T(8,128)(2,1)} %param.11), kind=kOutput, calls=%fused_computation.48 | convolution fusion | flops 5905580032 | bytes 17039360 | tf_op jit(solution)/shard_map/dot_general | solution.py:123
  174.1 10.9 %add_convert_fusion.2 = bf16[1024,2048]{1,0:T(8,128)(2,1)S(1)} fusion(f32[1024,2048]{1,0:T(8,128)} %fusion.39, bf16[1024,1408]{1,0:T(8,128)(2,1)} %get-tuple-element.143, bf16[1,2048,1408]{2,1,0:T(8,128)(2,1)} %param.10), kind=kOutput, calls=%fused_computation.4 | convolution fusion | flops 5909774336 | bytes 21233664 | tf_op jit(solution)/shard_map/dot_general | solution.py:123
  185.1 9.9 %fusion.63 = bf16[1024,2048]{1,0:T(8,128)(2,1)S(1)} fusion(bf16[1024,1408]{1,0:T(8,128)(2,1)} %get-tuple-element.184, bf16[1,1408,2048]{2,1,0:T(8,128)(2,1)S(1)} %bitcast.153), kind=kOutput, calls=%fused_computation.88 | convolution fusion | flops 5907677184 | bytes 12845056 | tf_op jit(solution)/shard_map/dot_general | solution.py:118
  201.6 7.4 constant_dynamic-update-slice_fusion.67
  213.6 8.4 %fusion.37 = f32[1024,1408]{1,0:T(8,128)} fusion(bf16[1024,2048]{1,0:T(8,128)(2,1)S(1)} %get-tuple-element.240, bf16[1,2048,1408]{2,1,0:T(8,128)(2,1)S(1)} %bitcast.143), kind=kOutput, calls=%fused_computation.46 | convolution fusion | flops 5905580032 | bytes 15728640 | tf_op jit(solution)/shard_map/dot_general | solution.py:115
  222.0 12.5 %collective-permute-done.45 = bf16[256,2048]{1,0:T(8,128)(2,1)S(1)} collective-permute-done((bf16[256,2048]{1,0:T(8,128)(2,1)S(1)}, bf16[256,2048]{1,0:T(8,128)(2,1)S(1)}, u32[]{:S(2)}, u32[]{:S(2)}) %collective-permute-start.45) | collective-permute-done | bytes 1048608 | tf_op jit(solution)/shard_map/ppermute | solution.py:32
  240.7 14.3 %fusion.15 = f32[1024,1408]{1,0:T(8,128)} fusion(bf16[1,1408,2048]{2,1,0:T(8,128)(2,1)} %param.12, bf16[256,2048]{1,0:T(8,128)(2,1)S(1)} %collective-permute-done.29, bf16[256,2048]{1,0:T(8,128)(2,1)S(1)} %collective-permute-done.28, bf16[256,2048]{1,0:T(8,128)(2,1)S(1)} %collective-permute-done.27, bf16[256,2048]{1,0:T(8,128)(2,1)S(1)} %collective-permute-done.26, ...), kind=kOutput, calls=%fused_computation.24 | convolution fusion | flops 5926551552 | bytes 15732736 | tf_op jit(solution)/shard_map/dot_general | solution.py:120
  255.0 18.5 %constant_dynamic-update-slice_fusion.51 = (bf16[4096,1408]{1,0:T(8,128)(2,1)}, bf16[1024,1408]{1,0:T(8,128)(2,1)}, bf16[4096,1408]{1,0:T(8,128)(2,1)}, bf16[102...) fusion(bf16[4096,1408]{1,0:T(8,128)(2,1)} %get-tuple-element.142, ...), kind=kOutput, calls=%fused_computation.223 | convolution fusion | flops 5931532288 | bytes 38798336 | tf_op jit(solution)/shard_map/dot_general | solution.py:114
  273.5 11.8 %fusion.35 = f32[1024,2048]{1,0:T(8,128)} fusion(bf16[1024,1408]{1,0:T(8,128)(2,1)} %get-tuple-element.182, bf16[1,2048,1408]{2,1,0:T(8,128)(2,1)} %param.11), kind=kOutput, calls=%fused_computation.44 | convolution fusion | flops 5905580032 | bytes 17039360 | tf_op jit(solution)/shard_map/dot_general | solution.py:123
  285.3 10.9 %add_convert_fusion.1 = bf16[1024,2048]{1,0:T(8,128)(2,1)S(1)} fusion(f32[1024,2048]{1,0:T(8,128)} %fusion.35, bf16[1024,1408]{1,0:T(8,128)(2,1)S(1)} %copy-done.76, bf16[1,2048,1408]{2,1,0:T(8,128)(2,1)} %param.10), kind=kOutput, calls=%fused_computation.2 | convolution fusion | flops 5909774336 | bytes 21233664 | tf_op jit(solution)/shard_map/dot_general | solution.py:123
  296.3 10.1 %fusion.66 = bf16[1024,2048]{1,0:T(8,128)(2,1)S(1)} fusion(bf16[1024,1408]{1,0:T(8,128)(2,1)S(1)} %copy-done.74, bf16[1,1408,2048]{2,1,0:T(8,128)(2,1)} %param.12), kind=kOutput, calls=%fused_computation.89 | convolution fusion | flops 5907677184 | bytes 12845056 | tf_op jit(solution)/shard_map/dot_general | solution.py:118
  306.5 8.2 %constant_dynamic-update-slice_fusion.66 = bf16[4096,2048]{1,0:T(8,128)(2,1)} fusion(bf16[4096,2048]{1,0:T(8,128)(2,1)} %constant_dynamic-update-slice_fusion.67, bf16[256,2048]{1,0:T(8,128)(2,1)S(1)} %collective-permute-done.29, bf16[256,2048]{1,0:T(8,128)(2,1)S(1)} %collective-permute-done.28, bf16[256,2048]{1,0:T(8,128)(2,1)S(1)} %collective-permute-done.27, ...), kind=kLoop, calls=%fused_computation.238 | loop fusion | flops 20971520 | bytes 8392704
  330.8 8.4 %fusion.33 = f32[1024,1408]{1,0:T(8,128)} fusion(bf16[1024,2048]{1,0:T(8,128)(2,1)S(1)} %get-tuple-element.232, bf16[1,2048,1408]{2,1,0:T(8,128)(2,1)S(1)} %bitcast.145), kind=kOutput, calls=%fused_computation.42 | convolution fusion | flops 5905580032 | bytes 15728640 | tf_op jit(solution)/shard_map/dot_general | solution.py:115
  341.4 14.6 %fusion.11 = f32[1024,1408]{1,0:T(8,128)} fusion(bf16[1,1408,2048]{2,1,0:T(8,128)(2,1)} %param.12, bf16[256,2048]{1,0:T(8,128)(2,1)S(1)} %collective-permute-done.48, bf16[256,2048]{1,0:T(8,128)(2,1)S(1)} %collective-permute-done.47, bf16[256,2048]{1,0:T(8,128)(2,1)S(1)} %collective-permute-done.46, bf16[256,2048]{1,0:T(8,128)(2,1)S(1)} %collective-permute-done.45, ...), kind=kOutput, calls=%fused_computation.20 | convolution fusion | flops 5926551552 | bytes 15732736 | tf_op jit(solution)/shard_map/dot_general | solution.py:120
  356.0 18.6 %constant_dynamic-update-slice_fusion.50 = (bf16[4096,1408]{1,0:T(8,128)(2,1)}, bf16[1024,1408]{1,0:T(8,128)(2,1)}, bf16[4096,1408]{1,0:T(8,128)(2,1)}, bf16[102...) fusion(bf16[4096,1408]{1,0:T(8,128)(2,1)} %get-tuple-element.140, ...), kind=kOutput, calls=%fused_computation.222 | convolution fusion | flops 5931532288 | bytes 38798336 | tf_op jit(solution)/shard_map/dot_general | solution.py:114
  374.6 11.8 %fusion.31 = f32[1024,2048]{1,0:T(8,128)} fusion(bf16[1024,1408]{1,0:T(8,128)(2,1)} %get-tuple-element.178, bf16[1,2048,1408]{2,1,0:T(8,128)(2,1)} %param.11), kind=kOutput, calls=%fused_computation.40 | convolution fusion | flops 5905580032 | bytes 17039360 | tf_op jit(solution)/shard_map/dot_general | solution.py:123
  386.4 10.9 %add_convert_fusion = bf16[1024,2048]{1,0:T(8,128)(2,1)S(1)} fusion(f32[1024,2048]{1,0:T(8,128)} %fusion.31, bf16[1024,1408]{1,0:T(8,128)(2,1)S(1)} %copy-done.77, bf16[1,2048,1408]{2,1,0:T(8,128)(2,1)} %param.10), kind=kOutput, calls=%fused_computation | convolution fusion | flops 5909774336 | bytes 21233664 | tf_op jit(solution)/shard_map/dot_general | solution.py:123
  399.0 4.2 convert_add_fusion
  404.4 8.8 %fusion.69 = bf16[1024,2048]{1,0:T(8,128)(2,1)S(1)} fusion(bf16[1024,1408]{1,0:T(8,128)(2,1)S(1)} %copy-done.73, bf16[1,1408,2048]{2,1,0:T(8,128)(2,1)} %param.12), kind=kOutput, calls=%fused_computation.90 | convolution fusion | flops 5907677184 | bytes 12845056 | tf_op jit(solution)/shard_map/dot_general | solution.py:118
  420.4 8.4 %constant_dynamic-update-slice_fusion.65 = bf16[4096,2048]{1,0:T(8,128)(2,1)} fusion(bf16[4096,2048]{1,0:T(8,128)(2,1)} %constant_dynamic-update-slice_fusion.66, bf16[256,2048]{1,0:T(8,128)(2,1)S(1)} %copy-done.27, bf16[256,2048]{1,0:T(8,128)(2,1)S(1)} %copy-done.25, bf16[256,2048]{1,0:T(8,128)(2,1)S(1)} %collective-permute-done.46, ...), kind=kLoop, calls=%fused_computation.237 | loop fusion | flops 20971520 | bytes 8392704
  430.6 7.8 fusion.7
  446.0 6.2 fusion.78
  452.2 13.0 %constant_dynamic-update-slice_fusion.49 = (bf16[4096,1408]{1,0:T(8,128)(2,1)}, bf16[512,1408]{1,0:T(8,128)(2,1)}, bf16[4096,1408]{1,0:T(8,128)(2,1)}, bf16[512,...) fusion(bf16[4096,1408]{1,0:T(8,128)(2,1)} %get-tuple-element.138, ...), kind=kOutput, calls=%fused_computation.221 | convolution fusion | flops 2969239552 | bytes 22282752 | tf_op jit(solution)/shard_map/dot_general | solution.py:114
  466.8 3.1 collective-permute-done.25
  471.8 2.8 add_add_fusion.20
  474.6 8.1 %fusion.27 = f32[512,2048]{1,0:T(8,128)} fusion(bf16[512,1408]{1,0:T(8,128)(2,1)S(1)} %copy-done.72, bf16[1,2048,1408]{2,1,0:T(8,128)(2,1)} %param.11), kind=kOutput, calls=%fused_computation.36 | convolution fusion | flops 2952790016 | bytes 11403264 | tf_op jit(solution)/shard_map/dot_general | solution.py:123
  482.6 8.4 %collective-permute-done.14 = f32[256,1024]{1,0:T(8,128)S(1)} collective-permute-done((f32[256,1024]{1,0:T(8,128)}, f32[256,1024]{1,0:T(8,128)S(1)}, u32[]{:S(2)}, u32[]{:S(2)}) %collective-permute-start.14) | collective-permute-done | bytes 1048608 | tf_op jit(solution)/shard_map/ppermute | solution.py:32
  496.4 7.9 add_convert_fusion.4
  504.3 6.6 fusion.94
  521.4 3.7 add_add_fusion.18
  525.1 14.4 %collective-permute-done.44 = f32[256,1024]{1,0:T(8,128)S(1)} collective-permute-done((f32[256,1024]{1,0:T(8,128)S(1)}, f32[256,1024]{1,0:T(8,128)S(1)}, u32[]{:S(2)}, u32[]{:S(2)}) %collective-permute-start.44) | collective-permute-done | bytes 1048608 | tf_op jit(solution)/shard_map/ppermute | solution.py:32
  544.7 5.0 fusion.81
  553.9 12.9 %constant_dynamic-update-slice_fusion.48 = (bf16[4096,1408]{1,0:T(8,128)(2,1)}, bf16[512,1408]{1,0:T(8,128)(2,1)}, bf16[4096,1408]{1,0:T(8,128)(2,1)}, bf16[512,...) fusion(bf16[4096,1408]{1,0:T(8,128)(2,1)} %get-tuple-element.136, ...), kind=kOutput, calls=%fused_computation.220 | convolution fusion | flops 2965045248 | bytes 22282752 | tf_op jit(solution)/shard_map/dot_general | solution.py:114
  567.6 8.5 %collective-permute-done.60 = f32[256,1024]{1,0:T(8,128)} collective-permute-done((f32[256,1024]{1,0:T(8,128)}, f32[256,1024]{1,0:T(8,128)}, u32[]{:S(2)}, u32[]{:S(2)}) %collective-permute-start.60) | collective-permute-done | bytes 1048608 | tf_op jit(solution)/shard_map/ppermute | solution.py:32
  579.1 13.7 %collective-permute-done.52 = f32[256,1024]{1,0:T(8,128)} collective-permute-done((f32[256,1024]{1,0:T(8,128)}, f32[256,1024]{1,0:T(8,128)}, u32[]{:S(2)}, u32[]{:S(2)}) %collective-permute-start.52) | collective-permute-done | bytes 1048608 | tf_op jit(solution)/shard_map/ppermute | solution.py:32
  593.0 3.0 add_add_fusion.14
  600.6 33.6 %fusion.2 = bf16[1,2048,1408]{2,1,0:T(8,128)(2,1)} fusion(bf16[4096,2048]{1,0:T(8,128)(2,1)} %get-tuple-element.227, bf16[4096,1408]{1,0:T(8,128)(2,1)} %get-tuple-element.213), kind=kOutput, calls=%fused_computation.11 | convolution fusion | flops 23625203712 | bytes 34078720 | tf_op jit(solution)/shard_map/dot_general | solution.py:143
  636.3 3.9 collective-permute-done.67
  644.6 33.7 %fusion.1 = bf16[1,2048,1408]{2,1,0:T(8,128)(2,1)} fusion(bf16[4096,2048]{1,0:T(8,128)(2,1)} %get-tuple-element.227, bf16[4096,1408]{1,0:T(8,128)(2,1)} %get-tuple-element.134), kind=kOutput, calls=%fused_computation.10 | convolution fusion | flops 23625203712 | bytes 34078720 | tf_op jit(solution)/shard_map/dot_general | solution.py:142
  681.0 5.5 fusion.23
  688.3 13.0 %collective-permute-done.72 = f32[256,1024]{1,0:T(8,128)S(1)} collective-permute-done((f32[256,1024]{1,0:T(8,128)S(1)}, f32[256,1024]{1,0:T(8,128)S(1)}, u32[]{:S(2)}, u32[]{:S(2)}) %collective-permute-start.72) | collective-permute-done | bytes 1048608 | tf_op jit(solution)/shard_map/ppermute | solution.py:32
  704.8 6.5 add_convert_fusion.3
  715.3 3.6 fusion.97
  719.3 9.3 %collective-permute-done.81 = f32[4,256]{1,0:T(4,128)S(1)} collective-permute-done((f32[4,256]{1,0:T(4,128)S(1)}, f32[4,256]{1,0:T(4,128)S(1)}, u32[]{:S(2)}, u32[]{:S(2)}) %collective-permute-start.81) | collective-permute-done | bytes 4128 | tf_op jit(solution)/shard_map/ppermute | solution.py:32
  731.4 12.2 %collective-permute-done.77 = f32[256,1024]{1,0:T(8,128)S(1)} collective-permute-done((f32[256,1024]{1,0:T(8,128)S(1)}, f32[256,1024]{1,0:T(8,128)S(1)}, u32[]{:S(2)}, u32[]{:S(2)}) %collective-permute-start.77) | collective-permute-done | bytes 1048608 | tf_op jit(solution)/shard_map/ppermute | solution.py:32
  749.7 31.4 %fusion = bf16[1,1408,2048]{2,1,0:T(8,128)(2,1)} fusion(bf16[4096,1408]{1,0:T(8,128)(2,1)} %get-tuple-element.211, bf16[4096,2048]{1,0:T(8,128)(2,1)} %constant_dynamic-update-slice_fusion.63), kind=kOutput, calls=%fused_computation.9 | convolution fusion | flops 23625203712 | bytes 34078720 | tf_op jit(solution)/shard_map/dot_general | solution.py:144
  786.1 9.8 %collective-permute-done.82 = f32[256,1024]{1,0:T(8,128)S(1)} collective-permute-done((f32[256,1024]{1,0:T(8,128)S(1)}, f32[256,1024]{1,0:T(8,128)S(1)}, u32[]{:S(2)}, u32[]{:S(2)}) %collective-permute-start.82) | collective-permute-done | bytes 1048608 | tf_op jit(solution)/shard_map/ppermute | solution.py:32
  (452 shorter events, 166.2 us)
Async XLA Ops:
  5.2 88.2 %collective-permute-start.4 = (bf16[256,2048]{1,0:T(8,128)(2,1)}, bf16[256,2048]{1,0:T(8,128)(2,1)}, u32[]{:S(2)}, u32[]{:S(2)}) collective-permute-start(bf16[256,2048]{1,0:T(8,128)(2,1)} %param.7), channel_id=1, source_target_pairs={{0,4},{1,5},{4,8},{5,9},{8,12},{9,13},{12,14},{13,15},{14,10},{15,... | collective-permute-start | bytes 3145736 | tf_op jit(solution)/shard_map/ppermute | solution.py:32
  6.7 91.0 %collective-permute-start.5 = (bf16[256,2048]{1,0:T(8,128)(2,1)}, bf16[256,2048]{1,0:T(8,128)(2,1)}, u32[]{:S(2)}, u32[]{:S(2)}) collective-permute-start(bf16[256,2048]{1,0:T(8,128)(2,1)} %param.7), channel_id=1, source_target_pairs={{0,2},{1,3},{4,0},{5,1},{8,4},{9,5},{12,8},{13,9},{14,12},{15,13},... | collective-permute-start | bytes 3145736 | tf_op jit(solution)/shard_map/ppermute | solution.py:35
  7.2 506.0 %collective-permute-start.84 = (bf16[256,2048]{1,0:T(8,128)(2,1)}, bf16[256,2048]{1,0:T(8,128)(2,1)}, u32[]{:S(2)}, u32[]{:S(2)}) collective-permute-start(bf16[256,2048]{1,0:T(8,128)(2,1)} %param.7), channel_id=1, source_target_pairs={{0,1},{1,0},{4,5},{5,4},{8,9},{9,8},{12,13},{13,12},{14,15},{15,14... | collective-permute-start | bytes 3145736 | tf_op jit(solution)/shard_map/ppermute | solution.py:38
  7.2 82.1 %collective-permute-start.83 = (f32[8,256]{1,0:T(8,128)S(1)}, f32[8,256]{1,0:T(8,128)S(1)}, u32[]{:S(2)}, u32[]{:S(2)}) collective-permute-start(f32[8,256]{1,0:T(8,128)S(1)} %maximum_bitcast_fusion), channel_id=1, source_target_pairs={{1,0},{0,1},{5,4},{4,5},{9,8},{8,9},{13,12},{12,13},{15,14},{14,15... | collective-permute-start | bytes 24584 | tf_op jit(solution)/shard_map/ppermute | solution.py:42
  7.7 23.8 %collective-permute-start.1 = (f32[8,256]{1,0:T(8,128)S(1)}, f32[8,256]{1,0:T(8,128)S(1)}, u32[]{:S(2)}, u32[]{:S(2)}) collective-permute-start(f32[8,256]{1,0:T(8,128)S(1)} %maximum_bitcast_fusion), channel_id=1, source_target_pairs={{4,0},{5,1},{8,4},{9,5},{12,8},{13,9},{14,12},{15,13},{10,14},{11,... | collective-permute-start | bytes 24584 | tf_op jit(solution)/shard_map/ppermute | solution.py:42
  87.5 24.3 %collective-permute-start.9 = (bf16[256,2048]{1,0:T(8,128)(2,1)}, bf16[256,2048]{1,0:T(8,128)(2,1)S(1)}, u32[]{:S(2)}, u32[]{:S(2)}) collective-permute-start(bf16[256,2048]{1,0:T(8,128)(2,1)} %param.13), channel_id=1, source_target_pairs={{0,4},{1,5},{4,8},{5,9},{8,12},{9,13},{12,14},{13,15},{14,10},{15,... | collective-permute-start | bytes 3145736 | tf_op jit(solution)/shard_map/ppermute | solution.py:32
  93.4 26.2 %collective-permute-start.10 = (bf16[256,2048]{1,0:T(8,128)(2,1)}, bf16[256,2048]{1,0:T(8,128)(2,1)S(1)}, u32[]{:S(2)}, u32[]{:S(2)}) collective-permute-start(bf16[256,2048]{1,0:T(8,128)(2,1)} %param.13), channel_id=1, source_target_pairs={{0,2},{1,3},{4,0},{5,1},{8,4},{9,5},{12,8},{13,9},{14,12},{15,13},... | collective-permute-start | bytes 3145736 | tf_op jit(solution)/shard_map/ppermute | solution.py:35
  100.4 19.2 %collective-permute-start.7 = (bf16[256,2048]{1,0:T(8,128)(2,1)}, bf16[256,2048]{1,0:T(8,128)(2,1)S(1)}, u32[]{:S(2)}, u32[]{:S(2)}) collective-permute-start(bf16[256,2048]{1,0:T(8,128)(2,1)} %collective-permute-done.5), channel_id=1, source_target_pairs={{0,1},{1,0},{4,5},{5,4},{8,9},{9,8},{12,13},{13,12},{14,15},{15,14... | collective-permute-start | bytes 3145736 | tf_op jit(solution)/shard_map/ppermute | solution.py:38
  108.6 86.4 %collective-permute-start.19 = (bf16[256,2048]{1,0:T(8,128)(2,1)}, bf16[256,2048]{1,0:T(8,128)(2,1)S(1)}, u32[]{:S(2)}, u32[]{:S(2)}) collective-permute-start(bf16[256,2048]{1,0:T(8,128)(2,1)} %collective-permute-done.4), channel_id=1, source_target_pairs={{0,4},{1,5},{4,8},{5,9},{8,12},{9,13},{12,14},{13,15},{14,10},{15,... | collective-permute-start | bytes 3145736 | tf_op jit(solution)/shard_map/ppermute | solution.py:32
  111.8 87.8 %collective-permute-start.20 = (bf16[256,2048]{1,0:T(8,128)(2,1)}, bf16[256,2048]{1,0:T(8,128)(2,1)S(1)}, u32[]{:S(2)}, u32[]{:S(2)}) collective-permute-start(bf16[256,2048]{1,0:T(8,128)(2,1)} %collective-permute-done.5), channel_id=1, source_target_pairs={{0,2},{1,3},{4,0},{5,1},{8,4},{9,5},{12,8},{13,9},{14,12},{15,13},... | collective-permute-start | bytes 3145736 | tf_op jit(solution)/shard_map/ppermute | solution.py:35
  129.8 70.6 %collective-permute-start.26 = (bf16[256,2048]{1,0:T(8,128)(2,1)S(1)}, bf16[256,2048]{1,0:T(8,128)(2,1)S(1)}, u32[]{:S(2)}, u32[]{:S(2)}) collective-permute-start(bf16[256,2048]{1,0:T(8,128)(2,1)S(1)} %collective-permute-done.9), channel_id=1, source_target_pairs={{0,4},{1,5},{4,8},{5,9},{8,12},{9,13},{12,14},{13,15},{14,10},{15,... | collective-permute-start | bytes 3145736 | tf_op jit(solution)/shard_map/ppermute | solution.py:32
  131.3 77.7 %collective-permute-start.27 = (bf16[256,2048]{1,0:T(8,128)(2,1)S(1)}, bf16[256,2048]{1,0:T(8,128)(2,1)S(1)}, u32[]{:S(2)}, u32[]{:S(2)}) collective-permute-start(bf16[256,2048]{1,0:T(8,128)(2,1)S(1)} %collective-permute-done.10), channel_id=1, source_target_pairs={{0,2},{1,3},{4,0},{5,1},{8,4},{9,5},{12,8},{13,9},{14,12},{15,13},... | collective-permute-start | bytes 3145736 | tf_op jit(solution)/shard_map/ppermute | solution.py:35
  200.3 38.4 %collective-permute-start.28 = (bf16[256,2048]{1,0:T(8,128)(2,1)S(1)}, bf16[256,2048]{1,0:T(8,128)(2,1)S(1)}, u32[]{:S(2)}, u32[]{:S(2)}) collective-permute-start(bf16[256,2048]{1,0:T(8,128)(2,1)S(1)} %collective-permute-done.26), channel_id=1, source_target_pairs={{0,1},{1,0},{4,5},{5,4},{8,9},{9,8},{12,13},{13,12},{14,15},{15,14... | collective-permute-start | bytes 3145736 | tf_op jit(solution)/shard_map/ppermute | solution.py:38
  209.0 25.5 %collective-permute-start.45 = (bf16[256,2048]{1,0:T(8,128)(2,1)S(1)}, bf16[256,2048]{1,0:T(8,128)(2,1)S(1)}, u32[]{:S(2)}, u32[]{:S(2)}) collective-permute-start(bf16[256,2048]{1,0:T(8,128)(2,1)S(1)} %collective-permute-done.26), channel_id=1, source_target_pairs={{0,4},{1,5},{4,8},{5,9},{8,12},{9,13},{12,14},{13,15},{14,10},{15,... | collective-permute-start | bytes 3145736 | tf_op jit(solution)/shard_map/ppermute | solution.py:32
  210.6 29.7 %collective-permute-start.29 = (bf16[256,2048]{1,0:T(8,128)(2,1)S(1)}, bf16[256,2048]{1,0:T(8,128)(2,1)S(1)}, u32[]{:S(2)}, u32[]{:S(2)}) collective-permute-start(bf16[256,2048]{1,0:T(8,128)(2,1)S(1)} %collective-permute-done.27), channel_id=1, source_target_pairs={{0,1},{1,0},{4,5},{5,4},{8,9},{9,8},{12,13},{13,12},{14,15},{15,14... | collective-permute-start | bytes 3145736 | tf_op jit(solution)/shard_map/ppermute | solution.py:38
  211.9 25.4 %collective-permute-start.46 = (bf16[256,2048]{1,0:T(8,128)(2,1)S(1)}, bf16[256,2048]{1,0:T(8,128)(2,1)S(1)}, u32[]{:S(2)}, u32[]{:S(2)}) collective-permute-start(bf16[256,2048]{1,0:T(8,128)(2,1)S(1)} %collective-permute-done.27), channel_id=1, source_target_pairs={{0,2},{1,3},{4,0},{5,1},{8,4},{9,5},{12,8},{13,9},{14,12},{15,13},... | collective-permute-start | bytes 3145736 | tf_op jit(solution)/shard_map/ppermute | solution.py:35
  234.5 61.7 %collective-permute-start.38 = (bf16[256,2048]{1,0:T(8,128)(2,1)S(1)}, bf16[256,2048]{1,0:T(8,128)(2,1)}, u32[]{:S(2)}, u32[]{:S(2)}) collective-permute-start(bf16[256,2048]{1,0:T(8,128)(2,1)S(1)} %collective-permute-done.19), channel_id=1, source_target_pairs={{0,4},{1,5},{4,8},{5,9},{8,12},{9,13},{12,14},{13,15},{14,10},{15,... | collective-permute-start | bytes 3145736 | tf_op jit(solution)/shard_map/ppermute | solution.py:32
  237.4 69.1 %collective-permute-start.39 = (bf16[256,2048]{1,0:T(8,128)(2,1)S(1)}, bf16[256,2048]{1,0:T(8,128)(2,1)S(1)}, u32[]{:S(2)}, u32[]{:S(2)}) collective-permute-start(bf16[256,2048]{1,0:T(8,128)(2,1)S(1)} %collective-permute-done.20), channel_id=1, source_target_pairs={{0,2},{1,3},{4,0},{5,1},{8,4},{9,5},{12,8},{13,9},{14,12},{15,13},... | collective-permute-start | bytes 3145736 | tf_op jit(solution)/shard_map/ppermute | solution.py:35
  238.7 86.2 %collective-permute-start.61 = (bf16[256,1024]{1,0:T(8,128)(2,1)}, bf16[256,1024]{1,0:T(8,128)(2,1)}, u32[]{:S(2)}, u32[]{:S(2)}) collective-permute-start(bf16[256,1024]{1,0:T(8,128)(2,1)} %slice.671), channel_id=1, source_target_pairs={{0,4},{1,5},{4,8},{5,9},{8,12},{9,13},{12,14},{13,15},{14,10},{15,... | collective-permute-start | bytes 1572872 | tf_op jit(solution)/shard_map/ppermute | solution.py:32
  240.2 86.2 %collective-permute-start.62 = (bf16[256,1024]{1,0:T(8,128)(2,1)}, bf16[256,1024]{1,0:T(8,128)(2,1)}, u32[]{:S(2)}, u32[]{:S(2)}) collective-permute-start(bf16[256,1024]{1,0:T(8,128)(2,1)} %slice.672), channel_id=1, source_target_pairs={{0,2},{1,3},{4,0},{5,1},{8,4},{9,5},{12,8},{13,9},{14,12},{15,13},... | collective-permute-start | bytes 1572872 | tf_op jit(solution)/shard_map/ppermute | solution.py:35
  296.2 31.4 %collective-permute-start.40 = (bf16[256,2048]{1,0:T(8,128)(2,1)}, bf16[256,2048]{1,0:T(8,128)(2,1)S(1)}, u32[]{:S(2)}, u32[]{:S(2)}) collective-permute-start(bf16[256,2048]{1,0:T(8,128)(2,1)} %collective-permute-done.38), channel_id=1, source_target_pairs={{0,1},{1,0},{4,5},{5,4},{8,9},{9,8},{12,13},{13,12},{14,15},{15,14... | collective-permute-start | bytes 3145736 | tf_op jit(solution)/shard_map/ppermute | solution.py:38
  306.5 23.0 %collective-permute-start.41 = (bf16[256,2048]{1,0:T(8,128)(2,1)S(1)}, bf16[256,2048]{1,0:T(8,128)(2,1)S(1)}, u32[]{:S(2)}, u32[]{:S(2)}) collective-permute-start(bf16[256,2048]{1,0:T(8,128)(2,1)S(1)} %collective-permute-done.39), channel_id=1, source_target_pairs={{0,1},{1,0},{4,5},{5,4},{8,9},{9,8},{12,13},{13,12},{14,15},{15,14... | collective-permute-start | bytes 3145736 | tf_op jit(solution)/shard_map/ppermute | solution.py:38
  324.9 73.6 %collective-permute-start.13 = (bf16[512,2048]{1,0:T(8,128)(2,1)}, bf16[512,2048]{1,0:T(8,128)(2,1)}, u32[]{:S(2)}, u32[]{:S(2)}) collective-permute-start(bf16[512,2048]{1,0:T(8,128)(2,1)} %slice.618), channel_id=1, source_target_pairs={{0,1},{1,0},{4,5},{5,4},{8,9},{9,8},{12,13},{13,12},{14,15},{15,14... | collective-permute-start | bytes 6291464 | tf_op jit(solution)/shard_map/ppermute | solution.py:38
  326.4 86.8 %collective-permute-start.8 = (bf16[512,2048]{1,0:T(8,128)(2,1)}, bf16[512,2048]{1,0:T(8,128)(2,1)S(1)}, u32[]{:S(2)}, u32[]{:S(2)}) collective-permute-start(bf16[512,2048]{1,0:T(8,128)(2,1)} %slice.610), channel_id=1, source_target_pairs={{0,1},{1,0},{4,5},{5,4},{8,9},{9,8},{12,13},{13,12},{14,15},{15,14... | collective-permute-start | bytes 6291464 | tf_op jit(solution)/shard_map/ppermute | solution.py:38
  339.3 58.0 %collective-permute-start.55 = (bf16[256,1024]{1,0:T(8,128)(2,1)}, bf16[256,1024]{1,0:T(8,128)(2,1)S(1)}, u32[]{:S(2)}, u32[]{:S(2)}) collective-permute-start(bf16[256,1024]{1,0:T(8,128)(2,1)} %slice.663), channel_id=1, source_target_pairs={{0,4},{1,5},{4,8},{5,9},{8,12},{9,13},{12,14},{13,15},{14,10},{15,... | collective-permute-start | bytes 1572872 | tf_op jit(solution)/shard_map/ppermute | solution.py:32
  340.9 62.4 %collective-permute-start.56 = (bf16[256,1024]{1,0:T(8,128)(2,1)}, bf16[256,1024]{1,0:T(8,128)(2,1)S(1)}, u32[]{:S(2)}, u32[]{:S(2)}) collective-permute-start(bf16[256,1024]{1,0:T(8,128)(2,1)} %slice.664), channel_id=1, source_target_pairs={{0,2},{1,3},{4,0},{5,1},{8,4},{9,5},{12,8},{13,9},{14,12},{15,13},... | collective-permute-start | bytes 1572872 | tf_op jit(solution)/shard_map/ppermute | solution.py:35
  397.3 68.0 %collective-permute-start.30 = (bf16[512,2048]{1,0:T(8,128)(2,1)}, bf16[512,2048]{1,0:T(8,128)(2,1)}, u32[]{:S(2)}, u32[]{:S(2)}) collective-permute-start(bf16[512,2048]{1,0:T(8,128)(2,1)} %slice.636), channel_id=1, source_target_pairs={{0,1},{1,0},{4,5},{5,4},{8,9},{9,8},{12,13},{13,12},{14,15},{15,14... | collective-permute-start | bytes 6291464 | tf_op jit(solution)/shard_map/ppermute | solution.py:38
  398.5 41.7 %collective-permute-start.23 = (bf16[512,2048]{1,0:T(8,128)(2,1)}, bf16[512,2048]{1,0:T(8,128)(2,1)S(1)}, u32[]{:S(2)}, u32[]{:S(2)}) collective-permute-start(bf16[512,2048]{1,0:T(8,128)(2,1)} %slice.628), channel_id=1, source_target_pairs={{0,1},{1,0},{4,5},{5,4},{8,9},{9,8},{12,13},{13,12},{14,15},{15,14... | collective-permute-start | bytes 6291464 | tf_op jit(solution)/shard_map/ppermute | solution.py:38
  403.2 25.6 %collective-permute-start.63 = (bf16[256,2048]{1,0:T(8,128)(2,1)S(1)}, bf16[256,2048]{1,0:T(8,128)(2,1)S(1)}, u32[]{:S(2)}, u32[]{:S(2)}) collective-permute-start(bf16[256,2048]{1,0:T(8,128)(2,1)S(1)} %constant_dynamic-update-slice_fusion.28), channel_id=1, source_target_pairs={{0,1},{1,0},{4,5},{5,4},{8,9},{9,8},{12,13},{13,12},{14,15},{15,14... | collective-permute-start | bytes 3145736 | tf_op jit(solution)/shard_map/ppermute | solution.py:38
  413.3 32.1 %collective-permute-start.57 = (bf16[256,2048]{1,0:T(8,128)(2,1)}, bf16[256,2048]{1,0:T(8,128)(2,1)S(1)}, u32[]{:S(2)}, u32[]{:S(2)}) collective-permute-start(bf16[256,2048]{1,0:T(8,128)(2,1)} %get-tuple-element.256), channel_id=1, source_target_pairs={{0,1},{1,0},{4,5},{5,4},{8,9},{9,8},{12,13},{13,12},{14,15},{15,14... | collective-permute-start | bytes 3145736 | tf_op jit(solution)/shard_map/ppermute | solution.py:38
  428.8 96.3 %collective-permute-start.49 = (bf16[512,2048]{1,0:T(8,128)(2,1)}, bf16[512,2048]{1,0:T(8,128)(2,1)}, u32[]{:S(2)}, u32[]{:S(2)}) collective-permute-start(bf16[512,2048]{1,0:T(8,128)(2,1)} %slice.654), channel_id=1, source_target_pairs={{0,1},{1,0},{4,5},{5,4},{8,9},{9,8},{12,13},{13,12},{14,15},{15,14... | collective-permute-start | bytes 6291464 | tf_op jit(solution)/shard_map/ppermute | solution.py:38
  443.9 26.1 %collective-permute-start.25 = (f32[256,1024]{1,0:T(8,128)}, f32[256,1024]{1,0:T(8,128)S(1)}, u32[]{:S(2)}, u32[]{:S(2)}) collective-permute-start(f32[256,1024]{1,0:T(8,128)} %get-tuple-element.43), channel_id=1, source_target_pairs={{0,4},{1,5},{4,8},{5,9},{8,12},{9,13},{12,14},{13,15},{14,10},{15,... | collective-permute-start | bytes 3145736 | tf_op jit(solution)/shard_map/ppermute | solution.py:32
  445.4 26.3 %collective-permute-start.31 = (f32[256,1024]{1,0:T(8,128)}, f32[256,1024]{1,0:T(8,128)S(1)}, u32[]{:S(2)}, u32[]{:S(2)}) collective-permute-start(f32[256,1024]{1,0:T(8,128)} %get-tuple-element.44), channel_id=1, source_target_pairs={{0,2},{1,3},{4,0},{5,1},{8,4},{9,5},{12,8},{13,9},{14,12},{15,13},... | collective-permute-start | bytes 3145736 | tf_op jit(solution)/shard_map/ppermute | solution.py:35
  465.3 25.8 %collective-permute-start.14 = (f32[256,1024]{1,0:T(8,128)}, f32[256,1024]{1,0:T(8,128)S(1)}, u32[]{:S(2)}, u32[]{:S(2)}) collective-permute-start(f32[256,1024]{1,0:T(8,128)} %get-tuple-element.41), channel_id=1, source_target_pairs={{0,4},{1,5},{4,8},{5,9},{8,12},{9,13},{12,14},{13,15},{14,10},{15,... | collective-permute-start | bytes 3145736 | tf_op jit(solution)/shard_map/ppermute | solution.py:32
  469.9 22.6 %collective-permute-start.24 = (f32[256,1024]{1,0:T(8,128)S(1)}, f32[256,1024]{1,0:T(8,128)S(1)}, u32[]{:S(2)}, u32[]{:S(2)}) collective-permute-start(f32[256,1024]{1,0:T(8,128)S(1)} %get-tuple-element.42), channel_id=1, source_target_pairs={{0,2},{1,3},{4,0},{5,1},{8,4},{9,5},{12,8},{13,9},{14,12},{15,13},... | collective-permute-start | bytes 3145736 | tf_op jit(solution)/shard_map/ppermute | solution.py:35
  471.7 47.7 %collective-permute-start.42 = (bf16[512,2048]{1,0:T(8,128)(2,1)S(1)}, bf16[512,2048]{1,0:T(8,128)(2,1)S(1)}, u32[]{:S(2)}, u32[]{:S(2)}) collective-permute-start(bf16[512,2048]{1,0:T(8,128)(2,1)S(1)} %copy-done.16), channel_id=1, source_target_pairs={{0,1},{1,0},{4,5},{5,4},{8,9},{9,8},{12,13},{13,12},{14,15},{15,14... | collective-permute-start | bytes 6291464 | tf_op jit(solution)/shard_map/ppermute | solution.py:38
  494.4 26.4 %collective-permute-start.33 = (f32[256,1024]{1,0:T(8,128)}, f32[256,1024]{1,0:T(8,128)}, u32[]{:S(2)}, u32[]{:S(2)}) collective-permute-start(f32[256,1024]{1,0:T(8,128)} %get-tuple-element.46), channel_id=1, source_target_pairs={{0,4},{1,5},{4,8},{5,9},{8,12},{9,13},{12,14},{13,15},{14,10},{15,... | collective-permute-start | bytes 3145736 | tf_op jit(solution)/shard_map/ppermute | solution.py:32
  495.9 25.0 %collective-permute-start.43 = (f32[256,1024]{1,0:T(8,128)}, f32[256,1024]{1,0:T(8,128)}, u32[]{:S(2)}, u32[]{:S(2)}) collective-permute-start(f32[256,1024]{1,0:T(8,128)} %get-tuple-element.47), channel_id=1, source_target_pairs={{0,2},{1,3},{4,0},{5,1},{8,4},{9,5},{12,8},{13,9},{14,12},{15,13},... | collective-permute-start | bytes 3145736 | tf_op jit(solution)/shard_map/ppermute | solution.py:35
  517.4 22.1 %collective-permute-start.44 = (f32[256,1024]{1,0:T(8,128)S(1)}, f32[256,1024]{1,0:T(8,128)S(1)}, u32[]{:S(2)}, u32[]{:S(2)}) collective-permute-start(f32[256,1024]{1,0:T(8,128)S(1)} %copy-done.23), channel_id=1, source_target_pairs={{0,4},{1,5},{4,8},{5,9},{8,12},{9,13},{12,14},{13,15},{14,10},{15,... | collective-permute-start | bytes 3145736 | tf_op jit(solution)/shard_map/ppermute | solution.py:32
  519.4 21.3 %collective-permute-start.50 = (f32[256,1024]{1,0:T(8,128)S(1)}, f32[256,1024]{1,0:T(8,128)S(1)}, u32[]{:S(2)}, u32[]{:S(2)}) collective-permute-start(f32[256,1024]{1,0:T(8,128)S(1)} %get-tuple-element.49), channel_id=1, source_target_pairs={{0,2},{1,3},{4,0},{5,1},{8,4},{9,5},{12,8},{13,9},{14,12},{15,13},... | collective-permute-start | bytes 3145736 | tf_op jit(solution)/shard_map/ppermute | solution.py:35
  520.8 46.8 %collective-permute-start.64 = (bf16[256,2048]{1,0:T(8,128)(2,1)S(1)}, bf16[256,2048]{1,0:T(8,128)(2,1)}, u32[]{:S(2)}, u32[]{:S(2)}) collective-permute-start(bf16[256,2048]{1,0:T(8,128)(2,1)S(1)} %slice.674), channel_id=1, source_target_pairs={{0,1},{1,0},{4,5},{5,4},{8,9},{9,8},{12,13},{13,12},{14,15},{15,14... | collective-permute-start | bytes 3145736 | tf_op jit(solution)/shard_map/ppermute | solution.py:38
  520.9 30.8 %collective-permute-start.58 = (bf16[256,2048]{1,0:T(8,128)(2,1)S(1)}, bf16[256,2048]{1,0:T(8,128)(2,1)S(1)}, u32[]{:S(2)}, u32[]{:S(2)}) collective-permute-start(bf16[256,2048]{1,0:T(8,128)(2,1)S(1)} %slice.666), channel_id=1, source_target_pairs={{0,1},{1,0},{4,5},{5,4},{8,9},{9,8},{12,13},{13,12},{14,15},{15,14... | collective-permute-start | bytes 3145736 | tf_op jit(solution)/shard_map/ppermute | solution.py:38
  549.7 26.3 %collective-permute-start.60 = (f32[256,1024]{1,0:T(8,128)}, f32[256,1024]{1,0:T(8,128)}, u32[]{:S(2)}, u32[]{:S(2)}) collective-permute-start(f32[256,1024]{1,0:T(8,128)} %get-tuple-element.53), channel_id=1, source_target_pairs={{0,4},{1,5},{4,8},{5,9},{8,12},{9,13},{12,14},{13,15},{14,10},{15,... | collective-permute-start | bytes 3145736 | tf_op jit(solution)/shard_map/ppermute | solution.py:32
  550.2 26.1 %collective-permute-start.65 = (f32[256,1024]{1,0:T(8,128)S(1)}, f32[256,1024]{1,0:T(8,128)}, u32[]{:S(2)}, u32[]{:S(2)}) collective-permute-start(f32[256,1024]{1,0:T(8,128)S(1)} %get-tuple-element.54), channel_id=1, source_target_pairs={{0,2},{1,3},{4,0},{5,1},{8,4},{9,5},{12,8},{13,9},{14,12},{15,13},... | collective-permute-start | bytes 3145736 | tf_op jit(solution)/shard_map/ppermute | solution.py:35
  551.7 41.0 %collective-permute-start.52 = (f32[256,1024]{1,0:T(8,128)}, f32[256,1024]{1,0:T(8,128)}, u32[]{:S(2)}, u32[]{:S(2)}) collective-permute-start(f32[256,1024]{1,0:T(8,128)} %get-tuple-element.51), channel_id=1, source_target_pairs={{0,4},{1,5},{4,8},{5,9},{8,12},{9,13},{12,14},{13,15},{14,10},{15,... | collective-permute-start | bytes 3145736 | tf_op jit(solution)/shard_map/ppermute | solution.py:32
  552.2 40.8 %collective-permute-start.59 = (f32[256,1024]{1,0:T(8,128)}, f32[256,1024]{1,0:T(8,128)}, u32[]{:S(2)}, u32[]{:S(2)}) collective-permute-start(f32[256,1024]{1,0:T(8,128)} %get-tuple-element.52), channel_id=1, source_target_pairs={{0,2},{1,3},{4,0},{5,1},{8,4},{9,5},{12,8},{13,9},{14,12},{15,13},... | collective-permute-start | bytes 3145736 | tf_op jit(solution)/shard_map/ppermute | solution.py:35
  596.0 38.2 %collective-permute-start.71 = (f32[4,256]{1,0:T(4,128)S(1)}, f32[4,256]{1,0:T(4,128)S(1)}, u32[]{:S(2)}, u32[]{:S(2)}) collective-permute-start(f32[4,256]{1,0:T(4,128)S(1)} %get-tuple-element.60), channel_id=1, source_target_pairs={{0,4},{1,5},{4,8},{5,9},{8,12},{9,13},{12,14},{13,15},{14,10},{15,... | collective-permute-start | bytes 12296 | tf_op jit(solution)/shard_map/ppermute | solution.py:32
  596.5 37.7 %collective-permute-start.69 = (f32[256,1024]{1,0:T(8,128)S(1)}, f32[256,1024]{1,0:T(8,128)S(1)}, u32[]{:S(2)}, u32[]{:S(2)}) collective-permute-start(f32[256,1024]{1,0:T(8,128)S(1)} %get-tuple-element.58), channel_id=1, source_target_pairs={{0,4},{1,5},{4,8},{5,9},{8,12},{9,13},{12,14},{13,15},{14,10},{15,... | collective-permute-start | bytes 3145736 | tf_op jit(solution)/shard_map/ppermute | solution.py:32
  597.2 37.0 %collective-permute-start.70 = (f32[256,1024]{1,0:T(8,128)S(1)}, f32[256,1024]{1,0:T(8,128)}, u32[]{:S(2)}, u32[]{:S(2)}) collective-permute-start(f32[256,1024]{1,0:T(8,128)S(1)} %get-tuple-element.59), channel_id=1, source_target_pairs={{0,2},{1,3},{4,0},{5,1},{8,4},{9,5},{12,8},{13,9},{14,12},{15,13},... | collective-permute-start | bytes 3145736 | tf_op jit(solution)/shard_map/ppermute | solution.py:35
  598.5 41.7 %collective-permute-start.67 = (f32[256,1024]{1,0:T(8,128)}, f32[256,1024]{1,0:T(8,128)}, u32[]{:S(2)}, u32[]{:S(2)}) collective-permute-start(f32[256,1024]{1,0:T(8,128)} %get-tuple-element.56), channel_id=1, source_target_pairs={{0,4},{1,5},{4,8},{5,9},{8,12},{9,13},{12,14},{13,15},{14,10},{15,... | collective-permute-start | bytes 3145736 | tf_op jit(solution)/shard_map/ppermute | solution.py:32
  599.2 41.1 %collective-permute-start.68 = (f32[256,1024]{1,0:T(8,128)S(1)}, f32[256,1024]{1,0:T(8,128)}, u32[]{:S(2)}, u32[]{:S(2)}) collective-permute-start(f32[256,1024]{1,0:T(8,128)S(1)} %get-tuple-element.57), channel_id=1, source_target_pairs={{0,2},{1,3},{4,0},{5,1},{8,4},{9,5},{12,8},{13,9},{14,12},{15,13},... | collective-permute-start | bytes 3145736 | tf_op jit(solution)/shard_map/ppermute | solution.py:35
  642.3 44.2 %collective-permute-start.74 = (f32[256,1024]{1,0:T(8,128)S(1)}, f32[256,1024]{1,0:T(8,128)S(1)}, u32[]{:S(2)}, u32[]{:S(2)}) collective-permute-start(f32[256,1024]{1,0:T(8,128)S(1)} %get-tuple-element.63), channel_id=1, source_target_pairs={{0,4},{1,5},{4,8},{5,9},{8,12},{9,13},{12,14},{13,15},{14,10},{15,... | collective-permute-start | bytes 3145736 | tf_op jit(solution)/shard_map/ppermute | solution.py:32
  643.0 43.5 %collective-permute-start.75 = (f32[256,1024]{1,0:T(8,128)S(1)}, f32[256,1024]{1,0:T(8,128)S(1)}, u32[]{:S(2)}, u32[]{:S(2)}) collective-permute-start(f32[256,1024]{1,0:T(8,128)S(1)} %get-tuple-element.64), channel_id=1, source_target_pairs={{0,2},{1,3},{4,0},{5,1},{8,4},{9,5},{12,8},{13,9},{14,12},{15,13},... | collective-permute-start | bytes 3145736 | tf_op jit(solution)/shard_map/ppermute | solution.py:35
  678.9 22.4 %collective-permute-start.72 = (f32[256,1024]{1,0:T(8,128)S(1)}, f32[256,1024]{1,0:T(8,128)S(1)}, u32[]{:S(2)}, u32[]{:S(2)}) collective-permute-start(f32[256,1024]{1,0:T(8,128)S(1)} %get-tuple-element.61), channel_id=1, source_target_pairs={{0,4},{1,5},{4,8},{5,9},{8,12},{9,13},{12,14},{13,15},{14,10},{15,... | collective-permute-start | bytes 3145736 | tf_op jit(solution)/shard_map/ppermute | solution.py:32
  680.2 21.8 %collective-permute-start.73 = (f32[256,1024]{1,0:T(8,128)S(1)}, f32[256,1024]{1,0:T(8,128)S(1)}, u32[]{:S(2)}, u32[]{:S(2)}) collective-permute-start(f32[256,1024]{1,0:T(8,128)S(1)} %get-tuple-element.62), channel_id=1, source_target_pairs={{0,2},{1,3},{4,0},{5,1},{8,4},{9,5},{12,8},{13,9},{14,12},{15,13},... | collective-permute-start | bytes 3145736 | tf_op jit(solution)/shard_map/ppermute | solution.py:35
  702.5 26.1 %collective-permute-start.79 = (f32[256,1024]{1,0:T(8,128)S(1)}, f32[256,1024]{1,0:T(8,128)S(1)}, u32[]{:S(2)}, u32[]{:S(2)}) collective-permute-start(f32[256,1024]{1,0:T(8,128)S(1)} %get-tuple-element.68), channel_id=1, source_target_pairs={{0,4},{1,5},{4,8},{5,9},{8,12},{9,13},{12,14},{13,15},{14,10},{15,... | collective-permute-start | bytes 3145736 | tf_op jit(solution)/shard_map/ppermute | solution.py:32
  704.7 24.5 %collective-permute-start.80 = (f32[256,1024]{1,0:T(8,128)S(1)}, f32[256,1024]{1,0:T(8,128)S(1)}, u32[]{:S(2)}, u32[]{:S(2)}) collective-permute-start(f32[256,1024]{1,0:T(8,128)S(1)} %get-tuple-element.69), channel_id=1, source_target_pairs={{0,2},{1,3},{4,0},{5,1},{8,4},{9,5},{12,8},{13,9},{14,12},{15,13},... | collective-permute-start | bytes 3145736 | tf_op jit(solution)/shard_map/ppermute | solution.py:35
  713.3 30.3 %collective-permute-start.77 = (f32[256,1024]{1,0:T(8,128)S(1)}, f32[256,1024]{1,0:T(8,128)S(1)}, u32[]{:S(2)}, u32[]{:S(2)}) collective-permute-start(f32[256,1024]{1,0:T(8,128)S(1)} %get-tuple-element.66), channel_id=1, source_target_pairs={{0,4},{1,5},{4,8},{5,9},{8,12},{9,13},{12,14},{13,15},{14,10},{15,... | collective-permute-start | bytes 3145736 | tf_op jit(solution)/shard_map/ppermute | solution.py:32
  713.7 30.5 %collective-permute-start.78 = (f32[256,1024]{1,0:T(8,128)S(1)}, f32[256,1024]{1,0:T(8,128)S(1)}, u32[]{:S(2)}, u32[]{:S(2)}) collective-permute-start(f32[256,1024]{1,0:T(8,128)S(1)} %get-tuple-element.67), channel_id=1, source_target_pairs={{0,2},{1,3},{4,0},{5,1},{8,4},{9,5},{12,8},{13,9},{14,12},{15,13},... | collective-permute-start | bytes 3145736 | tf_op jit(solution)/shard_map/ppermute | solution.py:35
  728.5 56.0 %collective-permute-start.89 = (bf16[256,2048]{1,0:T(8,128)(2,1)S(1)}, bf16[256,2048]{1,0:T(8,128)(2,1)S(1)}, u32[]{:S(2)}, u32[]{:S(2)}) collective-permute-start(bf16[256,2048]{1,0:T(8,128)(2,1)S(1)} %slice.719), channel_id=1, source_target_pairs={{0,1},{1,0},{4,5},{5,4},{8,9},{9,8},{12,13},{13,12},{14,15},{15,14... | collective-permute-start | bytes 3145736 | tf_op jit(solution)/shard_map/ppermute | solution.py:38
  728.6 52.6 %collective-permute-start.85 = (bf16[256,2048]{1,0:T(8,128)(2,1)S(1)}, bf16[256,2048]{1,0:T(8,128)(2,1)S(1)}, u32[]{:S(2)}, u32[]{:S(2)}) collective-permute-start(bf16[256,2048]{1,0:T(8,128)(2,1)S(1)} %slice.714), channel_id=1, source_target_pairs={{0,1},{1,0},{4,5},{5,4},{8,9},{9,8},{12,13},{13,12},{14,15},{15,14... | collective-permute-start | bytes 3145736 | tf_op jit(solution)/shard_map/ppermute | solution.py:38
  745.9 38.6 %collective-permute-start.87 = (f32[256,1024]{1,0:T(8,128)S(1)}, f32[256,1024]{1,0:T(8,128)S(1)}, u32[]{:S(2)}, u32[]{:S(2)}) collective-permute-start(f32[256,1024]{1,0:T(8,128)S(1)} %get-tuple-element.73), channel_id=1, source_target_pairs={{0,4},{1,5},{4,8},{5,9},{8,12},{9,13},{12,14},{13,15},{14,10},{15,... | collective-permute-start | bytes 3145736 | tf_op jit(solution)/shard_map/ppermute | solution.py:32
  747.7 36.8 %collective-permute-start.90 = (f32[256,1024]{1,0:T(8,128)S(1)}, f32[256,1024]{1,0:T(8,128)S(1)}, u32[]{:S(2)}, u32[]{:S(2)}) collective-permute-start(f32[256,1024]{1,0:T(8,128)S(1)} %get-tuple-element.74), channel_id=1, source_target_pairs={{0,2},{1,3},{4,0},{5,1},{8,4},{9,5},{12,8},{13,9},{14,12},{15,13},... | collective-permute-start | bytes 3145736 | tf_op jit(solution)/shard_map/ppermute | solution.py:35
  748.3 33.6 %collective-permute-start.91 = (f32[4,256]{1,0:T(4,128)S(1)}, f32[4,256]{1,0:T(4,128)S(1)}, u32[]{:S(2)}, u32[]{:S(2)}) collective-permute-start(f32[4,256]{1,0:T(4,128)S(1)} %add_add_fusion.24), channel_id=1, source_target_pairs={{0,4},{1,5},{4,8},{5,9},{8,12},{9,13},{12,14},{13,15},{14,10},{15,... | collective-permute-start | bytes 12296 | tf_op jit(solution)/shard_map/ppermute | solution.py:32
  (122 other events, 1829.0 us)

commit v4 on v2

--- a/solution.py
+++ b/solution.py
@@ -45,6 +45,7 @@
     def gather_rings(*owns):
         width = owns[0].shape[1] // 2
         got = [[own] + [None] * (ring - 1) for own in owns]
+
         for k in range(1, half):
             for blocks in got:
                 blocks[ring - k] = cw(blocks[(ring - k + 1) % ring])
@@ -89,15 +90,15 @@
 
         def y_term(r, side):
             cols = slice(side * width, (side + 1) * width)
-            return gate[r * 2][:, None] * y_of[r, 0][:, cols].astype(f32) + gate_mate[r * 2][:, None] * y_mate[r][:, cols].astype(f32)
+            return gate[r * 2][:, None] * y_of[r][:, cols].astype(f32) + gate_mate[r * 2][:, None] * y_mate[r][:, cols].astype(f32)
 
         def dx_term(r, side):
             cols = slice(side * width, (side + 1) * width)
-            return dx_of[r, 0][:, cols].astype(f32) + dx_mate[r][:, cols].astype(f32)
+            return dx_of[r][:, cols].astype(f32) + dx_mate[r][:, cols].astype(f32)
 
         def dot_term(r):
             dyf = dy_blk[r][0].astype(f32)
-            own = jnp.sum(dyf * y_of[r, 0].astype(f32), axis=1)
+            own = jnp.sum(dyf * y_of[r].astype(f32), axis=1)
             mate = jnp.sum(dyf * y_mate[r].astype(f32), axis=1)
             return jnp.where(ids[r * 2] == me, own[:, None], 0.0).T + jnp.where(ids[r * 2] == (me ^ 1), mate[:, None], 0.0).T
 
@@ -112,7 +113,7 @@
                 y_acc, dx_acc, dot_acc = lax.optimization_barrier((y_acc, dx_acc, dot_acc))
 
         for n, offs in enumerate(chunks):
-            names = [(r, k) for r in offs for k in range(2)]
+            names = [(r, k) for k in range(2) for r in offs]
             x = jnp.concatenate([x_blk[r][k] for r, k in names])
             dy = jnp.concatenate([dy_blk[r][k] for r, k in names])
             pick = lambda v: jnp.concatenate([v[r * 2 + k] for r, k in names])[:, None]
@@ -128,11 +129,12 @@
             dg = (q * b * s * (1.0 + a * (1.0 - s))).astype(bf16)
             dx = (lax.dot_general(dg, w_gate, nt, preferred_element_type=f32) + lax.dot_general(du, w_up, nt, preferred_element_type=f32)).astype(bf16)
             saved.append((h, u, dg, du))
-            for i, (r, k) in enumerate(names):
+            split = len(offs) * tok_dev
+            o_mate, dxs_mate = swap(o[split:]), swap(dx[split:])
+            for i, r in enumerate(offs):
                 rows = slice(i * tok_dev, (i + 1) * tok_dev)
-                y_of[r, k], dx_of[r, k] = o[rows], dx[rows]
-            for r in offs:
-                y_mate[r], dx_mate[r] = swap(y_of[r, 1]), swap(dx_of[r, 1])
+                y_of[r], dx_of[r] = o[rows], dx[rows]
+                y_mate[r], dx_mate[r] = o_mate[rows], dxs_mate[rows]
             if n >= 1:
                 advance(n - 1)
 
@@ -142,7 +144,7 @@
         grad_tokens = jnp.concatenate(dx_acc, axis=1).astype(bf16)
         grad_gates = dot_acc.T
 
-        x_cat = jnp.concatenate([x_blk[r][k] for offs in chunks for r in offs for k in range(2)])
+        x_cat = jnp.concatenate([x_blk[r][k] for offs in chunks for k in range(2) for r in offs])
         h, u, dg, du = (jnp.concatenate(v) for v in zip(*saved))
         gwg = lax.dot_general(x_cat, dg, tn, preferred_element_type=f32).astype(bf16)
         gwu = lax.dot_general(x_cat, du, tn, preferred_element_type=f32).astype(bf16)

time: 802 us -> 769 us (0.959)
  waiting for transfers between devices: 197 us -> 146 us
  other arithmetic: 65.5 us -> 80.5 us
    ppermute x29, waiting for transfers between devices: 159 us -> 129 us  [cw(): return lax.ppermute(v, axes, cw_perm)]
    ppermute x22, waiting for transfers between devices: 38.2 us -> 17.2 us  [ccw(): return lax.ppermute(v, axes, ccw_perm)]
    add x12, other arithmetic: 20 us -> 29.3 us  [scatter_step(): return (left + term(ring - 1 - s, 0), right + term((1 + s) % ring, 1))]
    unnamed x277 -> x205, local copies, waits for them, and re-layouts: 28 us -> 30.7 us
  transfers between devices with their start and end apart: 83 -> 77, of which waited for: 25 -> 21; matrix products, arithmetic and copies ran while one was open for 64% -> 68% of each run, Pallas kernels for 0% -> 0%
where the time goes in v4:
time: 769 us; the launch traced here: 759 us
  matrix products  398 us (52%)
  waiting for transfers between devices  146 us (19%)
  other arithmetic  80.5 us (10%)
  starting transfers between devices  58.9 us (8%)
  local copies, waits for them, and re-layouts  49.4 us (6%)
  blocking collectives  23.6 us (3%)
    ppermute x29, waiting for transfers between devices, cw(): return lax.ppermute(v, axes, cw_perm)  129 us
    dot_general x5, matrix products, device_step(): a = jnp.where(on, jnp.dot(x, w_gate, preferred_element_type=f32), 0.0)  75.5 us
    dot_general x5, matrix products, device_step(): q = lax.dot_general(u, w_down, nt, preferred_element_type=f32)  54.8 us
    dot_general x5, matrix products, device_step(): lax.dot_general(du, w_up, nt, preferred_element_type=f32)  46.8 us
    dot_general x5, matrix products, device_step(): lax.dot_general(dg, w_gate, nt, preferred_element_type=f32)  44.4 us
    dot_general x5, matrix products, device_step(): o = jnp.dot(h, w_down, preferred_element_type=f32).astype(bf16)  41.2 us
    dot_general x5, matrix products, device_step(): b = jnp.where(on, jnp.dot(x, w_up, preferred_element_type=f32), 0.0)  36.5 us
    dot_general x1, matrix products, device_step(): lax.dot_general(x_cat, du, tn, preferred_element_type=f32).astype(bf16)  33.7 us
  transfers between devices with their start and end apart: 77, of which 21 were waited for; matrix products, arithmetic and copies ran while one was open for 68% of the time, Pallas kernels for 0%

profile of v4, /device:TPU:0, one launch (start us, length us, event | category | flops | bytes accessed | tf_op | source)
XLA Modules:
  0.0 758.7 jit_solution(2381068340697985589)
XLA Ops:
  2.2 23.6 %all_gather.3 = f32[4096,8]{0,1:T(8,128)S(1)} all-gather(f32[256,8]{0,1:T(8,128)S(1)} %pad_maximum_fusion.5), channel_id=1, replica_groups=mesh['dp'=2,'ei'=4,'eo'=4] {'ei','eo'}, dimensions={0}, use_global_device_ids=true | all-gather | bytes 139264 | tf_op jit(solution)/shard_map/all_gather | solution.py:74
  37.7 2.6 constant_dynamic-update-slice_fusion.32
  40.3 5.0 fusion.81
  45.4 6.2 fusion.3
  51.6 7.5 constant_dynamic-update-slice_fusion.38
  59.0 6.2 fusion.97
  65.3 3.5 fusion.23
  69.8 3.7 add_convert_fusion.3
  75.3 2.5 constant_dynamic-update-slice_fusion.31
  77.8 2.5 constant_dynamic-update-slice_fusion.30
  80.3 2.9 constant_dynamic-update-slice_fusion.53
  88.3 8.4 %fusion.41 = f32[1024,1408]{1,0:T(8,128)} fusion(bf16[1024,2048]{1,0:T(8,128)(2,1)S(1)} %get-tuple-element.222, bf16[1,2048,1408]{2,1,0:T(8,128)(2,1)S(1)} %copy-done.75), kind=kOutput, calls=%fused_computation.51 | convolution fusion | flops 5905580032 | bytes 15728640 | tf_op jit(solution)/shard_map/dot_general | solution.py:122
  98.5 11.6 %fusion.19 = f32[1024,1408]{1,0:T(8,128)} fusion(bf16[1,1408,2048]{2,1,0:T(8,128)(2,1)S(1)} %bitcast.273, bf16[256,2048]{1,0:T(8,128)(2,1)S(1)} %collective-permute-done.8, bf16[256,2048]{1,0:T(8,128)(2,1)S(1)} %collective-permute-done.7, bf16[256,2048]{1,0:T(8,128)(2,1)S(1)} %collective-permute-done.6, bf16[256,2048]{1,0:T(8,128)(2,1)S(1)} %collective-permute-done.5, ...), kind=kOutput, calls=%fused_computation.29 | convolution fusion | flops 5926551552 | bytes 15732736 | tf_op jit(solution)/shard_map/dot_general | solution.py:127
  110.1 18.5 %constant_dynamic-update-slice_fusion.37 = (bf16[4096,1408]{1,0:T(8,128)(2,1)}, bf16[1024,1408]{1,0:T(8,128)(2,1)}, bf16[4096,1408]{1,0:T(8,128)(2,1)}, bf16[102...) fusion(bf16[4096,1408]{1,0:T(8,128)(2,1)} %get-tuple-element.150, ...), kind=kOutput, calls=%fused_computation.210 | convolution fusion | flops 5931532288 | bytes 38798336 | tf_op jit(solution)/shard_map/dot_general | solution.py:121
  128.6 9.7 %fusion.63 = bf16[1024,2048]{1,0:T(8,128)(2,1)S(1)} fusion(bf16[1024,1408]{1,0:T(8,128)(2,1)} %get-tuple-element.162, bf16[1,1408,2048]{2,1,0:T(8,128)(2,1)} %param.13), kind=kOutput, calls=%fused_computation.89 | convolution fusion | flops 5907677184 | bytes 12845056 | tf_op jit(solution)/shard_map/dot_general | solution.py:125
  142.9 11.2 %fusion.39 = f32[1024,2048]{1,0:T(8,128)} fusion(bf16[1024,1408]{1,0:T(8,128)(2,1)S(1)} %copy-done.77, bf16[1,2048,1408]{2,1,0:T(8,128)(2,1)} %param.12), kind=kOutput, calls=%fused_computation.49 | convolution fusion | flops 5905580032 | bytes 17039360 | tf_op jit(solution)/shard_map/dot_general | solution.py:130
  154.2 10.0 %add_convert_fusion.2 = bf16[1024,2048]{1,0:T(8,128)(2,1)S(1)} fusion(f32[1024,2048]{1,0:T(8,128)} %fusion.39, bf16[1024,1408]{1,0:T(8,128)(2,1)} %get-tuple-element.149, bf16[1,2048,1408]{2,1,0:T(8,128)(2,1)S(1)} %bitcast.271), kind=kOutput, calls=%fused_computation.5 | convolution fusion | flops 5909774336 | bytes 21233664 | tf_op jit(solution)/shard_map/dot_general | solution.py:130
  173.3 8.5 %fusion.37 = f32[1024,1408]{1,0:T(8,128)} fusion(bf16[1024,2048]{1,0:T(8,128)(2,1)S(1)} %get-tuple-element.214, bf16[1,2048,1408]{2,1,0:T(8,128)(2,1)S(1)} %bitcast.263), kind=kOutput, calls=%fused_computation.47 | convolution fusion | flops 5905580032 | bytes 15728640 | tf_op jit(solution)/shard_map/dot_general | solution.py:122
  181.7 12.2 %collective-permute-done.33 = bf16[256,2048]{1,0:T(8,128)(2,1)S(1)} collective-permute-done((bf16[256,2048]{1,0:T(8,128)(2,1)S(1)}, bf16[256,2048]{1,0:T(8,128)(2,1)S(1)}, u32[]{:S(2)}, u32[]{:S(2)}) %collective-permute-start.33) | collective-permute-done | bytes 1048608 | tf_op jit(solution)/shard_map/ppermute | solution.py:37
  200.6 14.4 %fusion.15 = f32[1024,1408]{1,0:T(8,128)} fusion(bf16[1,1408,2048]{2,1,0:T(8,128)(2,1)} %param.13, bf16[256,2048]{1,0:T(8,128)(2,1)S(1)} %collective-permute-done.21, bf16[256,2048]{1,0:T(8,128)(2,1)S(1)} %collective-permute-done.20, bf16[256,2048]{1,0:T(8,128)(2,1)S(1)} %collective-permute-done.19, bf16[256,2048]{1,0:T(8,128)(2,1)S(1)} %collective-permute-done.18, ...), kind=kOutput, calls=%fused_computation.25 | convolution fusion | flops 5926551552 | bytes 15732736 | tf_op jit(solution)/shard_map/dot_general | solution.py:127
  215.0 18.1 %constant_dynamic-update-slice_fusion.36 = (bf16[4096,1408]{1,0:T(8,128)(2,1)}, bf16[1024,1408]{1,0:T(8,128)(2,1)}, bf16[4096,1408]{1,0:T(8,128)(2,1)}, bf16[102...) fusion(bf16[4096,1408]{1,0:T(8,128)(2,1)} %get-tuple-element.148, ...), kind=kOutput, calls=%fused_computation.209 | convolution fusion | flops 5931532288 | bytes 38798336 | tf_op jit(solution)/shard_map/dot_general | solution.py:121
  233.1 11.8 %fusion.35 = f32[1024,2048]{1,0:T(8,128)} fusion(bf16[1024,1408]{1,0:T(8,128)(2,1)} %get-tuple-element.160, bf16[1,2048,1408]{2,1,0:T(8,128)(2,1)} %param.12), kind=kOutput, calls=%fused_computation.45 | convolution fusion | flops 5905580032 | bytes 17039360 | tf_op jit(solution)/shard_map/dot_general | solution.py:130
  244.9 10.8 %add_convert_fusion.1 = bf16[1024,2048]{1,0:T(8,128)(2,1)S(1)} fusion(f32[1024,2048]{1,0:T(8,128)} %fusion.35, bf16[1024,1408]{1,0:T(8,128)(2,1)S(1)} %copy-done.78, bf16[1,2048,1408]{2,1,0:T(8,128)(2,1)} %param.11), kind=kOutput, calls=%fused_computation.3 | convolution fusion | flops 5909774336 | bytes 21233664 | tf_op jit(solution)/shard_map/dot_general | solution.py:130
  255.9 7.3 fusion.66
  277.0 8.4 %fusion.33 = f32[1024,1408]{1,0:T(8,128)} fusion(bf16[1024,2048]{1,0:T(8,128)(2,1)S(1)} %get-tuple-element.206, bf16[1,2048,1408]{2,1,0:T(8,128)(2,1)S(1)} %bitcast.265), kind=kOutput, calls=%fused_computation.43 | convolution fusion | flops 5905580032 | bytes 15728640 | tf_op jit(solution)/shard_map/dot_general | solution.py:122
  287.1 14.6 %fusion.11 = f32[1024,1408]{1,0:T(8,128)} fusion(bf16[1,1408,2048]{2,1,0:T(8,128)(2,1)} %param.13, bf16[256,2048]{1,0:T(8,128)(2,1)S(1)} %collective-permute-done.36, bf16[256,2048]{1,0:T(8,128)(2,1)S(1)} %collective-permute-done.35, bf16[256,2048]{1,0:T(8,128)(2,1)S(1)} %collective-permute-done.34, bf16[256,2048]{1,0:T(8,128)(2,1)S(1)} %collective-permute-done.33, ...), kind=kOutput, calls=%fused_computation.21 | convolution fusion | flops 5926551552 | bytes 15732736 | tf_op jit(solution)/shard_map/dot_general | solution.py:127
  301.7 18.5 %constant_dynamic-update-slice_fusion.35 = (bf16[4096,1408]{1,0:T(8,128)(2,1)}, bf16[1024,1408]{1,0:T(8,128)(2,1)}, bf16[4096,1408]{1,0:T(8,128)(2,1)}, bf16[102...) fusion(bf16[4096,1408]{1,0:T(8,128)(2,1)} %get-tuple-element.146, ...), kind=kOutput, calls=%fused_computation.208 | convolution fusion | flops 5931532288 | bytes 38798336 | tf_op jit(solution)/shard_map/dot_general | solution.py:121
  320.2 11.8 %fusion.31 = f32[1024,2048]{1,0:T(8,128)} fusion(bf16[1024,1408]{1,0:T(8,128)(2,1)} %get-tuple-element.156, bf16[1,2048,1408]{2,1,0:T(8,128)(2,1)} %param.12), kind=kOutput, calls=%fused_computation.41 | convolution fusion | flops 5905580032 | bytes 17039360 | tf_op jit(solution)/shard_map/dot_general | solution.py:130
  332.0 10.7 %add_convert_fusion = bf16[1024,2048]{1,0:T(8,128)(2,1)S(1)} fusion(f32[1024,2048]{1,0:T(8,128)} %fusion.31, bf16[1024,1408]{1,0:T(8,128)(2,1)S(1)} %copy-done.79, bf16[1,2048,1408]{2,1,0:T(8,128)(2,1)} %param.11), kind=kOutput, calls=%fused_computation.1 | convolution fusion | flops 5909774336 | bytes 21233664 | tf_op jit(solution)/shard_map/dot_general | solution.py:130
  342.8 11.4 %fusion.69 = bf16[1024,2048]{1,0:T(8,128)(2,1)S(1)} fusion(bf16[1024,1408]{1,0:T(8,128)(2,1)} %get-tuple-element.154, bf16[1,1408,2048]{2,1,0:T(8,128)(2,1)} %param.13), kind=kOutput, calls=%fused_computation.91 | convolution fusion | flops 5907677184 | bytes 12845056 | tf_op jit(solution)/shard_map/dot_general | solution.py:125
  354.4 2.8 fusion.113
  357.7 3.3 convert_add_fusion
  362.6 2.5 multiply_add_fusion
  365.5 2.2 constant_dynamic-update-slice_fusion.19
  368.0 2.2 constant_dynamic-update-slice_fusion.54
  375.6 8.0 %fusion.7 = f32[512,1408]{1,0:T(8,128)} fusion(bf16[1,1408,2048]{2,1,0:T(8,128)(2,1)} %param.13, bf16[256,2048]{1,0:T(8,128)(2,1)} %collective-permute-done.49, bf16[256,2048]{1,0:T(8,128)(2,1)S(1)} %constant_dynamic-update-slice_fusion.14, f32[512]{0:T(512)S(1)} %copy-done.70), kind=kOutput, calls=%fused_computation.17 | convolution fusion | flops 2959081472 | bytes 10749952 | tf_op jit(solution)/shard_map/dot_general | solution.py:127
  385.0 9.1 %collective-permute-done.17 = f32[256,1024]{1,0:T(8,128)} collective-permute-done((f32[256,1024]{1,0:T(8,128)}, f32[256,1024]{1,0:T(8,128)}, u32[]{:S(2)}, u32[]{:S(2)}) %collective-permute-start.17) | collective-permute-done | bytes 1048608 | tf_op jit(solution)/shard_map/ppermute | solution.py:37
  394.1 4.1 collective-permute-done.23
  398.1 4.1 add_add_fusion.20
  402.2 13.1 %collective-permute-done.10 = f32[256,1024]{1,0:T(8,128)} collective-permute-done((f32[256,1024]{1,0:T(8,128)}, f32[256,1024]{1,0:T(8,128)}, u32[]{:S(2)}, u32[]{:S(2)}) %collective-permute-start.10) | collective-permute-done | bytes 1048608 | tf_op jit(solution)/shard_map/ppermute | solution.py:37
  415.4 3.8 collective-permute-done.16
  419.2 3.3 add_add_fusion.22
  425.1 6.2 fusion.78
  431.3 12.9 %constant_dynamic-update-slice_fusion.34 = (bf16[4096,1408]{1,0:T(8,128)(2,1)}, bf16[512,1408]{1,0:T(8,128)(2,1)}, bf16[4096,1408]{1,0:T(8,128)(2,1)}, bf16[512,...) fusion(bf16[4096,1408]{1,0:T(8,128)(2,1)} %get-tuple-element.144, ...), kind=kOutput, calls=%fused_computation.207 | convolution fusion | flops 2969239552 | bytes 22282752 | tf_op jit(solution)/shard_map/dot_general | solution.py:121
  444.2 8.5 %fusion.27 = f32[512,2048]{1,0:T(8,128)} fusion(bf16[512,1408]{1,0:T(8,128)(2,1)} %get-tuple-element.192, bf16[1,2048,1408]{2,1,0:T(8,128)(2,1)} %param.12), kind=kOutput, calls=%fused_computation.37 | convolution fusion | flops 2952790016 | bytes 11403264 | tf_op jit(solution)/shard_map/dot_general | solution.py:130
  452.8 9.1 %add_convert_fusion.4 = bf16[512,2048]{1,0:T(8,128)(2,1)} fusion(f32[512,2048]{1,0:T(8,128)} %fusion.27, bf16[512,1408]{1,0:T(8,128)(2,1)} %get-tuple-element.143, bf16[1,2048,1408]{2,1,0:T(8,128)(2,1)} %param.11), kind=kOutput, calls=%fused_computation.87 | convolution fusion | flops 2954887168 | bytes 13500416 | tf_op jit(solution)/shard_map/dot_general | solution.py:130
  464.2 6.6 fusion.94
  473.2 3.8 add_add_fusion.16
  476.9 8.3 %collective-permute-done.25 = f32[256,1024]{1,0:T(8,128)S(1)} collective-permute-done((f32[256,1024]{1,0:T(8,128)}, f32[256,1024]{1,0:T(8,128)S(1)}, u32[]{:S(2)}, u32[]{:S(2)}) %collective-permute-start.25) | collective-permute-done | bytes 1048608 | tf_op jit(solution)/shard_map/ppermute | solution.py:37
  494.1 7.2 constant_dynamic-update-slice_fusion.52
  502.1 13.3 %collective-permute-done.46 = f32[256,1024]{1,0:T(8,128)} collective-permute-done((f32[256,1024]{1,0:T(8,128)}, f32[256,1024]{1,0:T(8,128)}, u32[]{:S(2)}, u32[]{:S(2)}) %collective-permute-start.46) | collective-permute-done | bytes 1048608 | tf_op jit(solution)/shard_map/ppermute | solution.py:37
  517.1 3.1 add_add_fusion.12
  520.2 13.4 %collective-permute-done.40 = f32[256,1024]{1,0:T(8,128)} collective-permute-done((f32[256,1024]{1,0:T(8,128)}, f32[256,1024]{1,0:T(8,128)}, u32[]{:S(2)}, u32[]{:S(2)}) %collective-permute-start.40) | collective-permute-done | bytes 1048608 | tf_op jit(solution)/shard_map/ppermute | solution.py:37
  534.9 3.4 add_add_fusion.14
  544.9 7.1 constant_dynamic-update-slice_fusion.51
  552.0 12.5 %collective-permute-done.57 = f32[4,256]{1,0:T(4,128)S(1)} collective-permute-done((f32[4,256]{1,0:T(4,128)S(1)}, f32[4,256]{1,0:T(4,128)S(1)}, u32[]{:S(2)}, u32[]{:S(2)}) %collective-permute-start.57) | collective-permute-done | bytes 4128 | tf_op jit(solution)/shard_map/ppermute | solution.py:37
  567.8 13.8 %collective-permute-done.53 = f32[256,1024]{1,0:T(8,128)S(1)} collective-permute-done((f32[256,1024]{1,0:T(8,128)}, f32[256,1024]{1,0:T(8,128)S(1)}, u32[]{:S(2)}, u32[]{:S(2)}) %collective-permute-start.53) | collective-permute-done | bytes 1048608 | tf_op jit(solution)/shard_map/ppermute | solution.py:37
  587.0 8.2 %constant_dynamic-update-slice_fusion.50 = bf16[4096,2048]{1,0:T(8,128)(2,1)} fusion(bf16[4096,2048]{1,0:T(8,128)(2,1)} %constant_dynamic-update-slice_fusion.51, bf16[256,2048]{1,0:T(8,128)(2,1)S(1)} %copy-done.38, bf16[256,2048]{1,0:T(8,128)(2,1)S(1)} %copy-done.36, bf16[256,2048]{1,0:T(8,128)(2,1)S(1)} %collective-permute-done.34, ...), kind=kLoop, calls=%fused_computation.223 | loop fusion | flops 20971520 | bytes 8392704
  597.2 3.0 constant_dynamic-update-slice_fusion.49
  603.0 23.7 %collective-permute-done.62 = f32[4,256]{1,0:T(4,128)S(1)} collective-permute-done((f32[4,256]{1,0:T(4,128)S(1)}, f32[4,256]{1,0:T(4,128)S(1)}, u32[]{:S(2)}, u32[]{:S(2)}) %collective-permute-start.62) | collective-permute-done | bytes 4128 | tf_op jit(solution)/shard_map/ppermute | solution.py:37
  635.3 33.7 %fusion.2 = bf16[1,2048,1408]{2,1,0:T(8,128)(2,1)} fusion(bf16[4096,2048]{1,0:T(8,128)(2,1)} %constant_dynamic-update-slice_fusion.18, bf16[4096,1408]{1,0:T(8,128)(2,1)} %get-tuple-element.191), kind=kOutput, calls=%fused_computation.12 | convolution fusion | flops 23625203712 | bytes 34078720 | tf_op jit(solution)/shard_map/dot_general | solution.py:150
  675.6 33.6 %fusion.1 = bf16[1,2048,1408]{2,1,0:T(8,128)(2,1)} fusion(bf16[4096,2048]{1,0:T(8,128)(2,1)} %constant_dynamic-update-slice_fusion.18, bf16[4096,1408]{1,0:T(8,128)(2,1)} %get-tuple-element.142), kind=kOutput, calls=%fused_computation.11 | convolution fusion | flops 23625203712 | bytes 34078720 | tf_op jit(solution)/shard_map/dot_general | solution.py:149
  713.5 31.5 %fusion = bf16[1,1408,2048]{2,1,0:T(8,128)(2,1)} fusion(bf16[4096,1408]{1,0:T(8,128)(2,1)} %get-tuple-element.189, bf16[4096,2048]{1,0:T(8,128)(2,1)} %constant_dynamic-update-slice_fusion.49), kind=kOutput, calls=%fused_computation.10 | convolution fusion | flops 23625203712 | bytes 34078720 | tf_op jit(solution)/shard_map/dot_general | solution.py:151
  747.2 8.8 %collective-permute-done.68 = f32[256,1024]{1,0:T(8,128)S(1)} collective-permute-done((f32[256,1024]{1,0:T(8,128)S(1)}, f32[256,1024]{1,0:T(8,128)S(1)}, u32[]{:S(2)}, u32[]{:S(2)}) %collective-permute-start.68) | collective-permute-done | bytes 1048608 | tf_op jit(solution)/shard_map/ppermute | solution.py:37
  (408 shorter events, 132.0 us)
Async XLA Ops:
  26.1 48.7 %collective-permute-start = (bf16[256,2048]{1,0:T(8,128)(2,1)}, bf16[256,2048]{1,0:T(8,128)(2,1)}, u32[]{:S(2)}, u32[]{:S(2)}) collective-permute-start(bf16[256,2048]{1,0:T(8,128)(2,1)} %param.8), channel_id=1, source_target_pairs={{0,4},{1,5},{4,8},{5,9},{8,12},{9,13},{12,14},{13,15},{14,10},{15,... | collective-permute-start | bytes 3145736 | tf_op jit(solution)/shard_map/ppermute | solution.py:37
  26.1 48.9 %collective-permute-start.1 = (bf16[256,2048]{1,0:T(8,128)(2,1)}, bf16[256,2048]{1,0:T(8,128)(2,1)}, u32[]{:S(2)}, u32[]{:S(2)}) collective-permute-start(bf16[256,2048]{1,0:T(8,128)(2,1)} %param.8), channel_id=1, source_target_pairs={{0,2},{1,3},{4,0},{5,1},{8,4},{9,5},{12,8},{13,9},{14,12},{15,13},... | collective-permute-start | bytes 3145736 | tf_op jit(solution)/shard_map/ppermute | solution.py:40
  28.1 55.1 %collective-permute-start.5 = (bf16[256,2048]{1,0:T(8,128)(2,1)}, bf16[256,2048]{1,0:T(8,128)(2,1)S(1)}, u32[]{:S(2)}, u32[]{:S(2)}) collective-permute-start(bf16[256,2048]{1,0:T(8,128)(2,1)} %param.14), channel_id=1, source_target_pairs={{0,4},{1,5},{4,8},{5,9},{8,12},{9,13},{12,14},{13,15},{14,10},{15,... | collective-permute-start | bytes 3145736 | tf_op jit(solution)/shard_map/ppermute | solution.py:37
  35.7 50.5 %collective-permute-start.6 = (bf16[256,2048]{1,0:T(8,128)(2,1)S(1)}, bf16[256,2048]{1,0:T(8,128)(2,1)S(1)}, u32[]{:S(2)}, u32[]{:S(2)}) collective-permute-start(bf16[256,2048]{1,0:T(8,128)(2,1)S(1)} %copy-done.8), channel_id=1, source_target_pairs={{0,2},{1,3},{4,0},{5,1},{8,4},{9,5},{12,8},{13,9},{14,12},{15,13},... | collective-permute-start | bytes 3145736 | tf_op jit(solution)/shard_map/ppermute | solution.py:40
  74.8 67.2 %collective-permute-start.11 = (bf16[256,2048]{1,0:T(8,128)(2,1)}, bf16[256,2048]{1,0:T(8,128)(2,1)S(1)}, u32[]{:S(2)}, u32[]{:S(2)}) collective-permute-start(bf16[256,2048]{1,0:T(8,128)(2,1)} %collective-permute-done), channel_id=1, source_target_pairs={{0,4},{1,5},{4,8},{5,9},{8,12},{9,13},{12,14},{13,15},{14,10},{15,... | collective-permute-start | bytes 3145736 | tf_op jit(solution)/shard_map/ppermute | solution.py:37
  83.2 71.0 %collective-permute-start.12 = (bf16[256,2048]{1,0:T(8,128)(2,1)}, bf16[256,2048]{1,0:T(8,128)(2,1)S(1)}, u32[]{:S(2)}, u32[]{:S(2)}) collective-permute-start(bf16[256,2048]{1,0:T(8,128)(2,1)} %collective-permute-done.1), channel_id=1, source_target_pairs={{0,2},{1,3},{4,0},{5,1},{8,4},{9,5},{12,8},{13,9},{14,12},{15,13},... | collective-permute-start | bytes 3145736 | tf_op jit(solution)/shard_map/ppermute | solution.py:40
  86.2 79.6 %collective-permute-start.18 = (bf16[256,2048]{1,0:T(8,128)(2,1)S(1)}, bf16[256,2048]{1,0:T(8,128)(2,1)S(1)}, u32[]{:S(2)}, u32[]{:S(2)}) collective-permute-start(bf16[256,2048]{1,0:T(8,128)(2,1)S(1)} %collective-permute-done.5), channel_id=1, source_target_pairs={{0,4},{1,5},{4,8},{5,9},{8,12},{9,13},{12,14},{13,15},{14,10},{15,... | collective-permute-start | bytes 3145736 | tf_op jit(solution)/shard_map/ppermute | solution.py:37
  96.7 72.1 %collective-permute-start.19 = (bf16[256,2048]{1,0:T(8,128)(2,1)S(1)}, bf16[256,2048]{1,0:T(8,128)(2,1)S(1)}, u32[]{:S(2)}, u32[]{:S(2)}) collective-permute-start(bf16[256,2048]{1,0:T(8,128)(2,1)S(1)} %collective-permute-done.6), channel_id=1, source_target_pairs={{0,2},{1,3},{4,0},{5,1},{8,4},{9,5},{12,8},{13,9},{14,12},{15,13},... | collective-permute-start | bytes 3145736 | tf_op jit(solution)/shard_map/ppermute | solution.py:40
  141.9 212.2 %collective-permute-start.4 = (bf16[512,2048]{1,0:T(8,128)(2,1)}, bf16[512,2048]{1,0:T(8,128)(2,1)}, u32[]{:S(2)}, u32[]{:S(2)}) collective-permute-start(bf16[512,2048]{1,0:T(8,128)(2,1)} %slice.681), channel_id=1, source_target_pairs={{0,1},{1,0},{4,5},{5,4},{8,9},{9,8},{12,13},{13,12},{14,15},{15,14... | collective-permute-start | bytes 6291464 | tf_op jit(solution)/shard_map/ppermute | solution.py:43
  142.0 27.3 %collective-permute-start.13 = (bf16[256,2048]{1,0:T(8,128)(2,1)S(1)}, bf16[256,2048]{1,0:T(8,128)(2,1)S(1)}, u32[]{:S(2)}, u32[]{:S(2)}) collective-permute-start(bf16[256,2048]{1,0:T(8,128)(2,1)S(1)} %collective-permute-done.11), channel_id=1, source_target_pairs={{0,1},{1,0},{4,5},{5,4},{8,9},{9,8},{12,13},{13,12},{14,15},{15,14... | collective-permute-start | bytes 3145736 | tf_op jit(solution)/shard_map/ppermute | solution.py:43
  165.8 32.7 %collective-permute-start.20 = (bf16[256,2048]{1,0:T(8,128)(2,1)S(1)}, bf16[256,2048]{1,0:T(8,128)(2,1)S(1)}, u32[]{:S(2)}, u32[]{:S(2)}) collective-permute-start(bf16[256,2048]{1,0:T(8,128)(2,1)S(1)} %collective-permute-done.18), channel_id=1, source_target_pairs={{0,1},{1,0},{4,5},{5,4},{8,9},{9,8},{12,13},{13,12},{14,15},{15,14... | collective-permute-start | bytes 3145736 | tf_op jit(solution)/shard_map/ppermute | solution.py:43
  168.8 25.1 %collective-permute-start.33 = (bf16[256,2048]{1,0:T(8,128)(2,1)S(1)}, bf16[256,2048]{1,0:T(8,128)(2,1)S(1)}, u32[]{:S(2)}, u32[]{:S(2)}) collective-permute-start(bf16[256,2048]{1,0:T(8,128)(2,1)S(1)} %collective-permute-done.18), channel_id=1, source_target_pairs={{0,4},{1,5},{4,8},{5,9},{8,12},{9,13},{12,14},{13,15},{14,10},{15,... | collective-permute-start | bytes 3145736 | tf_op jit(solution)/shard_map/ppermute | solution.py:37
  169.2 29.7 %collective-permute-start.21 = (bf16[256,2048]{1,0:T(8,128)(2,1)S(1)}, bf16[256,2048]{1,0:T(8,128)(2,1)S(1)}, u32[]{:S(2)}, u32[]{:S(2)}) collective-permute-start(bf16[256,2048]{1,0:T(8,128)(2,1)S(1)} %collective-permute-done.19), channel_id=1, source_target_pairs={{0,1},{1,0},{4,5},{5,4},{8,9},{9,8},{12,13},{13,12},{14,15},{15,14... | collective-permute-start | bytes 3145736 | tf_op jit(solution)/shard_map/ppermute | solution.py:43
  170.4 25.6 %collective-permute-start.34 = (bf16[256,2048]{1,0:T(8,128)(2,1)S(1)}, bf16[256,2048]{1,0:T(8,128)(2,1)S(1)}, u32[]{:S(2)}, u32[]{:S(2)}) collective-permute-start(bf16[256,2048]{1,0:T(8,128)(2,1)S(1)} %collective-permute-done.19), channel_id=1, source_target_pairs={{0,2},{1,3},{4,0},{5,1},{8,4},{9,5},{12,8},{13,9},{14,12},{15,13},... | collective-permute-start | bytes 3145736 | tf_op jit(solution)/shard_map/ppermute | solution.py:40
  193.9 61.8 %collective-permute-start.26 = (bf16[256,2048]{1,0:T(8,128)(2,1)S(1)}, bf16[256,2048]{1,0:T(8,128)(2,1)S(1)}, u32[]{:S(2)}, u32[]{:S(2)}) collective-permute-start(bf16[256,2048]{1,0:T(8,128)(2,1)S(1)} %collective-permute-done.11), channel_id=1, source_target_pairs={{0,4},{1,5},{4,8},{5,9},{8,12},{9,13},{12,14},{13,15},{14,10},{15,... | collective-permute-start | bytes 3145736 | tf_op jit(solution)/shard_map/ppermute | solution.py:37
  196.0 67.2 %collective-permute-start.27 = (bf16[256,2048]{1,0:T(8,128)(2,1)S(1)}, bf16[256,2048]{1,0:T(8,128)(2,1)S(1)}, u32[]{:S(2)}, u32[]{:S(2)}) collective-permute-start(bf16[256,2048]{1,0:T(8,128)(2,1)S(1)} %collective-permute-done.12), channel_id=1, source_target_pairs={{0,2},{1,3},{4,0},{5,1},{8,4},{9,5},{12,8},{13,9},{14,12},{15,13},... | collective-permute-start | bytes 3145736 | tf_op jit(solution)/shard_map/ppermute | solution.py:40
  198.5 72.6 %collective-permute-start.47 = (bf16[256,1024]{1,0:T(8,128)(2,1)}, bf16[256,1024]{1,0:T(8,128)(2,1)}, u32[]{:S(2)}, u32[]{:S(2)}) collective-permute-start(bf16[256,1024]{1,0:T(8,128)(2,1)} %slice.755), channel_id=1, source_target_pairs={{0,4},{1,5},{4,8},{5,9},{8,12},{9,13},{12,14},{13,15},{14,10},{15,... | collective-permute-start | bytes 1572872 | tf_op jit(solution)/shard_map/ppermute | solution.py:37
  198.9 73.4 %collective-permute-start.48 = (bf16[256,1024]{1,0:T(8,128)(2,1)}, bf16[256,1024]{1,0:T(8,128)(2,1)}, u32[]{:S(2)}, u32[]{:S(2)}) collective-permute-start(bf16[256,1024]{1,0:T(8,128)(2,1)} %slice.756), channel_id=1, source_target_pairs={{0,2},{1,3},{4,0},{5,1},{8,4},{9,5},{12,8},{13,9},{14,12},{15,13},... | collective-permute-start | bytes 1572872 | tf_op jit(solution)/shard_map/ppermute | solution.py:40
  255.8 18.1 %collective-permute-start.28 = (bf16[256,2048]{1,0:T(8,128)(2,1)S(1)}, bf16[256,2048]{1,0:T(8,128)(2,1)S(1)}, u32[]{:S(2)}, u32[]{:S(2)}) collective-permute-start(bf16[256,2048]{1,0:T(8,128)(2,1)S(1)} %collective-permute-done.26), channel_id=1, source_target_pairs={{0,1},{1,0},{4,5},{5,4},{8,9},{9,8},{12,13},{13,12},{14,15},{15,14... | collective-permute-start | bytes 3145736 | tf_op jit(solution)/shard_map/ppermute | solution.py:43
  271.1 86.1 %collective-permute-start.9 = (bf16[512,2048]{1,0:T(8,128)(2,1)S(1)}, bf16[512,2048]{1,0:T(8,128)(2,1)}, u32[]{:S(2)}, u32[]{:S(2)}) collective-permute-start(bf16[512,2048]{1,0:T(8,128)(2,1)S(1)} %copy-done.20), channel_id=1, source_target_pairs={{0,1},{1,0},{4,5},{5,4},{8,9},{9,8},{12,13},{13,12},{14,15},{15,14... | collective-permute-start | bytes 6291464 | tf_op jit(solution)/shard_map/ppermute | solution.py:43
  272.3 92.8 %collective-permute-start.41 = (bf16[256,1024]{1,0:T(8,128)(2,1)}, bf16[256,1024]{1,0:T(8,128)(2,1)}, u32[]{:S(2)}, u32[]{:S(2)}) collective-permute-start(bf16[256,1024]{1,0:T(8,128)(2,1)} %slice.746), channel_id=1, source_target_pairs={{0,4},{1,5},{4,8},{5,9},{8,12},{9,13},{12,14},{13,15},{14,10},{15,... | collective-permute-start | bytes 1572872 | tf_op jit(solution)/shard_map/ppermute | solution.py:37
  285.4 82.3 %collective-permute-start.42 = (bf16[256,1024]{1,0:T(8,128)(2,1)}, bf16[256,1024]{1,0:T(8,128)(2,1)}, u32[]{:S(2)}, u32[]{:S(2)}) collective-permute-start(bf16[256,1024]{1,0:T(8,128)(2,1)} %slice.747), channel_id=1, source_target_pairs={{0,2},{1,3},{4,0},{5,1},{8,4},{9,5},{12,8},{13,9},{14,12},{15,13},... | collective-permute-start | bytes 1572872 | tf_op jit(solution)/shard_map/ppermute | solution.py:40
  287.1 86.7 %collective-permute-start.15 = (bf16[512,2048]{1,0:T(8,128)(2,1)}, bf16[512,2048]{1,0:T(8,128)(2,1)S(1)}, u32[]{:S(2)}, u32[]{:S(2)}) collective-permute-start(bf16[512,2048]{1,0:T(8,128)(2,1)} %slice.704), channel_id=1, source_target_pairs={{0,1},{1,0},{4,5},{5,4},{8,9},{9,8},{12,13},{13,12},{14,15},{15,14... | collective-permute-start | bytes 6291464 | tf_op jit(solution)/shard_map/ppermute | solution.py:43
  354.2 29.4 %collective-permute-start.22 = (bf16[512,2048]{1,0:T(8,128)(2,1)S(1)}, bf16[512,2048]{1,0:T(8,128)(2,1)}, u32[]{:S(2)}, u32[]{:S(2)}) collective-permute-start(bf16[512,2048]{1,0:T(8,128)(2,1)S(1)} %copy-done.21), channel_id=1, source_target_pairs={{0,1},{1,0},{4,5},{5,4},{8,9},{9,8},{12,13},{13,12},{14,15},{15,14... | collective-permute-start | bytes 6291464 | tf_op jit(solution)/shard_map/ppermute | solution.py:43
  367.7 26.4 %collective-permute-start.17 = (f32[256,1024]{1,0:T(8,128)}, f32[256,1024]{1,0:T(8,128)}, u32[]{:S(2)}, u32[]{:S(2)}) collective-permute-start(f32[256,1024]{1,0:T(8,128)} %get-tuple-element.49), channel_id=1, source_target_pairs={{0,4},{1,5},{4,8},{5,9},{8,12},{9,13},{12,14},{13,15},{14,10},{15,... | collective-permute-start | bytes 3145736 | tf_op jit(solution)/shard_map/ppermute | solution.py:37
  371.8 26.3 %collective-permute-start.23 = (f32[256,1024]{1,0:T(8,128)}, f32[256,1024]{1,0:T(8,128)}, u32[]{:S(2)}, u32[]{:S(2)}) collective-permute-start(f32[256,1024]{1,0:T(8,128)} %get-tuple-element.50), channel_id=1, source_target_pairs={{0,2},{1,3},{4,0},{5,1},{8,4},{9,5},{12,8},{13,9},{14,12},{15,13},... | collective-permute-start | bytes 3145736 | tf_op jit(solution)/shard_map/ppermute | solution.py:40
  373.5 41.9 %collective-permute-start.10 = (f32[256,1024]{1,0:T(8,128)}, f32[256,1024]{1,0:T(8,128)}, u32[]{:S(2)}, u32[]{:S(2)}) collective-permute-start(f32[256,1024]{1,0:T(8,128)} %get-tuple-element.47), channel_id=1, source_target_pairs={{0,4},{1,5},{4,8},{5,9},{8,12},{9,13},{12,14},{13,15},{14,10},{15,... | collective-permute-start | bytes 3145736 | tf_op jit(solution)/shard_map/ppermute | solution.py:37
  373.8 45.4 %collective-permute-start.16 = (f32[256,1024]{1,0:T(8,128)S(1)}, f32[256,1024]{1,0:T(8,128)}, u32[]{:S(2)}, u32[]{:S(2)}) collective-permute-start(f32[256,1024]{1,0:T(8,128)S(1)} %get-tuple-element.48), channel_id=1, source_target_pairs={{0,2},{1,3},{4,0},{5,1},{8,4},{9,5},{12,8},{13,9},{14,12},{15,13},... | collective-permute-start | bytes 3145736 | tf_op jit(solution)/shard_map/ppermute | solution.py:40
  383.6 39.5 %collective-permute-start.43 = (bf16[256,2048]{1,0:T(8,128)(2,1)}, bf16[256,2048]{1,0:T(8,128)(2,1)S(1)}, u32[]{:S(2)}, u32[]{:S(2)}) collective-permute-start(bf16[256,2048]{1,0:T(8,128)(2,1)} %get-tuple-element.234), channel_id=1, source_target_pairs={{0,1},{1,0},{4,5},{5,4},{8,9},{9,8},{12,13},{13,12},{14,15},{15,14... | collective-permute-start | bytes 3145736 | tf_op jit(solution)/shard_map/ppermute | solution.py:43
  394.1 68.1 %collective-permute-start.30 = (bf16[512,2048]{1,0:T(8,128)(2,1)S(1)}, bf16[512,2048]{1,0:T(8,128)(2,1)S(1)}, u32[]{:S(2)}, u32[]{:S(2)}) collective-permute-start(bf16[512,2048]{1,0:T(8,128)(2,1)S(1)} %copy-done.22), channel_id=1, source_target_pairs={{0,1},{1,0},{4,5},{5,4},{8,9},{9,8},{12,13},{13,12},{14,15},{15,14... | collective-permute-start | bytes 6291464 | tf_op jit(solution)/shard_map/ppermute | solution.py:43
  398.1 72.9 %collective-permute-start.37 = (bf16[512,2048]{1,0:T(8,128)(2,1)}, bf16[512,2048]{1,0:T(8,128)(2,1)}, u32[]{:S(2)}, u32[]{:S(2)}) collective-permute-start(bf16[512,2048]{1,0:T(8,128)(2,1)} %slice.736), channel_id=1, source_target_pairs={{0,1},{1,0},{4,5},{5,4},{8,9},{9,8},{12,13},{13,12},{14,15},{15,14... | collective-permute-start | bytes 6291464 | tf_op jit(solution)/shard_map/ppermute | solution.py:43
  422.5 39.3 %collective-permute-start.39 = (f32[4,256]{1,0:T(4,128)S(1)}, f32[4,256]{1,0:T(4,128)S(1)}, u32[]{:S(2)}, u32[]{:S(2)}) collective-permute-start(f32[4,256]{1,0:T(4,128)S(1)} %bitcast_add_fusion.6), channel_id=1, source_target_pairs={{0,4},{1,5},{4,8},{5,9},{8,12},{9,13},{12,14},{13,15},{14,10},{15,... | collective-permute-start | bytes 12296 | tf_op jit(solution)/shard_map/ppermute | solution.py:37
  422.8 48.3 %collective-permute-start.32 = (f32[256,1024]{1,0:T(8,128)}, f32[256,1024]{1,0:T(8,128)}, u32[]{:S(2)}, u32[]{:S(2)}) collective-permute-start(f32[256,1024]{1,0:T(8,128)} %get-tuple-element.54), channel_id=1, source_target_pairs={{0,4},{1,5},{4,8},{5,9},{8,12},{9,13},{12,14},{13,15},{14,10},{15,... | collective-permute-start | bytes 3145736 | tf_op jit(solution)/shard_map/ppermute | solution.py:37
  423.1 49.9 %collective-permute-start.38 = (f32[256,1024]{1,0:T(8,128)}, f32[256,1024]{1,0:T(8,128)}, u32[]{:S(2)}, u32[]{:S(2)}) collective-permute-start(f32[256,1024]{1,0:T(8,128)} %get-tuple-element.55), channel_id=1, source_target_pairs={{0,2},{1,3},{4,0},{5,1},{8,4},{9,5},{12,8},{13,9},{14,12},{15,13},... | collective-permute-start | bytes 3145736 | tf_op jit(solution)/shard_map/ppermute | solution.py:40
  461.8 23.4 %collective-permute-start.25 = (f32[256,1024]{1,0:T(8,128)}, f32[256,1024]{1,0:T(8,128)S(1)}, u32[]{:S(2)}, u32[]{:S(2)}) collective-permute-start(f32[256,1024]{1,0:T(8,128)} %get-tuple-element.52), channel_id=1, source_target_pairs={{0,4},{1,5},{4,8},{5,9},{8,12},{9,13},{12,14},{13,15},{14,10},{15,... | collective-permute-start | bytes 3145736 | tf_op jit(solution)/shard_map/ppermute | solution.py:37
  462.1 23.5 %collective-permute-start.31 = (f32[256,1024]{1,0:T(8,128)}, f32[256,1024]{1,0:T(8,128)S(1)}, u32[]{:S(2)}, u32[]{:S(2)}) collective-permute-start(f32[256,1024]{1,0:T(8,128)} %get-tuple-element.53), channel_id=1, source_target_pairs={{0,2},{1,3},{4,0},{5,1},{8,4},{9,5},{12,8},{13,9},{14,12},{15,13},... | collective-permute-start | bytes 3145736 | tf_op jit(solution)/shard_map/ppermute | solution.py:40
  471.1 20.0 %collective-permute-start.44 = (bf16[256,2048]{1,0:T(8,128)(2,1)S(1)}, bf16[256,2048]{1,0:T(8,128)(2,1)S(1)}, u32[]{:S(2)}, u32[]{:S(2)}) collective-permute-start(bf16[256,2048]{1,0:T(8,128)(2,1)S(1)} %slice.750), channel_id=1, source_target_pairs={{0,1},{1,0},{4,5},{5,4},{8,9},{9,8},{12,13},{13,12},{14,15},{15,14... | collective-permute-start | bytes 3145736 | tf_op jit(solution)/shard_map/ppermute | solution.py:43
  471.2 21.6 %collective-permute-start.50 = (bf16[256,2048]{1,0:T(8,128)(2,1)S(1)}, bf16[256,2048]{1,0:T(8,128)(2,1)S(1)}, u32[]{:S(2)}, u32[]{:S(2)}) collective-permute-start(bf16[256,2048]{1,0:T(8,128)(2,1)S(1)} %slice.758), channel_id=1, source_target_pairs={{0,1},{1,0},{4,5},{5,4},{8,9},{9,8},{12,13},{13,12},{14,15},{15,14... | collective-permute-start | bytes 3145736 | tf_op jit(solution)/shard_map/ppermute | solution.py:43
  489.0 26.3 %collective-permute-start.46 = (f32[256,1024]{1,0:T(8,128)}, f32[256,1024]{1,0:T(8,128)}, u32[]{:S(2)}, u32[]{:S(2)}) collective-permute-start(f32[256,1024]{1,0:T(8,128)} %get-tuple-element.59), channel_id=1, source_target_pairs={{0,4},{1,5},{4,8},{5,9},{8,12},{9,13},{12,14},{13,15},{14,10},{15,... | collective-permute-start | bytes 3145736 | tf_op jit(solution)/shard_map/ppermute | solution.py:37
  490.7 26.3 %collective-permute-start.51 = (f32[256,1024]{1,0:T(8,128)}, f32[256,1024]{1,0:T(8,128)}, u32[]{:S(2)}, u32[]{:S(2)}) collective-permute-start(f32[256,1024]{1,0:T(8,128)} %get-tuple-element.60), channel_id=1, source_target_pairs={{0,2},{1,3},{4,0},{5,1},{8,4},{9,5},{12,8},{13,9},{14,12},{15,13},... | collective-permute-start | bytes 3145736 | tf_op jit(solution)/shard_map/ppermute | solution.py:40
  491.1 42.5 %collective-permute-start.40 = (f32[256,1024]{1,0:T(8,128)}, f32[256,1024]{1,0:T(8,128)}, u32[]{:S(2)}, u32[]{:S(2)}) collective-permute-start(f32[256,1024]{1,0:T(8,128)} %get-tuple-element.57), channel_id=1, source_target_pairs={{0,4},{1,5},{4,8},{5,9},{8,12},{9,13},{12,14},{13,15},{14,10},{15,... | collective-permute-start | bytes 3145736 | tf_op jit(solution)/shard_map/ppermute | solution.py:37
  493.7 41.2 %collective-permute-start.45 = (f32[256,1024]{1,0:T(8,128)}, f32[256,1024]{1,0:T(8,128)}, u32[]{:S(2)}, u32[]{:S(2)}) collective-permute-start(f32[256,1024]{1,0:T(8,128)} %get-tuple-element.58), channel_id=1, source_target_pairs={{0,2},{1,3},{4,0},{5,1},{8,4},{9,5},{12,8},{13,9},{14,12},{15,13},... | collective-permute-start | bytes 3145736 | tf_op jit(solution)/shard_map/ppermute | solution.py:40
  501.3 39.0 %collective-permute-start.70 = (bf16[256,2048]{1,0:T(8,128)(2,1)S(1)}, bf16[256,2048]{1,0:T(8,128)(2,1)S(1)}, u32[]{:S(2)}, u32[]{:S(2)}) collective-permute-start(bf16[256,2048]{1,0:T(8,128)(2,1)S(1)} %copy-done.26), channel_id=1, source_target_pairs={{0,1},{1,0},{4,5},{5,4},{8,9},{9,8},{12,13},{13,12},{14,15},{15,14... | collective-permute-start | bytes 3145736 | tf_op jit(solution)/shard_map/ppermute | solution.py:43
  538.3 26.3 %collective-permute-start.55 = (f32[256,1024]{1,0:T(8,128)}, f32[256,1024]{1,0:T(8,128)S(1)}, u32[]{:S(2)}, u32[]{:S(2)}) collective-permute-start(f32[256,1024]{1,0:T(8,128)} %get-tuple-element.64), channel_id=1, source_target_pairs={{0,4},{1,5},{4,8},{5,9},{8,12},{9,13},{12,14},{13,15},{14,10},{15,... | collective-permute-start | bytes 3145736 | tf_op jit(solution)/shard_map/ppermute | solution.py:37
  540.0 26.0 %collective-permute-start.56 = (f32[256,1024]{1,0:T(8,128)S(1)}, f32[256,1024]{1,0:T(8,128)S(1)}, u32[]{:S(2)}, u32[]{:S(2)}) collective-permute-start(f32[256,1024]{1,0:T(8,128)S(1)} %get-tuple-element.65), channel_id=1, source_target_pairs={{0,2},{1,3},{4,0},{5,1},{8,4},{9,5},{12,8},{13,9},{14,12},{15,13},... | collective-permute-start | bytes 3145736 | tf_op jit(solution)/shard_map/ppermute | solution.py:40
  541.0 23.6 %collective-permute-start.57 = (f32[4,256]{1,0:T(4,128)S(1)}, f32[4,256]{1,0:T(4,128)S(1)}, u32[]{:S(2)}, u32[]{:S(2)}) collective-permute-start(f32[4,256]{1,0:T(4,128)S(1)} %bitcast_add_fusion.4), channel_id=1, source_target_pairs={{0,4},{1,5},{4,8},{5,9},{8,12},{9,13},{12,14},{13,15},{14,10},{15,... | collective-permute-start | bytes 12296 | tf_op jit(solution)/shard_map/ppermute | solution.py:37
  542.7 38.9 %collective-permute-start.53 = (f32[256,1024]{1,0:T(8,128)}, f32[256,1024]{1,0:T(8,128)S(1)}, u32[]{:S(2)}, u32[]{:S(2)}) collective-permute-start(f32[256,1024]{1,0:T(8,128)} %get-tuple-element.62), channel_id=1, source_target_pairs={{0,4},{1,5},{4,8},{5,9},{8,12},{9,13},{12,14},{13,15},{14,10},{15,... | collective-permute-start | bytes 3145736 | tf_op jit(solution)/shard_map/ppermute | solution.py:37
  544.2 39.0 %collective-permute-start.54 = (f32[256,1024]{1,0:T(8,128)}, f32[256,1024]{1,0:T(8,128)}, u32[]{:S(2)}, u32[]{:S(2)}) collective-permute-start(f32[256,1024]{1,0:T(8,128)} %get-tuple-element.63), channel_id=1, source_target_pairs={{0,2},{1,3},{4,0},{5,1},{8,4},{9,5},{12,8},{13,9},{14,12},{15,13},... | collective-permute-start | bytes 3145736 | tf_op jit(solution)/shard_map/ppermute | solution.py:40
  584.9 41.8 %collective-permute-start.60 = (f32[256,1024]{1,0:T(8,128)S(1)}, f32[256,1024]{1,0:T(8,128)S(1)}, u32[]{:S(2)}, u32[]{:S(2)}) collective-permute-start(f32[256,1024]{1,0:T(8,128)S(1)} %get-tuple-element.69), channel_id=1, source_target_pairs={{0,4},{1,5},{4,8},{5,9},{8,12},{9,13},{12,14},{13,15},{14,10},{15,... | collective-permute-start | bytes 3145736 | tf_op jit(solution)/shard_map/ppermute | solution.py:37
  586.6 40.1 %collective-permute-start.61 = (f32[256,1024]{1,0:T(8,128)S(1)}, f32[256,1024]{1,0:T(8,128)S(1)}, u32[]{:S(2)}, u32[]{:S(2)}) collective-permute-start(f32[256,1024]{1,0:T(8,128)S(1)} %get-tuple-element.70), channel_id=1, source_target_pairs={{0,2},{1,3},{4,0},{5,1},{8,4},{9,5},{12,8},{13,9},{14,12},{15,13},... | collective-permute-start | bytes 3145736 | tf_op jit(solution)/shard_map/ppermute | solution.py:40
  595.2 33.6 %collective-permute-start.58 = (f32[256,1024]{1,0:T(8,128)S(1)}, f32[256,1024]{1,0:T(8,128)S(1)}, u32[]{:S(2)}, u32[]{:S(2)}) collective-permute-start(f32[256,1024]{1,0:T(8,128)S(1)} %get-tuple-element.67), channel_id=1, source_target_pairs={{0,4},{1,5},{4,8},{5,9},{8,12},{9,13},{12,14},{13,15},{14,10},{15,... | collective-permute-start | bytes 3145736 | tf_op jit(solution)/shard_map/ppermute | solution.py:37
  596.8 32.0 %collective-permute-start.59 = (f32[256,1024]{1,0:T(8,128)S(1)}, f32[256,1024]{1,0:T(8,128)S(1)}, u32[]{:S(2)}, u32[]{:S(2)}) collective-permute-start(f32[256,1024]{1,0:T(8,128)S(1)} %get-tuple-element.68), channel_id=1, source_target_pairs={{0,2},{1,3},{4,0},{5,1},{8,4},{9,5},{12,8},{13,9},{14,12},{15,13},... | collective-permute-start | bytes 3145736 | tf_op jit(solution)/shard_map/ppermute | solution.py:40
  600.2 26.5 %collective-permute-start.62 = (f32[4,256]{1,0:T(4,128)S(1)}, f32[4,256]{1,0:T(4,128)S(1)}, u32[]{:S(2)}, u32[]{:S(2)}) collective-permute-start(f32[4,256]{1,0:T(4,128)S(1)} %bitcast_add_fusion.3), channel_id=1, source_target_pairs={{0,4},{1,5},{4,8},{5,9},{8,12},{9,13},{12,14},{13,15},{14,10},{15,... | collective-permute-start | bytes 12296 | tf_op jit(solution)/shard_map/ppermute | solution.py:37
  629.3 39.7 %collective-permute-start.67 = (f32[4,256]{1,0:T(4,128)S(1)}, f32[4,256]{1,0:T(4,128)S(1)}, u32[]{:S(2)}, u32[]{:S(2)}) collective-permute-start(f32[4,256]{1,0:T(4,128)S(1)} %bitcast_add_fusion.2), channel_id=1, source_target_pairs={{0,4},{1,5},{4,8},{5,9},{8,12},{9,13},{12,14},{13,15},{14,10},{15,... | collective-permute-start | bytes 12296 | tf_op jit(solution)/shard_map/ppermute | solution.py:37
  631.1 38.0 %collective-permute-start.65 = (f32[256,1024]{1,0:T(8,128)S(1)}, f32[256,1024]{1,0:T(8,128)S(1)}, u32[]{:S(2)}, u32[]{:S(2)}) collective-permute-start(f32[256,1024]{1,0:T(8,128)S(1)} %get-tuple-element.74), channel_id=1, source_target_pairs={{0,4},{1,5},{4,8},{5,9},{8,12},{9,13},{12,14},{13,15},{14,10},{15,... | collective-permute-start | bytes 3145736 | tf_op jit(solution)/shard_map/ppermute | solution.py:37
  632.7 36.4 %collective-permute-start.66 = (f32[256,1024]{1,0:T(8,128)S(1)}, f32[256,1024]{1,0:T(8,128)S(1)}, u32[]{:S(2)}, u32[]{:S(2)}) collective-permute-start(f32[256,1024]{1,0:T(8,128)S(1)} %get-tuple-element.75), channel_id=1, source_target_pairs={{0,2},{1,3},{4,0},{5,1},{8,4},{9,5},{12,8},{13,9},{14,12},{15,13},... | collective-permute-start | bytes 3145736 | tf_op jit(solution)/shard_map/ppermute | solution.py:40
  633.1 38.5 %collective-permute-start.63 = (f32[256,1024]{1,0:T(8,128)S(1)}, f32[256,1024]{1,0:T(8,128)S(1)}, u32[]{:S(2)}, u32[]{:S(2)}) collective-permute-start(f32[256,1024]{1,0:T(8,128)S(1)} %get-tuple-element.72), channel_id=1, source_target_pairs={{0,4},{1,5},{4,8},{5,9},{8,12},{9,13},{12,14},{13,15},{14,10},{15,... | collective-permute-start | bytes 3145736 | tf_op jit(solution)/shard_map/ppermute | solution.py:37
  634.8 38.2 %collective-permute-start.64 = (f32[256,1024]{1,0:T(8,128)S(1)}, f32[256,1024]{1,0:T(8,128)S(1)}, u32[]{:S(2)}, u32[]{:S(2)}) collective-permute-start(f32[256,1024]{1,0:T(8,128)S(1)} %get-tuple-element.73), channel_id=1, source_target_pairs={{0,2},{1,3},{4,0},{5,1},{8,4},{9,5},{12,8},{13,9},{14,12},{15,13},... | collective-permute-start | bytes 3145736 | tf_op jit(solution)/shard_map/ppermute | solution.py:40
  669.0 76.6 %collective-permute-start.74 = (bf16[256,2048]{1,0:T(8,128)(2,1)S(1)}, bf16[256,2048]{1,0:T(8,128)(2,1)S(1)}, u32[]{:S(2)}, u32[]{:S(2)}) collective-permute-start(bf16[256,2048]{1,0:T(8,128)(2,1)S(1)} %copy-done.25), channel_id=1, source_target_pairs={{0,1},{1,0},{4,5},{5,4},{8,9},{9,8},{12,13},{13,12},{14,15},{15,14... | collective-permute-start | bytes 3145736 | tf_op jit(solution)/shard_map/ppermute | solution.py:43
  674.6 37.3 %collective-permute-start.76 = (f32[4,256]{1,0:T(4,128)S(1)}, f32[4,256]{1,0:T(4,128)S(1)}, u32[]{:S(2)}, u32[]{:S(2)}) collective-permute-start(f32[4,256]{1,0:T(4,128)S(1)} %bitcast_add_fusion.1), channel_id=1, source_target_pairs={{0,4},{1,5},{4,8},{5,9},{8,12},{9,13},{12,14},{13,15},{14,10},{15,... | collective-permute-start | bytes 12296 | tf_op jit(solution)/shard_map/ppermute | solution.py:37
  709.2 36.4 %collective-permute-start.72 = (f32[256,1024]{1,0:T(8,128)S(1)}, f32[256,1024]{1,0:T(8,128)S(1)}, u32[]{:S(2)}, u32[]{:S(2)}) collective-permute-start(f32[256,1024]{1,0:T(8,128)S(1)} %get-tuple-element.79), channel_id=1, source_target_pairs={{0,4},{1,5},{4,8},{5,9},{8,12},{9,13},{12,14},{13,15},{14,10},{15,... | collective-permute-start | bytes 3145736 | tf_op jit(solution)/shard_map/ppermute | solution.py:37
  710.0 35.6 %collective-permute-start.75 = (f32[256,1024]{1,0:T(8,128)S(1)}, f32[256,1024]{1,0:T(8,128)S(1)}, u32[]{:S(2)}, u32[]{:S(2)}) collective-permute-start(f32[256,1024]{1,0:T(8,128)S(1)} %get-tuple-element.80), channel_id=1, source_target_pairs={{0,2},{1,3},{4,0},{5,1},{8,4},{9,5},{12,8},{13,9},{14,12},{15,13},... | collective-permute-start | bytes 3145736 | tf_op jit(solution)/shard_map/ppermute | solution.py:40
  711.2 44.8 %collective-permute-start.68 = (f32[256,1024]{1,0:T(8,128)S(1)}, f32[256,1024]{1,0:T(8,128)S(1)}, u32[]{:S(2)}, u32[]{:S(2)}) collective-permute-start(f32[256,1024]{1,0:T(8,128)S(1)} %get-tuple-element.77), channel_id=1, source_target_pairs={{0,4},{1,5},{4,8},{5,9},{8,12},{9,13},{12,14},{13,15},{14,10},{15,... | collective-permute-start | bytes 3145736 | tf_op jit(solution)/shard_map/ppermute | solution.py:37
  712.0 44.7 %collective-permute-start.71 = (f32[256,1024]{1,0:T(8,128)S(1)}, f32[256,1024]{1,0:T(8,128)S(1)}, u32[]{:S(2)}, u32[]{:S(2)}) collective-permute-start(f32[256,1024]{1,0:T(8,128)S(1)} %get-tuple-element.78), channel_id=1, source_target_pairs={{0,2},{1,3},{4,0},{5,1},{8,4},{9,5},{12,8},{13,9},{14,12},{15,13},... | collective-permute-start | bytes 3145736 | tf_op jit(solution)/shard_map/ppermute | solution.py:40
  (107 other events, 1674.5 us)
